TPU v7x, 256 devices: a whole 4x4x8 slice. The times are simulated.
256 devices in a mesh: gx: 16 (over y, z_hi, core), gy: 16 (over x, z_lo).
Axes of the slice: x: 4, y: 4, z: 8 (z_hi: 2, z_lo: 4; z = z_hi * 4 + z_lo), core: 2. Of those that a mesh axis runs over, the one named last changes fastest.
Arguments:
- populations: float32 [19, 64, 128, 128], P(None, 'gx', 'gy'), may hold values from 0.004 to 0.8, as said below
- solid: int32 [64, 128, 128], P('gx', 'gy'), may hold values 0 or 1
- base_cell: int32 [3, 16, 16, 2, 768], P(None, 'gx', 'gy'), may hold values from 0 to 127, as said below
- offset: float32 [3, 16, 16, 2, 768], P(None, 'gx', 'gy'), may hold values from 0 to 1
- rest_displacement: float32 [3, 16, 16, 2, 768], P(None, 'gx', 'gy'), may hold values from 0 to 1
- stiffness: float32 [16, 16, 2], P('gx', 'gy'), may hold values from 0.006380062 to 0.063800626
- occupied: int32 [16, 16, 2], P('gx', 'gy'), may hold values from 0 to 1, as said below
- triangles: int32 [1280, 3], replicated, may hold values from 0 to 641, as said below
Outputs:
- populations_out: float32 [19, 64, 128, 128], P(None, 'gx', 'gy')
- offset_out: float32 [3, 16, 16, 2, 768], P(None, 'gx', 'gy')
Inputs may be any that keep to these rules, and one draw needn't show every extreme that they name: `populations`: every entry is positive. `base_cell`: component 0 of a vertex stored at index i of gx lies in [i * 4, (i + 1) * 4), component 1 of one stored at index j of gy lies in [j * 8, (j + 1) * 8), component 2 lies below 128. The occupied slots of a device come first; each device has at least one, and some device has all 2. `triangles`: each row holds three different vertex numbers below 642.
All inputs are finite; a program needn't handle non-finite values. No bound on the sum of `solid` on one device may be relied on, other than what follows from the above.
Results may differ from a plain program's by a relative error of at most 0.0001.
Values sent between devices are 32-bit elements; how exact they have to be, the bound alone decides.
No kernel may reach another device: no remote copies, remote signals or barrier semaphores. Data moves between devices by JAX's collectives and lax.ppermute only.
A program may use at most 64 MiB of HBM per device.

v0:
```python
import functools
import math

import jax
import jax.numpy as jnp
from jax import lax
from jax.experimental import pallas as pl
from jax.experimental.pallas import tpu as pltpu
from jax.sharding import PartitionSpec as P

SUBSTEPS = 3
AX = ("gx", "gy")

VELOCITIES = [
    [0, 0, 0],
    [1, 0, 0],
    [-1, 0, 0],
    [0, 1, 0],
    [0, -1, 0],
    [0, 0, 1],
    [0, 0, -1],
    [1, 1, 0],
    [-1, -1, 0],
    [1, -1, 0],
    [-1, 1, 0],
    [1, 0, 1],
    [-1, 0, -1],
    [1, 0, -1],
    [-1, 0, 1],
    [0, 1, 1],
    [0, -1, -1],
    [0, 1, -1],
    [0, -1, 1],
]
OPPOSITE = [0, 2, 1, 4, 3, 6, 5, 8, 7, 10, 9, 12, 11, 14, 13, 16, 15, 18, 17]
LATTICE_WEIGHTS = [1.0 / 3.0] + [1.0 / 18.0] * 6 + [1.0 / 36.0] * 12
RELAX = 0.8
CX, CY, CZ = 4, 8, 128
SLOTS, PAD = 2, 768
UP_X = [q for q in range(19) if VELOCITIES[q][0] == 1]
DOWN_X = [q for q in range(19) if VELOCITIES[q][0] == -1]
UP_Y = [q for q in range(19) if VELOCITIES[q][1] == 1]
DOWN_Y = [q for q in range(19) if VELOCITIES[q][1] == -1]
X_ORDER = [0, 1, 2, 3, 4, 5, -1]
Y_RIM = [8, 9, -1]
MAIN_ROWS = 3 * 7 * 8
RIM_ROWS = 3 * 3 * 8
TABLE_ROWS = MAIN_ROWS + RIM_ROWS
F32 = jnp.float32
HIGH = lax.Precision.HIGH
TILE = (8, CZ)


def tile_rows():
    return lax.broadcasted_iota(jnp.int32, TILE, 0)


def row_of(tile, r):
    return jnp.broadcast_to(tile[r : r + 1, :], (8, tile.shape[1]))


def choose(first, a, b):
    return jnp.where(first, a, b)


def stencil_kernels(offset):
    angle = offset * (math.pi / 2.0)
    c, s = jnp.cos(angle), jnp.sin(angle)
    return [(1.0 - s) * 0.25, (1.0 + c) * 0.25, (1.0 + s) * 0.25, (1.0 - c) * 0.25]


def pick(distance, kernels, r):
    out = jnp.zeros(distance.shape, F32)
    for n in range(4):
        out = jnp.where(distance == n, kernels[n][r : r + 1, :], out)
    return out


def vertex_tables(base, kernels, slot):
    rows = lax.broadcasted_iota(jnp.int32, (8, PAD), 0)
    x_value = jnp.where(rows < 6, rows, jnp.where(rows == 6, -1, 100))
    y_rim = jnp.where(rows < 2, rows + 8, jnp.where(rows == 2, -1, 100))
    base_x, base_y, base_z = [base[2 * a + slot : 2 * a + slot + 1, :] for a in range(3)]
    table_x = pick(x_value - base_x + 1, kernels, slot)
    table_y = pick(rows - base_y + 1, kernels, 2 + slot)
    table_rim = pick(y_rim - base_y + 1, kernels, 2 + slot)
    depth = lax.broadcasted_iota(jnp.int32, (CZ, PAD), 0)
    table_z = pick(jnp.bitwise_and(depth - base_z + 1, CZ - 1), kernels, 4 + slot)
    return table_x, table_y, table_rim, table_z


def vertex_force(offset, rest, scale, links_high, links_low):
    strain = offset - rest
    high = strain.astype(jnp.bfloat16)
    low = (strain - high.astype(F32)).astype(jnp.bfloat16)
    both = jnp.concatenate([high, low], axis=0)
    first = jnp.dot(both, links_high, preferred_element_type=F32)
    second = jnp.dot(both, links_low, preferred_element_type=F32)
    total = first + second
    return scale * (total[:8] + total[8:])


def spread(offset, rest, scale, base, links_high, links_low, terms, main_ref, rim_ref):
    force = vertex_force(offset, rest, scale, links_high, links_low)
    kernels = stencil_kernels(offset)
    grid = None
    for slot in range(SLOTS):
        table_x, table_y, table_rim, table_z = vertex_tables(base, kernels, slot)
        for a in range(3):
            pushed = force[2 * a + slot : 2 * a + slot + 1, :]
            along_x = table_x * pushed
            for n in range(7):
                terms[(a * 7 + n) * 8 : (a * 7 + n + 1) * 8, :] = row_of(along_x, n) * table_y
            along_y = table_rim * pushed
            for n in range(3):
                start = MAIN_ROWS + (a * 3 + n) * 8
                terms[start : start + 8, :] = row_of(along_y, n) * table_x
        part = lax.dot_general(
            terms[...], table_z, (((1,), (1,)), ((), ())), precision=HIGH, preferred_element_type=F32
        )
        grid = part if grid is None else grid + part
    main_ref[...] = grid[:MAIN_ROWS].reshape(3, 7, 8, CZ)
    rim_ref[...] = grid[MAIN_ROWS:].reshape(3, 3, 8, CZ)


def spread_messages(parity, main_ref, rim_ref, first_ref, second_ref):
    even = parity == 0
    zero = jnp.zeros((2, CZ), F32)
    for a in range(3):
        up_rows, down_rows = [], []
        for n in range(3):
            rim = rim_ref[a, n]
            up_rows.append(rim[4:6])
            down_rows.append(rim[6:8])
        ups = [main_ref[a, 4], main_ref[a, 5], jnp.concatenate(up_rows + [zero], axis=0)]
        downs = [main_ref[a, 6], main_ref[a, 6], jnp.concatenate(down_rows + [zero], axis=0)]
        for t in range(3):
            first_ref[a, t] = choose(even, ups[t], downs[t])
            second_ref[a, t] = choose(even, downs[t], ups[t])


def links_kernel(triangles_ref, high_ref, low_ref, incidence):
    vertex = lax.broadcasted_iota(jnp.int32, incidence.shape, 0)
    hit = jnp.zeros(incidence.shape, F32)
    for corner in range(3):
        hit = jnp.where(triangles_ref[corner : corner + 1, :] == vertex, 1.0, hit)
    incidence[...] = hit.astype(jnp.bfloat16)
    shared = lax.dot_general(
        incidence[...], incidence[...], (((1,), (1,)), ((), ())), preferred_element_type=F32
    )
    same = lax.broadcasted_iota(jnp.int32, shared.shape, 0) == lax.broadcasted_iota(
        jnp.int32, shared.shape, 1
    )
    shared = jnp.where(same, -2.0 * shared, shared)
    high = shared.astype(jnp.bfloat16)
    high_ref[...] = high
    low_ref[...] = (shared - high.astype(F32)).astype(jnp.bfloat16)


def spread_kernel(
    place_ref, offset_ref, rest_ref, scale_ref, base_ref, high_ref, low_ref,
    main_ref, rim_ref, first_ref, second_ref, terms,
):
    spread(
        offset_ref[...], rest_ref[...], scale_ref[...], base_ref[...],
        high_ref[...], low_ref[...], terms, main_ref, rim_ref,
    )
    spread_messages(place_ref[0], main_ref, rim_ref, first_ref, second_ref)


def force_corner_kernel(place_ref, rim_ref, first_in, second_in, first_ref, second_ref):
    even_x = place_ref[0] == 0
    even_y = place_ref[1] == 0
    rows = tile_rows()
    for a in range(3):
        above = choose(even_x, first_in[a, 2], second_in[a, 2])
        below = choose(even_x, second_in[a, 2], first_in[a, 2])
        whole = []
        for n in range(3):
            from_below = below[2 * n : 2 * n + 2]
            from_above = above[2 * n : 2 * n + 1]
            part = rim_ref[a, n][:4]
            whole.append(
                jnp.concatenate([part[0:2] + from_below, part[2:3], part[3:4] + from_above], axis=0)
            )
        up = jnp.concatenate([whole[0], whole[1]], axis=0)
        down = jnp.concatenate([whole[2], whole[2]], axis=0)
        first_ref[a] = choose(even_y, up, down)
        second_ref[a] = choose(even_y, down, up)


def moment_sums(members, rows):
    groups = {}
    for step in (0, 1, -1):
        of_step = [(q, t) for q, t in members if VELOCITIES[q][1] == step]
        sums = []
        for what in (None, 0, 2):
            total = None
            for q, t in of_step:
                weight = 1 if what is None else VELOCITIES[q][what]
                if weight == 0:
                    continue
                term = t if weight == 1 else -t
                total = term if total is None else total + term
            sums.append(jnp.zeros(TILE, F32) if total is None else total)
        groups[step] = sums
    up = [jnp.where(rows == 0, 0.0, t) for t in groups[1]]
    down = [jnp.where(rows == 7, 0.0, t) for t in groups[-1]]
    density, along_x, along_z = [groups[0][k] + up[k] + down[k] for k in range(3)]
    inside = [density, along_x, up[0] - down[0], along_z]
    edge = [
        jnp.where(rows == 0, groups[1][k], jnp.where(rows == 7, groups[-1][k], 0.0)) for k in range(3)
    ]
    return inside, edge


def pack_edges(edge):
    return edge[0] + pltpu.roll(edge[1], 2, 0) + pltpu.roll(edge[2], 4, 0)


def unpack_edges(packed, rows):
    keep = (rows == 0) | (rows == 7)
    tiles = [packed, pltpu.roll(packed, 6, 0), pltpu.roll(packed, 4, 0)]
    return [jnp.where(keep, t, 0.0) for t in tiles]


def collide_kernel(
    place_ref, populations_ref, solid_ref, main_ref, first_x, second_x, first_y, second_y,
    stepped_ref, force_ref, first_ref, second_ref,
):
    even_x = place_ref[0] == 0
    even_y = place_ref[1] == 0
    rows = tile_rows()
    for x in range(4):
        force = []
        for a in range(3):
            f = main_ref[a, x]
            if x < 2:
                f = f + choose(even_x, second_x[a, x], first_x[a, x])
            if x == 3:
                f = f + choose(even_x, first_x[a, 0], second_x[a, 0])
            below = choose(even_y, second_y[a], first_y[a])
            above = choose(even_y, first_y[a], second_y[a])
            f = f + jnp.where(
                rows == 0,
                row_of(below, x),
                jnp.where(rows == 1, row_of(below, 4 + x), jnp.where(rows == 7, row_of(above, x), 0.0)),
            )
            force_ref[a, x] = f
            force.append(f)
        current = [populations_ref[q, x] for q in range(19)]
        density = functools.reduce(lambda u, v: u + v, current)
        velocity = []
        for a in range(3):
            moving = force[a] * 0.5
            for q in range(19):
                if VELOCITIES[q][a] == 1:
                    moving = moving + current[q]
                elif VELOCITIES[q][a] == -1:
                    moving = moving - current[q]
            velocity.append(moving)
        inverse = 1.0 / density
        velocity = [m * inverse for m in velocity]
        squared = velocity[0] * velocity[0] + velocity[1] * velocity[1] + velocity[2] * velocity[2]
        working = velocity[0] * force[0] + velocity[1] * force[1] + velocity[2] * force[2]
        walled = solid_ref[x] != 0
        common = 1.0 - 1.5 * squared
        factor = 1.0 - 0.5 / RELAX
        for q in range(19):
            vector = VELOCITIES[q]
            w = LATTICE_WEIGHTS[q]
            if q == 0:
                equilibrium = w * density * common
                source = (-3.0 * factor * w) * working
            else:
                along, pushed = None, None
                for a in range(3):
                    if vector[a] == 0:
                        continue
                    u = velocity[a] if vector[a] == 1 else -velocity[a]
                    f = force[a] if vector[a] == 1 else -force[a]
                    along = u if along is None else along + u
                    pushed = f if pushed is None else pushed + f
                equilibrium = w * density * (common + along * (3.0 + 4.5 * along))
                source = (factor * w) * (3.0 * (pushed - working) + 9.0 * along * pushed)
            updated = current[q] - (current[q] - equilibrium) / RELAX + source
            relaxed = jnp.where(walled, current[OPPOSITE[q]], updated)
            if vector[2] != 0:
                relaxed = pltpu.roll(relaxed, vector[2] % CZ, 1)
            if vector[1] != 0:
                relaxed = pltpu.roll(relaxed, vector[1] % 8, 0)
            stepped_ref[q, (x + vector[0]) % 4] = relaxed
    messages = []
    for crossing, lines in ((UP_X, (3,)), (DOWN_X, (0, 1))):
        slot = 0 if crossing is UP_X else 3
        tiles = [stepped_ref[q, slot] for q in crossing]
        for x in lines:
            members = [
                (q, stepped_ref[q, x])
                for q in range(19)
                if not (x == 0 and VELOCITIES[q][0] == 1) and not (x == 3 and VELOCITIES[q][0] == -1)
            ]
            inside, edge = moment_sums(members, rows)
            for k in range(3):
                inside[1 + k] = inside[1 + k] + 0.5 * force_ref[k, x]
            tiles += inside + [pack_edges(edge)]
        messages.append(tiles)
    up, down = messages
    for t in range(15):
        u = up[t] if t < len(up) else down[t]
        first_ref[t] = choose(even_x, u, down[t])
        second_ref[t] = choose(even_x, down[t], u)


def flow_corner_kernel(
    place_ref, stepped_in, force_ref, first_x, second_x,
    stepped_ref, inside_ref, leaving_ref, first_ref, second_ref, edges, up_tiles, down_tiles,
):
    even_x = place_ref[0] == 0
    even_y = place_ref[1] == 0
    rows = tile_rows()
    below = [choose(even_x, second_x[t], first_x[t]) for t in range(10)]
    above = [choose(even_x, first_x[t], second_x[t]) for t in range(15)]
    out_up = [(q, stepped_in[q, 0]) for q in UP_X]
    out_down = [(q, stepped_in[q, 3]) for q in DOWN_X]
    for q in range(19):
        for x in range(4):
            s = stepped_in[q, x]
            if q in UP_X and x == 0:
                s = below[UP_X.index(q)]
            if q in DOWN_X and x == 3:
                s = above[DOWN_X.index(q)]
            stepped_ref[(q * 4 + x) * 8 : (q * 4 + x + 1) * 8, :] = s
    for n, x in enumerate(X_ORDER):
        if 0 <= x < 4:
            members = [(q, stepped_ref[(q * 4 + x) * 8 : (q * 4 + x + 1) * 8, :]) for q in range(19)]
            inside, edge = moment_sums(members, rows)
            for k in range(3):
                inside[1 + k] = inside[1 + k] + 0.5 * force_ref[k, x]
        else:
            received = below[5:10] if x == -1 else above[5 + 5 * (x - 4) : 10 + 5 * (x - 4)]
            inside, edge = received[:4], unpack_edges(received[4], rows)
            if x != 5:
                own_inside, own_edge = moment_sums(out_down if x == -1 else out_up, rows)
                inside = [u + v for u, v in zip(inside, own_inside)]
                edge = [u + v for u, v in zip(edge, own_edge)]
        for k in range(4):
            inside_ref[(k * 8 + n) * 8 : (k * 8 + n + 1) * 8, :] = inside[k]
        for k in range(3):
            edges[(k * 8 + n) * 8 : (k * 8 + n + 1) * 8, :] = edge[k]
    for k in range(4):
        inside_ref[(k * 8 + 7) * 8 : (k * 8 + 8) * 8, :] = jnp.ones(TILE, F32)
    for k in range(3):
        edges[(k * 8 + 7) * 8 : (k * 8 + 8) * 8, :] = jnp.zeros(TILE, F32)
    for k in range(3):
        up = edges[pl.ds(k * 64, 8, stride=8), :]
        down = edges[pl.ds(k * 64 + 7, 8, stride=8), :]
        leaving_ref[k] = up
        leaving_ref[3 + k] = down
        up_tiles[k] = up
        down_tiles[k] = down
    for t in range(3, 5):
        up_tiles[t] = jnp.zeros(TILE, F32)
        down_tiles[t] = jnp.zeros(TILE, F32)
    for t in range(5):
        up_tiles[t, 0:4, :] = stepped_ref[pl.ds(UP_Y[t] * 32, 4, stride=8), :]
        down_tiles[t, 0:4, :] = stepped_ref[pl.ds(DOWN_Y[t] * 32 + 7, 4, stride=8), :]
    for k in range(4):
        up_tiles[5 + k] = inside_ref[pl.ds(k * 64 + 7, 8, stride=8), :]
        down_tiles[5 + k] = inside_ref[pl.ds(k * 64, 8, stride=8), :]
        down_tiles[9 + k] = inside_ref[pl.ds(k * 64 + 1, 8, stride=8), :]
    for t in range(13):
        u = up_tiles[t] if t < 9 else down_tiles[t]
        d = down_tiles[t]
        first_ref[t] = choose(even_y, u, d)
        second_ref[t] = choose(even_y, d, u)


def finish_fluid(place_ref, stepped_ref, inside_ref, leaving_ref, first_y, second_y, out_ref, flow):
    even_y = place_ref[1] == 0
    rows = tile_rows()
    below = [choose(even_y, second_y[t], first_y[t]) for t in range(9)]
    above = [choose(even_y, first_y[t], second_y[t]) for t in range(13)]
    for q in range(19):
        for x in range(4):
            s = stepped_ref[(q * 4 + x) * 8 : (q * 4 + x + 1) * 8, :]
            if q in UP_Y:
                s = jnp.where(rows == 0, row_of(below[UP_Y.index(q)], x), s)
            if q in DOWN_Y:
                s = jnp.where(rows == 7, row_of(above[DOWN_Y.index(q)], x), s)
            out_ref[q, x] = s
    if flow is None:
        return

    def arriving(tiles, members):
        out = []
        for k, what in enumerate((None, 0, 2)):
            total = None
            for n, q in enumerate(members):
                weight = 1 if what is None else VELOCITIES[q][what]
                if weight:
                    term = tiles[n] if weight == 1 else -tiles[n]
                    total = term if total is None else total + term
            out.append(jnp.where(rows < 4, total, tiles[k]))
        return [out[0], out[1], None, out[2]]

    from_below = arriving(below, UP_Y)
    from_above = arriving(above, DOWN_Y)
    from_below[2] = from_below[0]
    from_above[2] = -from_above[0]
    for n in range(7):
        total = []
        for k in range(4):
            t = inside_ref[(k * 8 + n) * 8 : (k * 8 + n + 1) * 8, :]
            t = t + jnp.where(
                rows == 0,
                row_of(from_below[k], n),
                jnp.where(rows == 7, row_of(from_above[k], n), 0.0),
            )
            total.append(t)
        inverse = 1.0 / total[0]
        for a in range(3):
            flow[(a * 7 + n) * 8 : (a * 7 + n + 1) * 8, :] = total[1 + a] * inverse
    up = [leaving_ref[0], leaving_ref[1], leaving_ref[0], leaving_ref[2]]
    down = [leaving_ref[3], leaving_ref[4], -leaving_ref[3], leaving_ref[5]]
    rims = (
        [above[5 + k] + up[k] for k in range(4)],
        [above[9 + k] for k in range(4)],
        [below[5 + k] + down[k] for k in range(4)],
    )
    for n, total in enumerate(rims):
        inverse = 1.0 / jnp.where(rows == 7, 1.0, total[0])
        for a in range(3):
            start = MAIN_ROWS + (a * 3 + n) * 8
            flow[start : start + 8, :] = jnp.where(rows == 7, 0.0, total[1 + a] * inverse)


def sample(offset, live, base, flow):
    kernels = stencil_kernels(offset)
    moved = [None] * 8
    zero = jnp.zeros((1, PAD), F32)
    for slot in range(SLOTS):
        table_x, table_y, table_rim, table_z = vertex_tables(base, kernels, slot)
        along = jnp.dot(flow[...], table_z, precision=HIGH, preferred_element_type=F32)
        for a in range(3):
            inner = None
            for n in range(7):
                tile = along[(a * 7 + n) * 8 : (a * 7 + n + 1) * 8, :]
                term = tile * row_of(table_x, n)
                inner = term if inner is None else inner + term
            total = inner * table_y
            outer = None
            for n in range(3):
                start = MAIN_ROWS + (a * 3 + n) * 8
                term = along[start : start + 8, :] * row_of(table_rim, n)
                outer = term if outer is None else outer + term
            total = total + outer * table_x
            moved[2 * a + slot] = jnp.sum(total, axis=0, keepdims=True)
    stacked = jnp.concatenate(moved[:6] + [zero, zero], axis=0)
    return offset + live * stacked


def next_kernel(
    place_ref, stepped_ref, inside_ref, leaving_ref, first_y, second_y,
    offset_ref, rest_ref, scale_ref, live_ref, base_ref, high_ref, low_ref,
    out_ref, offset_out, main_ref, rim_ref, first_ref, second_ref, flow, terms,
):
    finish_fluid(place_ref, stepped_ref, inside_ref, leaving_ref, first_y, second_y, out_ref, flow)
    offset = sample(offset_ref[...], live_ref[...], base_ref[...], flow)
    offset_out[...] = offset
    spread(
        offset, rest_ref[...], scale_ref[...], base_ref[...],
        high_ref[...], low_ref[...], terms, main_ref, rim_ref,
    )
    spread_messages(place_ref[0], main_ref, rim_ref, first_ref, second_ref)


def last_kernel(
    place_ref, stepped_ref, inside_ref, leaving_ref, first_y, second_y,
    offset_ref, live_ref, base_ref,
    out_ref, offset_out, flow,
):
    finish_fluid(place_ref, stepped_ref, inside_ref, leaving_ref, first_y, second_y, out_ref, flow)
    offset_out[...] = sample(offset_ref[...], live_ref[...], base_ref[...], flow)


INTERPRET = False


def call(kernel, outs, scratch, *operands, name):
    in_specs = [pl.BlockSpec(memory_space=pltpu.SMEM)] if kernel is not links_kernel else []
    in_specs += [pl.BlockSpec(memory_space=pltpu.VMEM)] * (len(operands) - len(in_specs))
    return pl.pallas_call(
        kernel,
        out_shape=[jax.ShapeDtypeStruct(shape, dtype) for shape, dtype in outs],
        in_specs=in_specs,
        out_specs=[pl.BlockSpec(memory_space=pltpu.VMEM)] * len(outs),
        scratch_shapes=[pltpu.VMEM(shape, dtype) for shape, dtype in scratch],
        compiler_params=pltpu.CompilerParams(vmem_limit_bytes=24 * 1024 * 1024),
        interpret=INTERPRET,
        name=name,
    )(*operands)


def partner(index, kind, size):
    return (index + 1) % size if (index + kind) % 2 == 0 else (index - 1) % size


def exchange(first, second, axis):
    size = lax.axis_size(axis)
    out = []
    for kind, message in ((0, first), (1, second)):
        pairs = [(i, partner(i, kind, size)) for i in range(size)]
        out.append(lax.ppermute(message, axis, pairs))
    return out


SPREAD_OUT = [
    ((3, 7, 8, CZ), F32),
    ((3, 3, 8, CZ), F32),
    ((3, 3, 8, CZ), F32),
    ((3, 3, 8, CZ), F32),
]
STEPPED = ((19, 4, 8, CZ), F32)


def local(populations, solid, base_cell, offset, rest_displacement, stiffness, occupied, triangles):
    place_x = lax.axis_index("gx")
    place_y = lax.axis_index("gy")
    place = jnp.stack([place_x % 2, place_y % 2]).astype(jnp.int32)

    def pad(rows):
        return jnp.pad(rows.reshape(6, PAD), ((0, 2), (0, 0)))

    start = jnp.stack([place_x * CX, place_y * CY, place_x * 0]).astype(jnp.int32)
    base = pad(base_cell.reshape(3, SLOTS, PAD) - start[:, None, None])
    where = pad(offset)
    rest = pad(rest_displacement)
    held = occupied.reshape(1, SLOTS, 1).astype(F32)
    spring = stiffness.reshape(1, SLOTS, 1) * held
    scale = pad(jnp.broadcast_to(spring, (3, SLOTS, PAD)))
    live = pad(jnp.broadcast_to(held, (3, SLOTS, PAD)))
    corners = triangles.T
    links = [((PAD, PAD), jnp.bfloat16)] * 2
    high, low = call(
        links_kernel, links, [((PAD, triangles.shape[0]), jnp.bfloat16)], corners, name="links"
    )
    terms = ((TABLE_ROWS, PAD), F32)
    flow = ((TABLE_ROWS, CZ), F32)
    main, rim, first, second = call(
        spread_kernel, SPREAD_OUT, [terms], place, where, rest, scale, base, high, low, name="spread"
    )
    for substep in range(SUBSTEPS):
        first_x, second_x = exchange(first, second, "gx")
        corner = call(
            force_corner_kernel, [((3, 8, CZ), F32)] * 2, [], place, rim, first_x, second_x,
            name="force_corner",
        )
        first_y, second_y = exchange(*corner, "gy")
        stepped, force, first, second = call(
            collide_kernel,
            [STEPPED, ((3, 4, 8, CZ), F32), ((15, 8, CZ), F32), ((15, 8, CZ), F32)],
            [],
            place, populations, solid, main, first_x, second_x, first_y, second_y,
            name="collide",
        )
        first_x, second_x = exchange(first, second, "gx")
        stepped, inside, leaving, first, second = call(
            flow_corner_kernel,
            [
                ((19 * 4 * 8, CZ), F32), ((4 * 8 * 8, CZ), F32), ((6, 8, CZ), F32),
                ((13, 8, CZ), F32), ((13, 8, CZ), F32),
            ],
            [((3 * 8 * 8, CZ), F32), ((5, 8, CZ), F32), ((13, 8, CZ), F32)][:1]
            + [((9, 8, CZ), F32), ((13, 8, CZ), F32)],
            place, stepped, force, first_x, second_x,
            name="flow_corner",
        )
        first_y, second_y = exchange(first, second, "gy")
        fluid = (place, stepped, inside, leaving, first_y, second_y)
        if substep < SUBSTEPS - 1:
            populations, where, main, rim, first, second = call(
                next_kernel, [STEPPED, ((8, PAD), F32)] + SPREAD_OUT, [flow, terms],
                *fluid, where, rest, scale, live, base, high, low, name="next",
            )
        else:
            populations, where = call(
                last_kernel, [STEPPED, ((8, PAD), F32)], [flow], *fluid, where, live, base, name="last"
            )
    return populations, where[:6].reshape(offset.shape)


def solution(mesh):
    in_specs = (
        P(None, "gx", "gy", None),
        P("gx", "gy", None),
        P(None, "gx", "gy", None, None),
        P(None, "gx", "gy", None, None),
        P(None, "gx", "gy", None, None),
        P("gx", "gy", None),
        P("gx", "gy", None),
        P(),
    )
    out_specs = (P(None, "gx", "gy", None), P(None, "gx", "gy", None, None))
    return jax.shard_map(local, mesh=mesh, in_specs=in_specs, out_specs=out_specs, check_vma=False)
```

profile of v0, /device:TPU:1, one launch (start us, length us, event | category | flops | bytes accessed | tf_op | source)
XLA Modules:
  0.0 134.1 jit_solution(1740112901537531874)
XLA Ops:
  0.6 0.7 bitcast_multiply_fusion
  1.3 0.1 broadcast_in_dim.16
  1.4 0.1 pad_add_fusion.1
  1.6 0.1 sub.14
  1.6 0.7 reshape.49
  2.4 0.1 broadcast_subtract_fusion
  2.5 0.7 reshape.46
  3.2 0.7 reshape.47
  4.0 0.7 copy-done.2
  4.7 2.4 %links.1 = (bf16[768,768]{1,0:T(8,128)(2,1)S(1)}, bf16[768,768]{1,0:T(8,128)(2,1)S(1)}) custom-call(s32[3,1280]{1,0:T(4,128)S(1)} %bitcast.14), custom_call_target="tpu_custom_call" | custom-call | tf_op jit(solution)/shard_map/links/pallas_call | solution.py:493
  7.2 0.1 pad_add_fusion.place_ref
  7.3 2.0 %spread.1 = (f32[3,7,8,128]{3,2,1,0:T(8,128)S(1)}, f32[3,3,8,128]{3,2,1,0:T(8,128)S(1)}, f32[3,3,8,128]{3,2,1,0:T(8,128)S(1)}, f32[3,3,8,128]{3,2,1,0:T(8,128)S(1)}) custom-call(s32[2]{0:T(128)S(1)} %pad_add_fusion.place_ref, f32[8,768]{1,0:T(8,128)S(1)} %pad.21.offset_ref, f32[8,768]{1,0:T(8,128)S(1)} %pad.22.rest_ref, f32[8,768]{1,0:T(8,128)S(1)} %pad.24.scale_ref, ...), custom_call_target="tpu_custom_call" | custom-call | tf_op jit(solution)/shard_map/spread/pallas_call | solution.py:493
  9.3 3.3 %collective-permute-start = (f32[3,3,8,128]{3,2,1,0:T(8,128)S(1)}, f32[3,3,8,128]{3,2,1,0:T(8,128)S(1)}, u32[]{:S(2)}, u32[]{:S(2)}) collective-permute-start(f32[3,3,8,128]{3,2,1,0:T(8,128)S(1)} %get-tuple-element.58), channel_id=1, source_target_pairs={{0,16},{16,0},{32,48},{48,32},{64,80},{80,64},{96,112},{112,96},{1... | collective-permute-start | bytes 110600 | tf_op jit(solution)/shard_map/ppermute | solution.py:514
  12.6 5.2 %collective-permute-start.1 = (f32[3,3,8,128]{3,2,1,0:T(8,128)S(1)}, f32[3,3,8,128]{3,2,1,0:T(8,128)S(1)}, u32[]{:S(2)}, u32[]{:S(2)}) collective-permute-start(f32[3,3,8,128]{3,2,1,0:T(8,128)S(1)} %get-tuple-element.59), channel_id=1, source_target_pairs={{0,240},{16,32},{32,16},{48,64},{64,48},{80,96},{96,80},{112,128},... | collective-permute-start | bytes 110600 | tf_op jit(solution)/shard_map/ppermute | solution.py:514
  17.8 2.1 %collective-permute-done.1.second_in.second_x = f32[3,3,8,128]{3,2,1,0:T(8,128)S(1)} collective-permute-done((f32[3,3,8,128]{3,2,1,0:T(8,128)S(1)}, f32[3,3,8,128]{3,2,1,0:T(8,128)S(1)}, u32[]{:S(2)}, u32[]{:S(2)}) %collective-permute-start.1) | collective-permute-done | bytes 36896 | tf_op jit(solution)/shard_map/ppermute | solution.py:514
  19.9 0.6 force_corner.3
  20.4 0.7 collective-permute-start.2
  21.1 5.4 %collective-permute-start.3 = (f32[3,8,128]{2,1,0:T(8,128)S(1)}, f32[3,8,128]{2,1,0:T(8,128)S(1)}, u32[]{:S(2)}, u32[]{:S(2)}) collective-permute-start(f32[3,8,128]{2,1,0:T(8,128)S(1)} %get-tuple-element.62), channel_id=1, source_target_pairs={{0,15},{1,2},{2,1},{3,4},{4,3},{5,6},{6,5},{7,8},{8,7},{9,10},{10,... | collective-permute-start | bytes 36872 | tf_op jit(solution)/shard_map/ppermute | solution.py:514
  26.5 1.2 collective-permute-done.3.second_y
  27.7 0.9 collide.3
  28.6 4.0 %collective-permute-start.4 = (f32[15,8,128]{2,1,0:T(8,128)S(1)}, f32[15,8,128]{2,1,0:T(8,128)S(1)}, u32[]{:S(2)}, u32[]{:S(2)}) collective-permute-start(f32[15,8,128]{2,1,0:T(8,128)S(1)} %get-tuple-element.65), channel_id=1, source_target_pairs={{0,16},{16,0},{32,48},{48,32},{64,80},{80,64},{96,112},{112,96},{1... | collective-permute-start | bytes 184328 | tf_op jit(solution)/shard_map/ppermute | solution.py:514
  32.6 2.9 %collective-permute-start.5 = (f32[15,8,128]{2,1,0:T(8,128)S(1)}, f32[15,8,128]{2,1,0:T(8,128)S(1)}, u32[]{:S(2)}, u32[]{:S(2)}) collective-permute-start(f32[15,8,128]{2,1,0:T(8,128)S(1)} %get-tuple-element.66), channel_id=1, source_target_pairs={{0,240},{16,32},{32,16},{48,64},{64,48},{80,96},{96,80},{112,128},... | collective-permute-start | bytes 184328 | tf_op jit(solution)/shard_map/ppermute | solution.py:514
  35.5 4.7 %collective-permute-done.5.second_x = f32[15,8,128]{2,1,0:T(8,128)S(1)} collective-permute-done((f32[15,8,128]{2,1,0:T(8,128)S(1)}, f32[15,8,128]{2,1,0:T(8,128)S(1)}, u32[]{:S(2)}, u32[]{:S(2)}) %collective-permute-start.5) | collective-permute-done | bytes 61472 | tf_op jit(solution)/shard_map/ppermute | solution.py:514
  40.1 0.6 flow_corner.3
  40.8 0.1 collective-permute-start.6
  40.9 5.3 %collective-permute-start.7 = (f32[13,8,128]{2,1,0:T(8,128)S(1)}, f32[13,8,128]{2,1,0:T(8,128)S(1)}, u32[]{:S(2)}, u32[]{:S(2)}) collective-permute-start(f32[13,8,128]{2,1,0:T(8,128)S(1)} %get-tuple-element.71), channel_id=1, source_target_pairs={{0,15},{1,2},{2,1},{3,4},{4,3},{5,6},{6,5},{7,8},{8,7},{9,10},{10,... | collective-permute-start | bytes 159752 | tf_op jit(solution)/shard_map/ppermute | solution.py:514
  46.2 0.1 broadcast_in_dim.18
  46.3 2.0 %collective-permute-done.7.second_y = f32[13,8,128]{2,1,0:T(8,128)S(1)} collective-permute-done((f32[13,8,128]{2,1,0:T(8,128)S(1)}, f32[13,8,128]{2,1,0:T(8,128)S(1)}, u32[]{:S(2)}, u32[]{:S(2)}) %collective-permute-start.7) | collective-permute-done | bytes 53280 | tf_op jit(solution)/shard_map/ppermute | solution.py:514
  48.4 3.5 %next.2 = (f32[19,4,8,128]{3,2,1,0:T(8,128)S(1)}, f32[8,768]{1,0:T(8,128)S(1)}, f32[3,7,8,128]{3,2,1,0:T(8,128)S(1)}, f32[3,3,8,128]{3,2,1,0:T(8,128)S(1)}, f32[...) custom-call(s32[2]{0:T(128)S(1)} %pad_add_fusion.place_ref, f32[608,128]{1,0:T(8,128)S(1)} %get-tuple-element.67.stepped_ref, ...), custom_call_target="tpu_custom_call" | custom-call | tf_op jit(solution)/shard_map/next/pallas_call | solution.py:493
  51.8 3.9 %collective-permute-start.8 = (f32[3,3,8,128]{3,2,1,0:T(8,128)S(1)}, f32[3,3,8,128]{3,2,1,0:T(8,128)S(1)}, u32[]{:S(2)}, u32[]{:S(2)}) collective-permute-start(f32[3,3,8,128]{3,2,1,0:T(8,128)S(1)} %get-tuple-element.74), channel_id=1, source_target_pairs={{0,16},{16,0},{32,48},{48,32},{64,80},{80,64},{96,112},{112,96},{1... | collective-permute-start | bytes 110600 | tf_op jit(solution)/shard_map/ppermute | solution.py:514
  55.7 0.3 collective-permute-start.9
  56.0 0.6 collective-permute-done.8.first_in.first_x
  56.6 6.6 %collective-permute-done.9.second_in.second_x = f32[3,3,8,128]{3,2,1,0:T(8,128)S(1)} collective-permute-done((f32[3,3,8,128]{3,2,1,0:T(8,128)S(1)}, f32[3,3,8,128]{3,2,1,0:T(8,128)S(1)}, u32[]{:S(2)}, u32[]{:S(2)}) %collective-permute-start.9) | collective-permute-done | bytes 36896 | tf_op jit(solution)/shard_map/ppermute | solution.py:514
  63.3 0.6 force_corner.4
  63.8 0.1 collective-permute-start.10
  63.9 3.2 %collective-permute-start.11 = (f32[3,8,128]{2,1,0:T(8,128)S(1)}, f32[3,8,128]{2,1,0:T(8,128)S(1)}, u32[]{:S(2)}, u32[]{:S(2)}) collective-permute-start(f32[3,8,128]{2,1,0:T(8,128)S(1)} %get-tuple-element.78), channel_id=1, source_target_pairs={{0,15},{1,2},{2,1},{3,4},{4,3},{5,6},{6,5},{7,8},{8,7},{9,10},{10,... | collective-permute-start | bytes 36872 | tf_op jit(solution)/shard_map/ppermute | solution.py:514
  67.2 3.3 %collective-permute-done.11.second_y = f32[3,8,128]{2,1,0:T(8,128)S(1)} collective-permute-done((f32[3,8,128]{2,1,0:T(8,128)S(1)}, f32[3,8,128]{2,1,0:T(8,128)S(1)}, u32[]{:S(2)}, u32[]{:S(2)}) %collective-permute-start.11) | collective-permute-done | bytes 12320 | tf_op jit(solution)/shard_map/ppermute | solution.py:514
  70.5 0.9 collide.4
  71.4 3.3 %collective-permute-start.12 = (f32[15,8,128]{2,1,0:T(8,128)S(1)}, f32[15,8,128]{2,1,0:T(8,128)S(1)}, u32[]{:S(2)}, u32[]{:S(2)}) collective-permute-start(f32[15,8,128]{2,1,0:T(8,128)S(1)} %get-tuple-element.81), channel_id=1, source_target_pairs={{0,16},{16,0},{32,48},{48,32},{64,80},{80,64},{96,112},{112,96},{1... | collective-permute-start | bytes 184328 | tf_op jit(solution)/shard_map/ppermute | solution.py:514
  74.7 0.9 collective-permute-done.12.first_x
  75.6 6.7 %collective-permute-done.13.second_x = f32[15,8,128]{2,1,0:T(8,128)S(1)} collective-permute-done((f32[15,8,128]{2,1,0:T(8,128)S(1)}, f32[15,8,128]{2,1,0:T(8,128)S(1)}, u32[]{:S(2)}, u32[]{:S(2)}) %collective-permute-start.13) | collective-permute-done | bytes 61472 | tf_op jit(solution)/shard_map/ppermute | solution.py:514
  82.3 0.6 flow_corner.4
  82.9 0.1 collective-permute-start.14
  83.0 3.4 %collective-permute-start.15 = (f32[13,8,128]{2,1,0:T(8,128)S(1)}, f32[13,8,128]{2,1,0:T(8,128)S(1)}, u32[]{:S(2)}, u32[]{:S(2)}) collective-permute-start(f32[13,8,128]{2,1,0:T(8,128)S(1)} %get-tuple-element.87), channel_id=1, source_target_pairs={{0,15},{1,2},{2,1},{3,4},{4,3},{5,6},{6,5},{7,8},{8,7},{9,10},{10,... | collective-permute-start | bytes 159752 | tf_op jit(solution)/shard_map/ppermute | solution.py:514
  86.4 0.2 collective-permute-done.14.first_y
  86.6 3.8 %collective-permute-done.15.second_y = f32[13,8,128]{2,1,0:T(8,128)S(1)} collective-permute-done((f32[13,8,128]{2,1,0:T(8,128)S(1)}, f32[13,8,128]{2,1,0:T(8,128)S(1)}, u32[]{:S(2)}, u32[]{:S(2)}) %collective-permute-start.15) | collective-permute-done | bytes 53280 | tf_op jit(solution)/shard_map/ppermute | solution.py:514
  90.3 3.5 %next.3 = (f32[19,4,8,128]{3,2,1,0:T(8,128)S(1)}, f32[8,768]{1,0:T(8,128)S(1)}, f32[3,7,8,128]{3,2,1,0:T(8,128)S(1)}, f32[3,3,8,128]{3,2,1,0:T(8,128)S(1)}, f32[...) custom-call(s32[2]{0:T(128)S(1)} %pad_add_fusion.place_ref, f32[608,128]{1,0:T(8,128)S(1)} %get-tuple-element.83.stepped_ref, ...), custom_call_target="tpu_custom_call" | custom-call | tf_op jit(solution)/shard_map/next/pallas_call | solution.py:493
  93.8 3.1 %collective-permute-start.16 = (f32[3,3,8,128]{3,2,1,0:T(8,128)S(1)}, f32[3,3,8,128]{3,2,1,0:T(8,128)S(1)}, u32[]{:S(2)}, u32[]{:S(2)}) collective-permute-start(f32[3,3,8,128]{3,2,1,0:T(8,128)S(1)} %get-tuple-element.91), channel_id=1, source_target_pairs={{0,16},{16,0},{32,48},{48,32},{64,80},{80,64},{96,112},{112,96},{1... | collective-permute-start | bytes 110600 | tf_op jit(solution)/shard_map/ppermute | solution.py:514
  96.9 0.9 collective-permute-done.16.first_in.first_x
  97.8 6.4 %collective-permute-done.17.second_in.second_x = f32[3,3,8,128]{3,2,1,0:T(8,128)S(1)} collective-permute-done((f32[3,3,8,128]{3,2,1,0:T(8,128)S(1)}, f32[3,3,8,128]{3,2,1,0:T(8,128)S(1)}, u32[]{:S(2)}, u32[]{:S(2)}) %collective-permute-start.17) | collective-permute-done | bytes 36896 | tf_op jit(solution)/shard_map/ppermute | solution.py:514
  104.2 0.6 force_corner.5
  104.8 0.1 collective-permute-start.18
  104.9 3.4 %collective-permute-start.19 = (f32[3,8,128]{2,1,0:T(8,128)S(1)}, f32[3,8,128]{2,1,0:T(8,128)S(1)}, u32[]{:S(2)}, u32[]{:S(2)}) collective-permute-start(f32[3,8,128]{2,1,0:T(8,128)S(1)} %get-tuple-element.95), channel_id=1, source_target_pairs={{0,15},{1,2},{2,1},{3,4},{4,3},{5,6},{6,5},{7,8},{8,7},{9,10},{10,... | collective-permute-start | bytes 36872 | tf_op jit(solution)/shard_map/ppermute | solution.py:514
  108.3 3.2 %collective-permute-done.19.second_y = f32[3,8,128]{2,1,0:T(8,128)S(1)} collective-permute-done((f32[3,8,128]{2,1,0:T(8,128)S(1)}, f32[3,8,128]{2,1,0:T(8,128)S(1)}, u32[]{:S(2)}, u32[]{:S(2)}) %collective-permute-start.19) | collective-permute-done | bytes 12320 | tf_op jit(solution)/shard_map/ppermute | solution.py:514
  111.4 0.9 collide.5
  112.3 3.4 %collective-permute-start.20 = (f32[15,8,128]{2,1,0:T(8,128)S(1)}, f32[15,8,128]{2,1,0:T(8,128)S(1)}, u32[]{:S(2)}, u32[]{:S(2)}) collective-permute-start(f32[15,8,128]{2,1,0:T(8,128)S(1)} %get-tuple-element.98), channel_id=1, source_target_pairs={{0,16},{16,0},{32,48},{48,32},{64,80},{80,64},{96,112},{112,96},{1... | collective-permute-start | bytes 184328 | tf_op jit(solution)/shard_map/ppermute | solution.py:514
  115.7 0.9 collective-permute-done.20.first_x
  116.6 6.8 %collective-permute-done.21.second_x = f32[15,8,128]{2,1,0:T(8,128)S(1)} collective-permute-done((f32[15,8,128]{2,1,0:T(8,128)S(1)}, f32[15,8,128]{2,1,0:T(8,128)S(1)}, u32[]{:S(2)}, u32[]{:S(2)}) %collective-permute-start.21) | collective-permute-done | bytes 61472 | tf_op jit(solution)/shard_map/ppermute | solution.py:514
  123.4 0.6 flow_corner.5
  124.0 0.1 collective-permute-start.22
  124.1 3.6 %collective-permute-start.23 = (f32[13,8,128]{2,1,0:T(8,128)S(1)}, f32[13,8,128]{2,1,0:T(8,128)S(1)}, u32[]{:S(2)}, u32[]{:S(2)}) collective-permute-start(f32[13,8,128]{2,1,0:T(8,128)S(1)} %get-tuple-element.104), channel_id=1, source_target_pairs={{0,15},{1,2},{2,1},{3,4},{4,3},{5,6},{6,5},{7,8},{8,7},{9,10},{10,... | collective-permute-start | bytes 159752 | tf_op jit(solution)/shard_map/ppermute | solution.py:514
  127.7 3.6 %collective-permute-done.23.second_y = f32[13,8,128]{2,1,0:T(8,128)S(1)} collective-permute-done((f32[13,8,128]{2,1,0:T(8,128)S(1)}, f32[13,8,128]{2,1,0:T(8,128)S(1)}, u32[]{:S(2)}, u32[]{:S(2)}) %collective-permute-start.23) | collective-permute-done | bytes 53280 | tf_op jit(solution)/shard_map/ppermute | solution.py:514
  131.3 2.2 %last.1 = (f32[19,4,8,128]{3,2,1,0:T(8,128)}, f32[8,768]{1,0:T(8,128)S(1)}) custom-call(s32[2]{0:T(128)S(1)} %pad_add_fusion.place_ref, f32[608,128]{1,0:T(8,128)S(1)} %get-tuple-element.100.stepped_ref, f32[256,128]{1,0:T(8,128)S(1)} %get-tuple-element.101.inside_ref, f32[6,8,128]{2,1,0:T(8,128)S(1)} %get-tuple-element.102.leaving_ref, ...), custom_call_target="tpu_custom_call" | custom-call | tf_op jit(solution)/shard_map/last/pallas_call | solution.py:493
  133.5 0.6 reshape.50
  (28 shorter events, 0.3 us)
Async XLA Ops:
  4.0 0.7 copy-start.2
  7.3 20.4 %copy-start = (f32[19,4,8,128]{3,2,1,0:T(8,128)S(1)}, f32[19,4,8,128]{3,2,1,0:T(8,128)}, u32[]{:S(2)}) copy-start(f32[19,4,8,128]{3,2,1,0:T(8,128)} %populations_ref.1) | copy-start | bytes 933892
  7.3 20.4 %copy-start.1 = (s32[4,8,128]{2,1,0:T(8,128)S(1)}, s32[4,8,128]{2,1,0:T(8,128)}, u32[]{:S(2)}) copy-start(s32[4,8,128]{2,1,0:T(8,128)} %solid_ref.5) | copy-start | bytes 49156
  7.3 38.9 %copy-start.3 = (s32[1,1,2]{2,1,0:T(1,128)S(1)}, s32[1,1,2]{2,1,0:T(1,128)}, u32[]{:S(2)}) copy-start(s32[1,1,2]{2,1,0:T(1,128)} %param.14) | copy-start | bytes 28
  9.3 8.5 %collective-permute-start = (f32[3,3,8,128]{3,2,1,0:T(8,128)S(1)}, f32[3,3,8,128]{3,2,1,0:T(8,128)S(1)}, u32[]{:S(2)}, u32[]{:S(2)}) collective-permute-start(f32[3,3,8,128]{3,2,1,0:T(8,128)S(1)} %get-tuple-element.58), channel_id=1, source_target_pairs={{0,16},{16,0},{32,48},{48,32},{64,80},{80,64},{96,112},{112,96},{1... | collective-permute-start | bytes 110600 | tf_op jit(solution)/shard_map/ppermute | solution.py:514
  12.6 7.3 %collective-permute-start.1 = (f32[3,3,8,128]{3,2,1,0:T(8,128)S(1)}, f32[3,3,8,128]{3,2,1,0:T(8,128)S(1)}, u32[]{:S(2)}, u32[]{:S(2)}) collective-permute-start(f32[3,3,8,128]{3,2,1,0:T(8,128)S(1)} %get-tuple-element.59), channel_id=1, source_target_pairs={{0,240},{16,32},{32,16},{48,64},{64,48},{80,96},{96,80},{112,128},... | collective-permute-start | bytes 110600 | tf_op jit(solution)/shard_map/ppermute | solution.py:514
  20.4 6.1 %collective-permute-start.2 = (f32[3,8,128]{2,1,0:T(8,128)S(1)}, f32[3,8,128]{2,1,0:T(8,128)S(1)}, u32[]{:S(2)}, u32[]{:S(2)}) collective-permute-start(f32[3,8,128]{2,1,0:T(8,128)S(1)} %get-tuple-element.61), channel_id=1, source_target_pairs={{0,1},{1,0},{2,3},{3,2},{4,5},{5,4},{6,7},{7,6},{8,9},{9,8},{10,11... | collective-permute-start | bytes 36872 | tf_op jit(solution)/shard_map/ppermute | solution.py:514
  21.1 6.6 %collective-permute-start.3 = (f32[3,8,128]{2,1,0:T(8,128)S(1)}, f32[3,8,128]{2,1,0:T(8,128)S(1)}, u32[]{:S(2)}, u32[]{:S(2)}) collective-permute-start(f32[3,8,128]{2,1,0:T(8,128)S(1)} %get-tuple-element.62), channel_id=1, source_target_pairs={{0,15},{1,2},{2,1},{3,4},{4,3},{5,6},{6,5},{7,8},{8,7},{9,10},{10,... | collective-permute-start | bytes 36872 | tf_op jit(solution)/shard_map/ppermute | solution.py:514
  28.6 6.9 %collective-permute-start.4 = (f32[15,8,128]{2,1,0:T(8,128)S(1)}, f32[15,8,128]{2,1,0:T(8,128)S(1)}, u32[]{:S(2)}, u32[]{:S(2)}) collective-permute-start(f32[15,8,128]{2,1,0:T(8,128)S(1)} %get-tuple-element.65), channel_id=1, source_target_pairs={{0,16},{16,0},{32,48},{48,32},{64,80},{80,64},{96,112},{112,96},{1... | collective-permute-start | bytes 184328 | tf_op jit(solution)/shard_map/ppermute | solution.py:514
  32.6 7.6 %collective-permute-start.5 = (f32[15,8,128]{2,1,0:T(8,128)S(1)}, f32[15,8,128]{2,1,0:T(8,128)S(1)}, u32[]{:S(2)}, u32[]{:S(2)}) collective-permute-start(f32[15,8,128]{2,1,0:T(8,128)S(1)} %get-tuple-element.66), channel_id=1, source_target_pairs={{0,240},{16,32},{32,16},{48,64},{64,48},{80,96},{96,80},{112,128},... | collective-permute-start | bytes 184328 | tf_op jit(solution)/shard_map/ppermute | solution.py:514
  40.8 5.5 %collective-permute-start.6 = (f32[13,8,128]{2,1,0:T(8,128)S(1)}, f32[13,8,128]{2,1,0:T(8,128)S(1)}, u32[]{:S(2)}, u32[]{:S(2)}) collective-permute-start(f32[13,8,128]{2,1,0:T(8,128)S(1)} %get-tuple-element.70), channel_id=1, source_target_pairs={{0,1},{1,0},{2,3},{3,2},{4,5},{5,4},{6,7},{7,6},{8,9},{9,8},{10,11... | collective-permute-start | bytes 159752 | tf_op jit(solution)/shard_map/ppermute | solution.py:514
  40.9 7.4 %collective-permute-start.7 = (f32[13,8,128]{2,1,0:T(8,128)S(1)}, f32[13,8,128]{2,1,0:T(8,128)S(1)}, u32[]{:S(2)}, u32[]{:S(2)}) collective-permute-start(f32[13,8,128]{2,1,0:T(8,128)S(1)} %get-tuple-element.71), channel_id=1, source_target_pairs={{0,15},{1,2},{2,1},{3,4},{4,3},{5,6},{6,5},{7,8},{8,7},{9,10},{10,... | collective-permute-start | bytes 159752 | tf_op jit(solution)/shard_map/ppermute | solution.py:514
  51.8 4.8 %collective-permute-start.8 = (f32[3,3,8,128]{3,2,1,0:T(8,128)S(1)}, f32[3,3,8,128]{3,2,1,0:T(8,128)S(1)}, u32[]{:S(2)}, u32[]{:S(2)}) collective-permute-start(f32[3,3,8,128]{3,2,1,0:T(8,128)S(1)} %get-tuple-element.74), channel_id=1, source_target_pairs={{0,16},{16,0},{32,48},{48,32},{64,80},{80,64},{96,112},{112,96},{1... | collective-permute-start | bytes 110600 | tf_op jit(solution)/shard_map/ppermute | solution.py:514
  55.7 7.5 %collective-permute-start.9 = (f32[3,3,8,128]{3,2,1,0:T(8,128)S(1)}, f32[3,3,8,128]{3,2,1,0:T(8,128)S(1)}, u32[]{:S(2)}, u32[]{:S(2)}) collective-permute-start(f32[3,3,8,128]{3,2,1,0:T(8,128)S(1)} %get-tuple-element.75), channel_id=1, source_target_pairs={{0,240},{16,32},{32,16},{48,64},{64,48},{80,96},{96,80},{112,128},... | collective-permute-start | bytes 110600 | tf_op jit(solution)/shard_map/ppermute | solution.py:514
  63.8 3.3 %collective-permute-start.10 = (f32[3,8,128]{2,1,0:T(8,128)S(1)}, f32[3,8,128]{2,1,0:T(8,128)S(1)}, u32[]{:S(2)}, u32[]{:S(2)}) collective-permute-start(f32[3,8,128]{2,1,0:T(8,128)S(1)} %get-tuple-element.77), channel_id=1, source_target_pairs={{0,1},{1,0},{2,3},{3,2},{4,5},{5,4},{6,7},{7,6},{8,9},{9,8},{10,11... | collective-permute-start | bytes 36872 | tf_op jit(solution)/shard_map/ppermute | solution.py:514
  63.9 6.6 %collective-permute-start.11 = (f32[3,8,128]{2,1,0:T(8,128)S(1)}, f32[3,8,128]{2,1,0:T(8,128)S(1)}, u32[]{:S(2)}, u32[]{:S(2)}) collective-permute-start(f32[3,8,128]{2,1,0:T(8,128)S(1)} %get-tuple-element.78), channel_id=1, source_target_pairs={{0,15},{1,2},{2,1},{3,4},{4,3},{5,6},{6,5},{7,8},{8,7},{9,10},{10,... | collective-permute-start | bytes 36872 | tf_op jit(solution)/shard_map/ppermute | solution.py:514
  71.4 4.2 %collective-permute-start.12 = (f32[15,8,128]{2,1,0:T(8,128)S(1)}, f32[15,8,128]{2,1,0:T(8,128)S(1)}, u32[]{:S(2)}, u32[]{:S(2)}) collective-permute-start(f32[15,8,128]{2,1,0:T(8,128)S(1)} %get-tuple-element.81), channel_id=1, source_target_pairs={{0,16},{16,0},{32,48},{48,32},{64,80},{80,64},{96,112},{112,96},{1... | collective-permute-start | bytes 184328 | tf_op jit(solution)/shard_map/ppermute | solution.py:514
  74.7 7.6 %collective-permute-start.13 = (f32[15,8,128]{2,1,0:T(8,128)S(1)}, f32[15,8,128]{2,1,0:T(8,128)S(1)}, u32[]{:S(2)}, u32[]{:S(2)}) collective-permute-start(f32[15,8,128]{2,1,0:T(8,128)S(1)} %get-tuple-element.82), channel_id=1, source_target_pairs={{0,240},{16,32},{32,16},{48,64},{64,48},{80,96},{96,80},{112,128},... | collective-permute-start | bytes 184328 | tf_op jit(solution)/shard_map/ppermute | solution.py:514
  82.9 3.6 %collective-permute-start.14 = (f32[13,8,128]{2,1,0:T(8,128)S(1)}, f32[13,8,128]{2,1,0:T(8,128)S(1)}, u32[]{:S(2)}, u32[]{:S(2)}) collective-permute-start(f32[13,8,128]{2,1,0:T(8,128)S(1)} %get-tuple-element.86), channel_id=1, source_target_pairs={{0,1},{1,0},{2,3},{3,2},{4,5},{5,4},{6,7},{7,6},{8,9},{9,8},{10,11... | collective-permute-start | bytes 159752 | tf_op jit(solution)/shard_map/ppermute | solution.py:514
  83.0 7.3 %collective-permute-start.15 = (f32[13,8,128]{2,1,0:T(8,128)S(1)}, f32[13,8,128]{2,1,0:T(8,128)S(1)}, u32[]{:S(2)}, u32[]{:S(2)}) collective-permute-start(f32[13,8,128]{2,1,0:T(8,128)S(1)} %get-tuple-element.87), channel_id=1, source_target_pairs={{0,15},{1,2},{2,1},{3,4},{4,3},{5,6},{6,5},{7,8},{8,7},{9,10},{10,... | collective-permute-start | bytes 159752 | tf_op jit(solution)/shard_map/ppermute | solution.py:514
  93.8 4.0 %collective-permute-start.16 = (f32[3,3,8,128]{3,2,1,0:T(8,128)S(1)}, f32[3,3,8,128]{3,2,1,0:T(8,128)S(1)}, u32[]{:S(2)}, u32[]{:S(2)}) collective-permute-start(f32[3,3,8,128]{3,2,1,0:T(8,128)S(1)} %get-tuple-element.91), channel_id=1, source_target_pairs={{0,16},{16,0},{32,48},{48,32},{64,80},{80,64},{96,112},{112,96},{1... | collective-permute-start | bytes 110600 | tf_op jit(solution)/shard_map/ppermute | solution.py:514
  96.9 7.3 %collective-permute-start.17 = (f32[3,3,8,128]{3,2,1,0:T(8,128)S(1)}, f32[3,3,8,128]{3,2,1,0:T(8,128)S(1)}, u32[]{:S(2)}, u32[]{:S(2)}) collective-permute-start(f32[3,3,8,128]{3,2,1,0:T(8,128)S(1)} %get-tuple-element.92), channel_id=1, source_target_pairs={{0,240},{16,32},{32,16},{48,64},{64,48},{80,96},{96,80},{112,128},... | collective-permute-start | bytes 110600 | tf_op jit(solution)/shard_map/ppermute | solution.py:514
  104.8 3.5 %collective-permute-start.18 = (f32[3,8,128]{2,1,0:T(8,128)S(1)}, f32[3,8,128]{2,1,0:T(8,128)S(1)}, u32[]{:S(2)}, u32[]{:S(2)}) collective-permute-start(f32[3,8,128]{2,1,0:T(8,128)S(1)} %get-tuple-element.94), channel_id=1, source_target_pairs={{0,1},{1,0},{2,3},{3,2},{4,5},{5,4},{6,7},{7,6},{8,9},{9,8},{10,11... | collective-permute-start | bytes 36872 | tf_op jit(solution)/shard_map/ppermute | solution.py:514
  104.9 6.5 %collective-permute-start.19 = (f32[3,8,128]{2,1,0:T(8,128)S(1)}, f32[3,8,128]{2,1,0:T(8,128)S(1)}, u32[]{:S(2)}, u32[]{:S(2)}) collective-permute-start(f32[3,8,128]{2,1,0:T(8,128)S(1)} %get-tuple-element.95), channel_id=1, source_target_pairs={{0,15},{1,2},{2,1},{3,4},{4,3},{5,6},{6,5},{7,8},{8,7},{9,10},{10,... | collective-permute-start | bytes 36872 | tf_op jit(solution)/shard_map/ppermute | solution.py:514
  112.3 4.3 %collective-permute-start.20 = (f32[15,8,128]{2,1,0:T(8,128)S(1)}, f32[15,8,128]{2,1,0:T(8,128)S(1)}, u32[]{:S(2)}, u32[]{:S(2)}) collective-permute-start(f32[15,8,128]{2,1,0:T(8,128)S(1)} %get-tuple-element.98), channel_id=1, source_target_pairs={{0,16},{16,0},{32,48},{48,32},{64,80},{80,64},{96,112},{112,96},{1... | collective-permute-start | bytes 184328 | tf_op jit(solution)/shard_map/ppermute | solution.py:514
  115.7 7.7 %collective-permute-start.21 = (f32[15,8,128]{2,1,0:T(8,128)S(1)}, f32[15,8,128]{2,1,0:T(8,128)S(1)}, u32[]{:S(2)}, u32[]{:S(2)}) collective-permute-start(f32[15,8,128]{2,1,0:T(8,128)S(1)} %get-tuple-element.99), channel_id=1, source_target_pairs={{0,240},{16,32},{32,16},{48,64},{64,48},{80,96},{96,80},{112,128},... | collective-permute-start | bytes 184328 | tf_op jit(solution)/shard_map/ppermute | solution.py:514
  124.0 3.7 %collective-permute-start.22 = (f32[13,8,128]{2,1,0:T(8,128)S(1)}, f32[13,8,128]{2,1,0:T(8,128)S(1)}, u32[]{:S(2)}, u32[]{:S(2)}) collective-permute-start(f32[13,8,128]{2,1,0:T(8,128)S(1)} %get-tuple-element.103), channel_id=1, source_target_pairs={{0,1},{1,0},{2,3},{3,2},{4,5},{5,4},{6,7},{7,6},{8,9},{9,8},{10,11... | collective-permute-start | bytes 159752 | tf_op jit(solution)/shard_map/ppermute | solution.py:514
  124.1 7.1 %collective-permute-start.23 = (f32[13,8,128]{2,1,0:T(8,128)S(1)}, f32[13,8,128]{2,1,0:T(8,128)S(1)}, u32[]{:S(2)}, u32[]{:S(2)}) collective-permute-start(f32[13,8,128]{2,1,0:T(8,128)S(1)} %get-tuple-element.104), channel_id=1, source_target_pairs={{0,15},{1,2},{2,1},{3,4},{4,3},{5,6},{6,5},{7,8},{8,7},{9,10},{10,... | collective-permute-start | bytes 159752 | tf_op jit(solution)/shard_map/ppermute | solution.py:514
where the time goes:
time: 134 us
  starting transfers between devices  54.8 us (41%)
  waiting for transfers between devices  53.8 us (40%)
  Pallas kernels  19.8 us (15%)
  local copies, waits for them, and re-layouts  4.08 us (3%)
    ppermute x24, starting transfers between devices, exchange(): out.append(lax.ppermute(message, axis, pairs))  54.8 us
    ppermute x24, waiting for transfers between devices, exchange(): out.append(lax.ppermute(message, axis, pairs))  53.8 us
    pallas_call x14, Pallas kernels, call(): pl.pallas_call(kernel, out_shape=[jax.ShapeDtypeStruct(shape, dtype) for...  19.8 us
  transfers between devices with their start and end apart: 24, of which 17 were waited for; matrix products, arithmetic and copies ran while one was open for 0% of the time, Pallas kernels for 0%

commit v1 on v0

--- a/solution.py
+++ b/solution.py
@@ -55,6 +55,21 @@
     return lax.broadcasted_iota(jnp.int32, TILE, 0)
 
 
+def wide(row):
+    return jnp.concatenate([row] * (PAD // CZ), axis=1)
+
+
+def six_rows(ref):
+    return jnp.concatenate([ref[0], ref[1], ref[2], jnp.zeros((2, PAD), ref.dtype)], axis=0)
+
+
+def own_base(info_ref, base_ref):
+    base = six_rows(base_ref)
+    rows = lax.broadcasted_iota(jnp.int32, TILE, 0)
+    start = jnp.where(rows < 2, info_ref[2], jnp.where(rows < 4, info_ref[3], 0.0))
+    return base - wide(start.astype(jnp.int32))
+
+
 def row_of(tile, r):
     return jnp.broadcast_to(tile[r : r + 1, :], (8, tile.shape[1]))
 
@@ -89,19 +104,26 @@
     return table_x, table_y, table_rim, table_z
 
 
-def vertex_force(offset, rest, scale, links_high, links_low):
+def halves(rows):
+    high = rows.astype(jnp.bfloat16)
+    return jnp.concatenate([high, (rows - high.astype(F32)).astype(jnp.bfloat16)], axis=0)
+
+
+def vertex_force(offset, rest, scale, incidence):
     strain = offset - rest
-    high = strain.astype(jnp.bfloat16)
-    low = (strain - high.astype(F32)).astype(jnp.bfloat16)
-    both = jnp.concatenate([high, low], axis=0)
-    first = jnp.dot(both, links_high, preferred_element_type=F32)
-    second = jnp.dot(both, links_low, preferred_element_type=F32)
-    total = first + second
-    return scale * (total[:8] + total[8:])
-
-
-def spread(offset, rest, scale, base, links_high, links_low, terms, main_ref, rim_ref):
-    force = vertex_force(offset, rest, scale, links_high, links_low)
+    summed = jnp.dot(halves(strain), incidence[...], preferred_element_type=F32)
+    summed = summed[:8] + summed[8:]
+    rows = lax.broadcasted_iota(jnp.int32, summed.shape, 0)
+    summed = jnp.where(rows == 6, 1.0, summed)
+    pulled = lax.dot_general(
+        halves(summed), incidence[...], (((1,), (1,)), ((), ())), preferred_element_type=F32
+    )
+    pulled = pulled[:8] + pulled[8:]
+    return scale * (pulled - 3.0 * pulled[6:7] * strain)
+
+
+def spread(offset, rest, scale, base, incidence, terms, main_ref, rim_ref):
+    force = vertex_force(offset, rest, scale, incidence)
     kernels = stencil_kernels(offset)
     grid = None
     for slot in range(SLOTS):
@@ -123,8 +145,8 @@
     rim_ref[...] = grid[MAIN_ROWS:].reshape(3, 3, 8, CZ)
 
 
-def spread_messages(parity, main_ref, rim_ref, first_ref, second_ref):
-    even = parity == 0
+def spread_messages(info_ref, main_ref, rim_ref, first_ref, second_ref):
+    even = info_ref[0] == 0.0
     zero = jnp.zeros((2, CZ), F32)
     for a in range(3):
         up_rows, down_rows = [], []
@@ -139,38 +161,33 @@
             second_ref[a, t] = choose(even, downs[t], ups[t])
 
 
-def links_kernel(triangles_ref, high_ref, low_ref, incidence):
-    vertex = lax.broadcasted_iota(jnp.int32, incidence.shape, 0)
-    hit = jnp.zeros(incidence.shape, F32)
-    for corner in range(3):
-        hit = jnp.where(triangles_ref[corner : corner + 1, :] == vertex, 1.0, hit)
-    incidence[...] = hit.astype(jnp.bfloat16)
-    shared = lax.dot_general(
-        incidence[...], incidence[...], (((1,), (1,)), ((), ())), preferred_element_type=F32
+def incidence_kernel(triangles_ref, incidence_ref):
+    vertex = lax.broadcasted_iota(jnp.int32, incidence_ref.shape, 0)
+    corners = [triangles_ref[corner : corner + 1, :] == vertex for corner in range(3)]
+    hit = corners[0] | corners[1] | corners[2]
+    incidence_ref[...] = jnp.where(hit, 1.0, 0.0).astype(jnp.bfloat16)
+
+
+def spread_kernel(
+    info_ref, offset_in, rest_in, base_in, populations_in, solid_in, incidence_ref,
+    main_ref, rim_ref, first_ref, second_ref,
+    offset_ref, rest_ref, base_ref, populations_ref, solid_ref, terms,
+):
+    offset_ref[...] = six_rows(offset_in)
+    rest_ref[...] = six_rows(rest_in)
+    base_ref[...] = own_base(info_ref, base_in)
+    populations_ref[...] = populations_in[...]
+    solid_ref[...] = solid_in[...]
+    spread(
+        offset_ref[...], rest_ref[...], wide(info_ref[4]), base_ref[...],
+        incidence_ref, terms, main_ref, rim_ref,
     )
-    same = lax.broadcasted_iota(jnp.int32, shared.shape, 0) == lax.broadcasted_iota(
-        jnp.int32, shared.shape, 1
-    )
-    shared = jnp.where(same, -2.0 * shared, shared)
-    high = shared.astype(jnp.bfloat16)
-    high_ref[...] = high
-    low_ref[...] = (shared - high.astype(F32)).astype(jnp.bfloat16)
-
-
-def spread_kernel(
-    place_ref, offset_ref, rest_ref, scale_ref, base_ref, high_ref, low_ref,
-    main_ref, rim_ref, first_ref, second_ref, terms,
-):
-    spread(
-        offset_ref[...], rest_ref[...], scale_ref[...], base_ref[...],
-        high_ref[...], low_ref[...], terms, main_ref, rim_ref,
-    )
-    spread_messages(place_ref[0], main_ref, rim_ref, first_ref, second_ref)
-
-
-def force_corner_kernel(place_ref, rim_ref, first_in, second_in, first_ref, second_ref):
-    even_x = place_ref[0] == 0
-    even_y = place_ref[1] == 0
+    spread_messages(info_ref, main_ref, rim_ref, first_ref, second_ref)
+
+
+def force_corner_kernel(info_ref, rim_ref, first_in, second_in, first_ref, second_ref):
+    even_x = info_ref[0] == 0.0
+    even_y = info_ref[1] == 0.0
     rows = tile_rows()
     for a in range(3):
         above = choose(even_x, first_in[a, 2], second_in[a, 2])
@@ -225,11 +242,11 @@
 
 
 def collide_kernel(
-    place_ref, populations_ref, solid_ref, main_ref, first_x, second_x, first_y, second_y,
+    info_ref, populations_ref, solid_ref, main_ref, first_x, second_x, first_y, second_y,
     stepped_ref, force_ref, first_ref, second_ref,
 ):
-    even_x = place_ref[0] == 0
-    even_y = place_ref[1] == 0
+    even_x = info_ref[0] == 0.0
+    even_y = info_ref[1] == 0.0
     rows = tile_rows()
     for x in range(4):
         force = []
@@ -313,11 +330,11 @@
 
 
 def flow_corner_kernel(
-    place_ref, stepped_in, force_ref, first_x, second_x,
+    info_ref, stepped_in, force_ref, first_x, second_x,
     stepped_ref, inside_ref, leaving_ref, first_ref, second_ref, edges, up_tiles, down_tiles,
 ):
-    even_x = place_ref[0] == 0
-    even_y = place_ref[1] == 0
+    even_x = info_ref[0] == 0.0
+    even_y = info_ref[1] == 0.0
     rows = tile_rows()
     below = [choose(even_x, second_x[t], first_x[t]) for t in range(10)]
     above = [choose(even_x, first_x[t], second_x[t]) for t in range(15)]
@@ -359,47 +376,50 @@
         leaving_ref[3 + k] = down
         up_tiles[k] = up
         down_tiles[k] = down
-    for t in range(3, 5):
-        up_tiles[t] = jnp.zeros(TILE, F32)
-        down_tiles[t] = jnp.zeros(TILE, F32)
-    for t in range(5):
-        up_tiles[t, 0:4, :] = stepped_ref[pl.ds(UP_Y[t] * 32, 4, stride=8), :]
-        down_tiles[t, 0:4, :] = stepped_ref[pl.ds(DOWN_Y[t] * 32 + 7, 4, stride=8), :]
+    for n in range(5):
+        t, r = (n, 0) if n < 4 else (3, 4)
+        up_tiles[t, r : r + 4, :] = stepped_ref[pl.ds(UP_Y[n] * 32, 4, stride=8), :]
+        down_tiles[t, r : r + 4, :] = stepped_ref[pl.ds(DOWN_Y[n] * 32 + 7, 4, stride=8), :]
     for k in range(4):
-        up_tiles[5 + k] = inside_ref[pl.ds(k * 64 + 7, 8, stride=8), :]
-        down_tiles[5 + k] = inside_ref[pl.ds(k * 64, 8, stride=8), :]
-        down_tiles[9 + k] = inside_ref[pl.ds(k * 64 + 1, 8, stride=8), :]
-    for t in range(13):
-        u = up_tiles[t] if t < 9 else down_tiles[t]
+        up_tiles[4 + k] = inside_ref[pl.ds(k * 64 + 7, 8, stride=8), :]
+        down_tiles[4 + k] = inside_ref[pl.ds(k * 64, 8, stride=8), :]
+    inverse = 1.0 / inside_ref[pl.ds(1, 8, stride=8), :]
+    for k in range(3):
+        down_tiles[8 + k] = inside_ref[pl.ds((k + 1) * 64 + 1, 8, stride=8), :] * inverse
+    for t in range(11):
+        u = up_tiles[t] if t < 8 else down_tiles[t]
         d = down_tiles[t]
         first_ref[t] = choose(even_y, u, d)
         second_ref[t] = choose(even_y, d, u)
 
 
-def finish_fluid(place_ref, stepped_ref, inside_ref, leaving_ref, first_y, second_y, out_ref, flow):
-    even_y = place_ref[1] == 0
+def crossing(tiles, n, x):
+    return row_of(tiles[n], x) if n < 4 else row_of(tiles[3], 4 + x)
+
+
+def finish_fluid(info_ref, stepped_ref, inside_ref, leaving_ref, first_y, second_y, out_ref, flow):
+    even_y = info_ref[1] == 0.0
     rows = tile_rows()
-    below = [choose(even_y, second_y[t], first_y[t]) for t in range(9)]
-    above = [choose(even_y, first_y[t], second_y[t]) for t in range(13)]
+    below = [choose(even_y, second_y[t], first_y[t]) for t in range(8)]
+    above = [choose(even_y, first_y[t], second_y[t]) for t in range(11)]
     for q in range(19):
         for x in range(4):
             s = stepped_ref[(q * 4 + x) * 8 : (q * 4 + x + 1) * 8, :]
             if q in UP_Y:
-                s = jnp.where(rows == 0, row_of(below[UP_Y.index(q)], x), s)
+                s = jnp.where(rows == 0, crossing(below, UP_Y.index(q), x), s)
             if q in DOWN_Y:
-                s = jnp.where(rows == 7, row_of(above[DOWN_Y.index(q)], x), s)
+                s = jnp.where(rows == 7, crossing(above, DOWN_Y.index(q), x), s)
             out_ref[q, x] = s
-    if flow is None:
-        return
 
     def arriving(tiles, members):
+        crossed = list(tiles[:4]) + [pltpu.roll(tiles[3], 4, 0)]
         out = []
         for k, what in enumerate((None, 0, 2)):
             total = None
             for n, q in enumerate(members):
                 weight = 1 if what is None else VELOCITIES[q][what]
                 if weight:
-                    term = tiles[n] if weight == 1 else -tiles[n]
+                    term = crossed[n] if weight == 1 else -crossed[n]
                     total = term if total is None else total + term
             out.append(jnp.where(rows < 4, total, tiles[k]))
         return [out[0], out[1], None, out[2]]
@@ -424,15 +444,17 @@
     up = [leaving_ref[0], leaving_ref[1], leaving_ref[0], leaving_ref[2]]
     down = [leaving_ref[3], leaving_ref[4], -leaving_ref[3], leaving_ref[5]]
     rims = (
-        [above[5 + k] + up[k] for k in range(4)],
-        [above[9 + k] for k in range(4)],
-        [below[5 + k] + down[k] for k in range(4)],
+        (0, [above[4 + k] + up[k] for k in range(4)]),
+        (2, [below[4 + k] + down[k] for k in range(4)]),
     )
-    for n, total in enumerate(rims):
+    for n, total in rims:
         inverse = 1.0 / jnp.where(rows == 7, 1.0, total[0])
         for a in range(3):
             start = MAIN_ROWS + (a * 3 + n) * 8
             flow[start : start + 8, :] = jnp.where(rows == 7, 0.0, total[1 + a] * inverse)
+    for a in range(3):
+        start = MAIN_ROWS + (a * 3 + 1) * 8
+        flow[start : start + 8, :] = above[8 + a]
 
 
 def sample(offset, live, base, flow):
@@ -461,39 +483,36 @@
 
 
 def next_kernel(
-    place_ref, stepped_ref, inside_ref, leaving_ref, first_y, second_y,
-    offset_ref, rest_ref, scale_ref, live_ref, base_ref, high_ref, low_ref,
+    info_ref, stepped_ref, inside_ref, leaving_ref, first_y, second_y,
+    offset_ref, rest_ref, base_ref, incidence_ref,
     out_ref, offset_out, main_ref, rim_ref, first_ref, second_ref, flow, terms,
 ):
-    finish_fluid(place_ref, stepped_ref, inside_ref, leaving_ref, first_y, second_y, out_ref, flow)
-    offset = sample(offset_ref[...], live_ref[...], base_ref[...], flow)
+    finish_fluid(info_ref, stepped_ref, inside_ref, leaving_ref, first_y, second_y, out_ref, flow)
+    base = base_ref[...]
+    offset = sample(offset_ref[...], wide(info_ref[5]), base, flow)
     offset_out[...] = offset
-    spread(
-        offset, rest_ref[...], scale_ref[...], base_ref[...],
-        high_ref[...], low_ref[...], terms, main_ref, rim_ref,
-    )
-    spread_messages(place_ref[0], main_ref, rim_ref, first_ref, second_ref)
+    spread(offset, rest_ref[...], wide(info_ref[4]), base, incidence_ref, terms, main_ref, rim_ref)
+    spread_messages(info_ref, main_ref, rim_ref, first_ref, second_ref)
 
 
 def last_kernel(
-    place_ref, stepped_ref, inside_ref, leaving_ref, first_y, second_y,
-    offset_ref, live_ref, base_ref,
+    info_ref, stepped_ref, inside_ref, leaving_ref, first_y, second_y, offset_ref, base_ref,
     out_ref, offset_out, flow,
 ):
-    finish_fluid(place_ref, stepped_ref, inside_ref, leaving_ref, first_y, second_y, out_ref, flow)
-    offset_out[...] = sample(offset_ref[...], live_ref[...], base_ref[...], flow)
+    finish_fluid(info_ref, stepped_ref, inside_ref, leaving_ref, first_y, second_y, out_ref, flow)
+    offset = sample(offset_ref[...], wide(info_ref[5]), base_ref[...], flow)
+    for a in range(3):
+        offset_out[a] = offset[2 * a : 2 * a + 2]
 
 
 INTERPRET = False
 
 
 def call(kernel, outs, scratch, *operands, name):
-    in_specs = [pl.BlockSpec(memory_space=pltpu.SMEM)] if kernel is not links_kernel else []
-    in_specs += [pl.BlockSpec(memory_space=pltpu.VMEM)] * (len(operands) - len(in_specs))
     return pl.pallas_call(
         kernel,
         out_shape=[jax.ShapeDtypeStruct(shape, dtype) for shape, dtype in outs],
-        in_specs=in_specs,
+        in_specs=[pl.BlockSpec(memory_space=pltpu.VMEM)] * len(operands),
         out_specs=[pl.BlockSpec(memory_space=pltpu.VMEM)] * len(outs),
         scratch_shapes=[pltpu.VMEM(shape, dtype) for shape, dtype in scratch],
         compiler_params=pltpu.CompilerParams(vmem_limit_bytes=24 * 1024 * 1024),
@@ -508,10 +527,10 @@
 
 def exchange(first, second, axis):
     size = lax.axis_size(axis)
-    out = []
-    for kind, message in ((0, first), (1, second)):
+    out = [None, None]
+    for kind, message in ((1, second), (0, first)):
         pairs = [(i, partner(i, kind, size)) for i in range(size)]
-        out.append(lax.ppermute(message, axis, pairs))
+        out[kind] = lax.ppermute(message, axis, pairs)
     return out
 
 
@@ -527,33 +546,35 @@
 def local(populations, solid, base_cell, offset, rest_displacement, stiffness, occupied, triangles):
     place_x = lax.axis_index("gx")
     place_y = lax.axis_index("gy")
-    place = jnp.stack([place_x % 2, place_y % 2]).astype(jnp.int32)
-
-    def pad(rows):
-        return jnp.pad(rows.reshape(6, PAD), ((0, 2), (0, 0)))
-
-    start = jnp.stack([place_x * CX, place_y * CY, place_x * 0]).astype(jnp.int32)
-    base = pad(base_cell.reshape(3, SLOTS, PAD) - start[:, None, None])
-    where = pad(offset)
-    rest = pad(rest_displacement)
-    held = occupied.reshape(1, SLOTS, 1).astype(F32)
-    spring = stiffness.reshape(1, SLOTS, 1) * held
-    scale = pad(jnp.broadcast_to(spring, (3, SLOTS, PAD)))
-    live = pad(jnp.broadcast_to(held, (3, SLOTS, PAD)))
-    corners = triangles.T
-    links = [((PAD, PAD), jnp.bfloat16)] * 2
-    high, low = call(
-        links_kernel, links, [((PAD, triangles.shape[0]), jnp.bfloat16)], corners, name="links"
-    )
+    held = occupied.reshape(SLOTS).astype(F32)
+    spring = stiffness.reshape(SLOTS) * held
+    lead = lax.broadcasted_iota(jnp.int32, (6, 8, CZ), 0)
+    even_row = lax.broadcasted_iota(jnp.int32, (6, 8, CZ), 1) % 2 == 0
+    info = jnp.where(even_row, held[0], held[1])
+    info = jnp.where(lead == 4, jnp.where(even_row, spring[0], spring[1]), info)
+    numbers = (place_x % 2, place_y % 2, place_x * CX, place_y * CY)
+    for n, number in enumerate(numbers):
+        info = jnp.where(lead == n, number.astype(F32), info)
+    stored = (3, SLOTS, PAD)
+    rows = (8, PAD)
     terms = ((TABLE_ROWS, PAD), F32)
     flow = ((TABLE_ROWS, CZ), F32)
-    main, rim, first, second = call(
-        spread_kernel, SPREAD_OUT, [terms], place, where, rest, scale, base, high, low, name="spread"
+    corners = triangles.T
+    (incidence,) = call(
+        incidence_kernel, [((PAD, corners.shape[1]), jnp.bfloat16)], [], corners, name="incidence"
+    )
+    main, rim, first, second, where, rest, base, populations, solid = call(
+        spread_kernel,
+        SPREAD_OUT
+        + [(rows, F32), (rows, F32), (rows, jnp.int32), STEPPED, (solid.shape, jnp.int32)],
+        [terms],
+        info, offset.reshape(stored), rest_displacement.reshape(stored), base_cell.reshape(stored),
+        populations, solid, incidence, name="spread",
     )
     for substep in range(SUBSTEPS):
         first_x, second_x = exchange(first, second, "gx")
         corner = call(
-            force_corner_kernel, [((3, 8, CZ), F32)] * 2, [], place, rim, first_x, second_x,
+            force_corner_kernel, [((3, 8, CZ), F32)] * 2, [], info, rim, first_x, second_x,
             name="force_corner",
         )
         first_y, second_y = exchange(*corner, "gy")
@@ -561,7 +582,7 @@
             collide_kernel,
             [STEPPED, ((3, 4, 8, CZ), F32), ((15, 8, CZ), F32), ((15, 8, CZ), F32)],
             [],
-            place, populations, solid, main, first_x, second_x, first_y, second_y,
+            info, populations, solid, main, first_x, second_x, first_y, second_y,
             name="collide",
         )
         first_x, second_x = exchange(first, second, "gx")
@@ -569,25 +590,24 @@
             flow_corner_kernel,
             [
                 ((19 * 4 * 8, CZ), F32), ((4 * 8 * 8, CZ), F32), ((6, 8, CZ), F32),
-                ((13, 8, CZ), F32), ((13, 8, CZ), F32),
+                ((11, 8, CZ), F32), ((11, 8, CZ), F32),
             ],
-            [((3 * 8 * 8, CZ), F32), ((5, 8, CZ), F32), ((13, 8, CZ), F32)][:1]
-            + [((9, 8, CZ), F32), ((13, 8, CZ), F32)],
-            place, stepped, force, first_x, second_x,
+            [((3 * 8 * 8, CZ), F32), ((8, 8, CZ), F32), ((11, 8, CZ), F32)],
+            info, stepped, force, first_x, second_x,
             name="flow_corner",
         )
         first_y, second_y = exchange(first, second, "gy")
-        fluid = (place, stepped, inside, leaving, first_y, second_y)
+        fluid = (info, stepped, inside, leaving, first_y, second_y)
         if substep < SUBSTEPS - 1:
             populations, where, main, rim, first, second = call(
-                next_kernel, [STEPPED, ((8, PAD), F32)] + SPREAD_OUT, [flow, terms],
-                *fluid, where, rest, scale, live, base, high, low, name="next",
+                next_kernel, [STEPPED, (rows, F32)] + SPREAD_OUT, [flow, terms],
+                *fluid, where, rest, base, incidence, name="next",
             )
         else:
             populations, where = call(
-                last_kernel, [STEPPED, ((8, PAD), F32)], [flow], *fluid, where, live, base, name="last"
+                last_kernel, [STEPPED, (stored, F32)], [flow], *fluid, where, base, name="last"
             )
-    return populations, where[:6].reshape(offset.shape)
+    return populations, where.reshape(offset.shape)
 
 
 def solution(mesh):

time: 134 us -> 128 us (0.955)
  Pallas kernels: 19.8 us -> 13.1 us
  other arithmetic: 0.9 us -> 3.93 us
  local copies, waits for them, and re-layouts: 4.08 us -> 1.9 us
    pallas_call x14, Pallas kernels: 19.8 us -> 13.1 us  [call(): pl.pallas_call(kernel, out_shape=[jax.ShapeDtypeStruct(shape, dtype) for...]
    reshape x4 -> x0, local copies, waits for them, and re-layouts: 2.83 us -> none  [the longest x2 1.47 us: pad(): return jnp.pad(rows.reshape(6, PAD), ((0, 2), (0, 0)))]
    select_n x0 -> x1, other arithmetic: none -> 2.57 us  [local(): info = jnp.where(lead == n, number.astype(F32), info)]
  transfers between devices with their start and end apart: 24 -> 24, of which waited for: 17 -> 16; matrix products, arithmetic and copies ran while one was open for 0% -> 0% of each run, Pallas kernels for 0% -> 0%
where the time goes in v1:
time: 128 us
  starting transfers between devices  54.9 us (43%)
  waiting for transfers between devices  53.4 us (42%)
  Pallas kernels  13.1 us (10%)
  other arithmetic  3.93 us (3%)
  local copies, waits for them, and re-layouts  1.9 us (1%)
    ppermute x24, starting transfers between devices, exchange(): out[kind] = lax.ppermute(message, axis, pairs)  54.9 us
    ppermute x24, waiting for transfers between devices, exchange(): out[kind] = lax.ppermute(message, axis, pairs)  53.4 us
    pallas_call x14, Pallas kernels, call(): pl.pallas_call(kernel, out_shape=[jax.ShapeDtypeStruct(shape, dtype) for...  13.1 us
    select_n x1, other arithmetic, local(): info = jnp.where(lead == n, number.astype(F32), info)  2.57 us
  transfers between devices with their start and end apart: 24, of which 16 were waited for; matrix products, arithmetic and copies ran while one was open for 0% of the time, Pallas kernels for 0%

profile of v1, /device:TPU:1, one launch (start us, length us, event | category | flops | bytes accessed | tf_op | source)
XLA Modules:
  0.0 128.1 jit_solution(1427344814947451240)
XLA Ops:
  0.7 0.7 convert_element_type.20
  1.4 0.7 convert_multiply_fusion
  2.1 0.6 fusion.1
  2.7 0.6 fusion
  3.2 0.7 copy-done.1
  4.0 1.0 incidence.1.incidence_ref
  5.0 2.6 %select_select_fusion.info_ref = f32[6,8,128]{2,1,0:T(8,128)S(1)} fusion(f32[]{:T(128)} %bitcast.3, f32[]{:T(128)} %bitcast.2, f32[]{:T(128)} %bitcast.1, f32[]{:T(128)} %bitcast, s32[8]{0:T(128)S(1)} %get-tuple-element.120, s32[8]{0:T(128)S(1)} %get-tuple-element.121, f32[]{:T(128)S(6)} %convert_element_type.19, f32[]{:T(128)S(6)} %convert_element_type.18, ...), kind=kLoop, calls=%fused_computation | loop fusion | flops 55296 | bytes 24710 | tf_op jit(solution)/shard_map/jit(_where)/select_n | solution.py:557
  7.6 2.3 %spread.1 = (f32[3,7,8,128]{3,2,1,0:T(8,128)S(1)}, f32[3,3,8,128]{3,2,1,0:T(8,128)S(1)}, f32[3,3,8,128]{3,2,1,0:T(8,128)S(1)}, f32[3,3,8,128]{3,2,1,0:T(8,128)S(...) custom-call(f32[6,8,128]{2,1,0:T(8,128)S(1)} %select_select_fusion.i, ...), custom_call_target="tpu_custom_call" | custom-call | tf_op jit(solution)/shard_map/spread/pallas_call | solution.py:512
  9.9 3.3 %collective-permute-start = (f32[3,3,8,128]{3,2,1,0:T(8,128)S(1)}, f32[3,3,8,128]{3,2,1,0:T(8,128)S(1)}, u32[]{:S(2)}, u32[]{:S(2)}) collective-permute-start(f32[3,3,8,128]{3,2,1,0:T(8,128)S(1)} %get-tuple-element.61), channel_id=1, source_target_pairs={{0,16},{16,0},{32,48},{48,32},{64,80},{80,64},{96,112},{112,96},{1... | collective-permute-start | bytes 110600 | tf_op jit(solution)/shard_map/ppermute | solution.py:533
  13.2 5.2 %collective-permute-start.1 = (f32[3,3,8,128]{3,2,1,0:T(8,128)S(1)}, f32[3,3,8,128]{3,2,1,0:T(8,128)S(1)}, u32[]{:S(2)}, u32[]{:S(2)}) collective-permute-start(f32[3,3,8,128]{3,2,1,0:T(8,128)S(1)} %get-tuple-element.62), channel_id=1, source_target_pairs={{0,240},{16,32},{32,16},{48,64},{64,48},{80,96},{96,80},{112,128},... | collective-permute-start | bytes 110600 | tf_op jit(solution)/shard_map/ppermute | solution.py:533
  18.4 0.0 collective-permute-done.first_in.first_x
  18.4 2.1 %collective-permute-done.1.second_in.second_x = f32[3,3,8,128]{3,2,1,0:T(8,128)S(1)} collective-permute-done((f32[3,3,8,128]{3,2,1,0:T(8,128)S(1)}, f32[3,3,8,128]{3,2,1,0:T(8,128)S(1)}, u32[]{:S(2)}, u32[]{:S(2)}) %collective-permute-start.1) | collective-permute-done | bytes 36896 | tf_op jit(solution)/shard_map/ppermute | solution.py:533
  20.5 0.7 collective-permute-start.2
  21.2 5.4 %collective-permute-start.3 = (f32[3,8,128]{2,1,0:T(8,128)S(1)}, f32[3,8,128]{2,1,0:T(8,128)S(1)}, u32[]{:S(2)}, u32[]{:S(2)}) collective-permute-start(f32[3,8,128]{2,1,0:T(8,128)S(1)} %get-tuple-element.65), channel_id=1, source_target_pairs={{0,15},{1,2},{2,1},{3,4},{4,3},{5,6},{6,5},{7,8},{8,7},{9,10},{10,... | collective-permute-start | bytes 36872 | tf_op jit(solution)/shard_map/ppermute | solution.py:533
  26.6 0.0 collective-permute-done.2.first_y
  26.6 1.2 collective-permute-done.3.second_y
  27.8 0.3 collide.3
  28.1 4.0 %collective-permute-start.4 = (f32[15,8,128]{2,1,0:T(8,128)S(1)}, f32[15,8,128]{2,1,0:T(8,128)S(1)}, u32[]{:S(2)}, u32[]{:S(2)}) collective-permute-start(f32[15,8,128]{2,1,0:T(8,128)S(1)} %get-tuple-element.68), channel_id=1, source_target_pairs={{0,16},{16,0},{32,48},{48,32},{64,80},{80,64},{96,112},{112,96},{1... | collective-permute-start | bytes 184328 | tf_op jit(solution)/shard_map/ppermute | solution.py:533
  32.1 2.9 %collective-permute-start.5 = (f32[15,8,128]{2,1,0:T(8,128)S(1)}, f32[15,8,128]{2,1,0:T(8,128)S(1)}, u32[]{:S(2)}, u32[]{:S(2)}) collective-permute-start(f32[15,8,128]{2,1,0:T(8,128)S(1)} %get-tuple-element.69), channel_id=1, source_target_pairs={{0,240},{16,32},{32,16},{48,64},{64,48},{80,96},{96,80},{112,128},... | collective-permute-start | bytes 184328 | tf_op jit(solution)/shard_map/ppermute | solution.py:533
  35.0 0.0 collective-permute-done.4.first_x
  35.0 4.7 %collective-permute-done.5.second_x = f32[15,8,128]{2,1,0:T(8,128)S(1)} collective-permute-done((f32[15,8,128]{2,1,0:T(8,128)S(1)}, f32[15,8,128]{2,1,0:T(8,128)S(1)}, u32[]{:S(2)}, u32[]{:S(2)}) %collective-permute-start.5) | collective-permute-done | bytes 61472 | tf_op jit(solution)/shard_map/ppermute | solution.py:533
  39.7 0.1 flow_corner.3
  39.8 0.1 collective-permute-start.6
  39.9 5.3 %collective-permute-start.7 = (f32[11,8,128]{2,1,0:T(8,128)S(1)}, f32[11,8,128]{2,1,0:T(8,128)S(1)}, u32[]{:S(2)}, u32[]{:S(2)}) collective-permute-start(f32[11,8,128]{2,1,0:T(8,128)S(1)} %get-tuple-element.74), channel_id=1, source_target_pairs={{0,15},{1,2},{2,1},{3,4},{4,3},{5,6},{6,5},{7,8},{8,7},{9,10},{10,... | collective-permute-start | bytes 135176 | tf_op jit(solution)/shard_map/ppermute | solution.py:533
  45.2 0.0 collective-permute-done.6.first_y
  45.2 1.9 %collective-permute-done.7.second_y = f32[11,8,128]{2,1,0:T(8,128)S(1)} collective-permute-done((f32[11,8,128]{2,1,0:T(8,128)S(1)}, f32[11,8,128]{2,1,0:T(8,128)S(1)}, u32[]{:S(2)}, u32[]{:S(2)}) %collective-permute-start.7) | collective-permute-done | bytes 45088 | tf_op jit(solution)/shard_map/ppermute | solution.py:533
  47.1 3.4 %next.2 = (f32[19,4,8,128]{3,2,1,0:T(8,128)S(1)}, f32[8,768]{1,0:T(8,128)S(1)}, f32[3,7,8,128]{3,2,1,0:T(8,128)S(1)}, f32[3,3,8,128]{3,2,1,0:T(8,128)S(1)}, f32[...) custom-call(f32[6,8,128]{2,1,0:T(8,128)S(1)} %select_select_fusion.info_ref, ...), custom_call_target="tpu_custom_call" | custom-call | tf_op jit(solution)/shard_map/next/pallas_call | solution.py:512
  50.5 4.0 %collective-permute-start.8 = (f32[3,3,8,128]{3,2,1,0:T(8,128)S(1)}, f32[3,3,8,128]{3,2,1,0:T(8,128)S(1)}, u32[]{:S(2)}, u32[]{:S(2)}) collective-permute-start(f32[3,3,8,128]{3,2,1,0:T(8,128)S(1)} %get-tuple-element.80), channel_id=1, source_target_pairs={{0,16},{16,0},{32,48},{48,32},{64,80},{80,64},{96,112},{112,96},{1... | collective-permute-start | bytes 110600 | tf_op jit(solution)/shard_map/ppermute | solution.py:533
  54.5 0.2 collective-permute-start.9
  54.6 0.7 collective-permute-done.8.first_in.first_x
  55.4 6.4 %collective-permute-done.9.second_in.second_x = f32[3,3,8,128]{3,2,1,0:T(8,128)S(1)} collective-permute-done((f32[3,3,8,128]{3,2,1,0:T(8,128)S(1)}, f32[3,3,8,128]{3,2,1,0:T(8,128)S(1)}, u32[]{:S(2)}, u32[]{:S(2)}) %collective-permute-start.9) | collective-permute-done | bytes 36896 | tf_op jit(solution)/shard_map/ppermute | solution.py:533
  61.8 0.3 collective-permute-start.10
  62.1 3.3 %collective-permute-start.11 = (f32[3,8,128]{2,1,0:T(8,128)S(1)}, f32[3,8,128]{2,1,0:T(8,128)S(1)}, u32[]{:S(2)}, u32[]{:S(2)}) collective-permute-start(f32[3,8,128]{2,1,0:T(8,128)S(1)} %get-tuple-element.84), channel_id=1, source_target_pairs={{0,15},{1,2},{2,1},{3,4},{4,3},{5,6},{6,5},{7,8},{8,7},{9,10},{10,... | collective-permute-start | bytes 36872 | tf_op jit(solution)/shard_map/ppermute | solution.py:533
  65.4 0.0 collective-permute-done.10.first_y
  65.4 3.3 %collective-permute-done.11.second_y = f32[3,8,128]{2,1,0:T(8,128)S(1)} collective-permute-done((f32[3,8,128]{2,1,0:T(8,128)S(1)}, f32[3,8,128]{2,1,0:T(8,128)S(1)}, u32[]{:S(2)}, u32[]{:S(2)}) %collective-permute-start.11) | collective-permute-done | bytes 12320 | tf_op jit(solution)/shard_map/ppermute | solution.py:533
  68.6 0.3 collide.4
  69.0 3.4 %collective-permute-start.12 = (f32[15,8,128]{2,1,0:T(8,128)S(1)}, f32[15,8,128]{2,1,0:T(8,128)S(1)}, u32[]{:S(2)}, u32[]{:S(2)}) collective-permute-start(f32[15,8,128]{2,1,0:T(8,128)S(1)} %get-tuple-element.87), channel_id=1, source_target_pairs={{0,16},{16,0},{32,48},{48,32},{64,80},{80,64},{96,112},{112,96},{1... | collective-permute-start | bytes 184328 | tf_op jit(solution)/shard_map/ppermute | solution.py:533
  72.4 0.0 collective-permute-start.13
  72.4 0.9 collective-permute-done.12.first_x
  73.3 6.7 %collective-permute-done.13.second_x = f32[15,8,128]{2,1,0:T(8,128)S(1)} collective-permute-done((f32[15,8,128]{2,1,0:T(8,128)S(1)}, f32[15,8,128]{2,1,0:T(8,128)S(1)}, u32[]{:S(2)}, u32[]{:S(2)}) %collective-permute-start.13) | collective-permute-done | bytes 61472 | tf_op jit(solution)/shard_map/ppermute | solution.py:533
  79.9 0.1 flow_corner.4
  80.0 0.1 collective-permute-start.14
  80.1 3.4 %collective-permute-start.15 = (f32[11,8,128]{2,1,0:T(8,128)S(1)}, f32[11,8,128]{2,1,0:T(8,128)S(1)}, u32[]{:S(2)}, u32[]{:S(2)}) collective-permute-start(f32[11,8,128]{2,1,0:T(8,128)S(1)} %get-tuple-element.93), channel_id=1, source_target_pairs={{0,15},{1,2},{2,1},{3,4},{4,3},{5,6},{6,5},{7,8},{8,7},{9,10},{10,... | collective-permute-start | bytes 135176 | tf_op jit(solution)/shard_map/ppermute | solution.py:533
  83.5 0.0 collective-permute-done.14.first_y
  83.5 3.7 %collective-permute-done.15.second_y = f32[11,8,128]{2,1,0:T(8,128)S(1)} collective-permute-done((f32[11,8,128]{2,1,0:T(8,128)S(1)}, f32[11,8,128]{2,1,0:T(8,128)S(1)}, u32[]{:S(2)}, u32[]{:S(2)}) %collective-permute-start.15) | collective-permute-done | bytes 45088 | tf_op jit(solution)/shard_map/ppermute | solution.py:533
  87.3 3.4 %next.3 = (f32[19,4,8,128]{3,2,1,0:T(8,128)S(1)}, f32[8,768]{1,0:T(8,128)S(1)}, f32[3,7,8,128]{3,2,1,0:T(8,128)S(1)}, f32[3,3,8,128]{3,2,1,0:T(8,128)S(1)}, f32[...) custom-call(f32[6,8,128]{2,1,0:T(8,128)S(1)} %select_select_fusion.info_ref, ...), custom_call_target="tpu_custom_call" | custom-call | tf_op jit(solution)/shard_map/next/pallas_call | solution.py:512
  90.7 3.2 %collective-permute-start.16 = (f32[3,3,8,128]{3,2,1,0:T(8,128)S(1)}, f32[3,3,8,128]{3,2,1,0:T(8,128)S(1)}, u32[]{:S(2)}, u32[]{:S(2)}) collective-permute-start(f32[3,3,8,128]{3,2,1,0:T(8,128)S(1)} %get-tuple-element.97), channel_id=1, source_target_pairs={{0,16},{16,0},{32,48},{48,32},{64,80},{80,64},{96,112},{112,96},{1... | collective-permute-start | bytes 110600 | tf_op jit(solution)/shard_map/ppermute | solution.py:533
  93.9 0.0 collective-permute-start.17
  93.9 0.9 collective-permute-done.16.first_in.first_x
  94.7 6.6 %collective-permute-done.17.second_in.second_x = f32[3,3,8,128]{3,2,1,0:T(8,128)S(1)} collective-permute-done((f32[3,3,8,128]{3,2,1,0:T(8,128)S(1)}, f32[3,3,8,128]{3,2,1,0:T(8,128)S(1)}, u32[]{:S(2)}, u32[]{:S(2)}) %collective-permute-start.17) | collective-permute-done | bytes 36896 | tf_op jit(solution)/shard_map/ppermute | solution.py:533
  101.3 0.1 collective-permute-start.18
  101.4 3.2 %collective-permute-start.19 = (f32[3,8,128]{2,1,0:T(8,128)S(1)}, f32[3,8,128]{2,1,0:T(8,128)S(1)}, u32[]{:S(2)}, u32[]{:S(2)}) collective-permute-start(f32[3,8,128]{2,1,0:T(8,128)S(1)} %get-tuple-element.101), channel_id=1, source_target_pairs={{0,15},{1,2},{2,1},{3,4},{4,3},{5,6},{6,5},{7,8},{8,7},{9,10},{10,... | collective-permute-start | bytes 36872 | tf_op jit(solution)/shard_map/ppermute | solution.py:533
  104.7 0.0 collective-permute-done.18.first_y
  104.7 3.3 %collective-permute-done.19.second_y = f32[3,8,128]{2,1,0:T(8,128)S(1)} collective-permute-done((f32[3,8,128]{2,1,0:T(8,128)S(1)}, f32[3,8,128]{2,1,0:T(8,128)S(1)}, u32[]{:S(2)}, u32[]{:S(2)}) %collective-permute-start.19) | collective-permute-done | bytes 12320 | tf_op jit(solution)/shard_map/ppermute | solution.py:533
  108.0 0.3 collide.5
  108.3 3.3 %collective-permute-start.20 = (f32[15,8,128]{2,1,0:T(8,128)S(1)}, f32[15,8,128]{2,1,0:T(8,128)S(1)}, u32[]{:S(2)}, u32[]{:S(2)}) collective-permute-start(f32[15,8,128]{2,1,0:T(8,128)S(1)} %get-tuple-element.104), channel_id=1, source_target_pairs={{0,16},{16,0},{32,48},{48,32},{64,80},{80,64},{96,112},{112,96},{1... | collective-permute-start | bytes 184328 | tf_op jit(solution)/shard_map/ppermute | solution.py:533
  111.6 0.0 collective-permute-start.21
  111.6 0.9 collective-permute-done.20.first_x
  112.5 6.7 %collective-permute-done.21.second_x = f32[15,8,128]{2,1,0:T(8,128)S(1)} collective-permute-done((f32[15,8,128]{2,1,0:T(8,128)S(1)}, f32[15,8,128]{2,1,0:T(8,128)S(1)}, u32[]{:S(2)}, u32[]{:S(2)}) %collective-permute-start.21) | collective-permute-done | bytes 61472 | tf_op jit(solution)/shard_map/ppermute | solution.py:533
  119.2 0.1 flow_corner.5
  119.3 0.1 collective-permute-start.22
  119.4 3.6 %collective-permute-start.23 = (f32[11,8,128]{2,1,0:T(8,128)S(1)}, f32[11,8,128]{2,1,0:T(8,128)S(1)}, u32[]{:S(2)}, u32[]{:S(2)}) collective-permute-start(f32[11,8,128]{2,1,0:T(8,128)S(1)} %get-tuple-element.110), channel_id=1, source_target_pairs={{0,15},{1,2},{2,1},{3,4},{4,3},{5,6},{6,5},{7,8},{8,7},{9,10},{10,... | collective-permute-start | bytes 135176 | tf_op jit(solution)/shard_map/ppermute | solution.py:533
  122.9 3.5 %collective-permute-done.23.second_y = f32[11,8,128]{2,1,0:T(8,128)S(1)} collective-permute-done((f32[11,8,128]{2,1,0:T(8,128)S(1)}, f32[11,8,128]{2,1,0:T(8,128)S(1)}, u32[]{:S(2)}, u32[]{:S(2)}) %collective-permute-start.23) | collective-permute-done | bytes 45088 | tf_op jit(solution)/shard_map/ppermute | solution.py:533
  126.4 1.7 %last.1 = (f32[19,4,8,128]{3,2,1,0:T(8,128)}, f32[3,2,768]{2,1,0:T(2,128)}) custom-call(f32[6,8,128]{2,1,0:T(8,128)S(1)} %select_select_fusion.info_ref, f32[608,128]{1,0:T(8,128)S(1)} %get-tuple-element.106.stepped_ref, f32[256,128]{1,0:T(8,128)S(1)} %get-tuple-element.107.inside_ref, f32[6,8,128]{2,1,0:T(8,128)S(1)} %get-tuple-element.108.leaving_ref, ...), custom_call_target="tpu_custom_call" | custom-call | tf_op jit(solution)/shard_map/last/pallas_call | solution.py:512
  (20 shorter events, 0.1 us)
Async XLA Ops:
  0.6 6.9 %copy-start = (f32[19,4,8,128]{3,2,1,0:T(8,128)S(1)}, f32[19,4,8,128]{3,2,1,0:T(8,128)}, u32[]{:S(2)}) copy-start(f32[19,4,8,128]{3,2,1,0:T(8,128)} %populations_in.1) | copy-start | bytes 933892
  3.2 0.7 copy-start.1
  4.0 3.6 %copy-start.2 = (f32[3,1,1,2,768]{4,3,2,1,0:T(2,128)S(1)}, f32[3,1,1,2,768]{4,3,2,1,0:T(2,128)}, u32[]{:S(2)}) copy-start(f32[3,1,1,2,768]{4,3,2,1,0:T(2,128)} %param.11) | copy-start | bytes 55300
  4.0 3.6 %copy-start.3 = (f32[3,1,1,2,768]{4,3,2,1,0:T(2,128)S(1)}, f32[3,1,1,2,768]{4,3,2,1,0:T(2,128)}, u32[]{:S(2)}) copy-start(f32[3,1,1,2,768]{4,3,2,1,0:T(2,128)} %param.12) | copy-start | bytes 55300
  4.0 3.6 %copy-start.4 = (s32[3,1,1,2,768]{4,3,2,1,0:T(2,128)S(1)}, s32[3,1,1,2,768]{4,3,2,1,0:T(2,128)}, u32[]{:S(2)}) copy-start(s32[3,1,1,2,768]{4,3,2,1,0:T(2,128)} %param.10) | copy-start | bytes 55300
  4.0 3.6 %copy-start.5 = (s32[4,8,128]{2,1,0:T(8,128)S(1)}, s32[4,8,128]{2,1,0:T(8,128)}, u32[]{:S(2)}) copy-start(s32[4,8,128]{2,1,0:T(8,128)} %solid_in.1) | copy-start | bytes 49156
  9.9 8.5 %collective-permute-start = (f32[3,3,8,128]{3,2,1,0:T(8,128)S(1)}, f32[3,3,8,128]{3,2,1,0:T(8,128)S(1)}, u32[]{:S(2)}, u32[]{:S(2)}) collective-permute-start(f32[3,3,8,128]{3,2,1,0:T(8,128)S(1)} %get-tuple-element.61), channel_id=1, source_target_pairs={{0,16},{16,0},{32,48},{48,32},{64,80},{80,64},{96,112},{112,96},{1... | collective-permute-start | bytes 110600 | tf_op jit(solution)/shard_map/ppermute | solution.py:533
  13.2 7.3 %collective-permute-start.1 = (f32[3,3,8,128]{3,2,1,0:T(8,128)S(1)}, f32[3,3,8,128]{3,2,1,0:T(8,128)S(1)}, u32[]{:S(2)}, u32[]{:S(2)}) collective-permute-start(f32[3,3,8,128]{3,2,1,0:T(8,128)S(1)} %get-tuple-element.62), channel_id=1, source_target_pairs={{0,240},{16,32},{32,16},{48,64},{64,48},{80,96},{96,80},{112,128},... | collective-permute-start | bytes 110600 | tf_op jit(solution)/shard_map/ppermute | solution.py:533
  20.5 6.1 %collective-permute-start.2 = (f32[3,8,128]{2,1,0:T(8,128)S(1)}, f32[3,8,128]{2,1,0:T(8,128)S(1)}, u32[]{:S(2)}, u32[]{:S(2)}) collective-permute-start(f32[3,8,128]{2,1,0:T(8,128)S(1)} %get-tuple-element.64), channel_id=1, source_target_pairs={{0,1},{1,0},{2,3},{3,2},{4,5},{5,4},{6,7},{7,6},{8,9},{9,8},{10,11... | collective-permute-start | bytes 36872 | tf_op jit(solution)/shard_map/ppermute | solution.py:533
  21.2 6.6 %collective-permute-start.3 = (f32[3,8,128]{2,1,0:T(8,128)S(1)}, f32[3,8,128]{2,1,0:T(8,128)S(1)}, u32[]{:S(2)}, u32[]{:S(2)}) collective-permute-start(f32[3,8,128]{2,1,0:T(8,128)S(1)} %get-tuple-element.65), channel_id=1, source_target_pairs={{0,15},{1,2},{2,1},{3,4},{4,3},{5,6},{6,5},{7,8},{8,7},{9,10},{10,... | collective-permute-start | bytes 36872 | tf_op jit(solution)/shard_map/ppermute | solution.py:533
  28.1 6.9 %collective-permute-start.4 = (f32[15,8,128]{2,1,0:T(8,128)S(1)}, f32[15,8,128]{2,1,0:T(8,128)S(1)}, u32[]{:S(2)}, u32[]{:S(2)}) collective-permute-start(f32[15,8,128]{2,1,0:T(8,128)S(1)} %get-tuple-element.68), channel_id=1, source_target_pairs={{0,16},{16,0},{32,48},{48,32},{64,80},{80,64},{96,112},{112,96},{1... | collective-permute-start | bytes 184328 | tf_op jit(solution)/shard_map/ppermute | solution.py:533
  32.1 7.6 %collective-permute-start.5 = (f32[15,8,128]{2,1,0:T(8,128)S(1)}, f32[15,8,128]{2,1,0:T(8,128)S(1)}, u32[]{:S(2)}, u32[]{:S(2)}) collective-permute-start(f32[15,8,128]{2,1,0:T(8,128)S(1)} %get-tuple-element.69), channel_id=1, source_target_pairs={{0,240},{16,32},{32,16},{48,64},{64,48},{80,96},{96,80},{112,128},... | collective-permute-start | bytes 184328 | tf_op jit(solution)/shard_map/ppermute | solution.py:533
  39.8 5.4 %collective-permute-start.6 = (f32[11,8,128]{2,1,0:T(8,128)S(1)}, f32[11,8,128]{2,1,0:T(8,128)S(1)}, u32[]{:S(2)}, u32[]{:S(2)}) collective-permute-start(f32[11,8,128]{2,1,0:T(8,128)S(1)} %get-tuple-element.73), channel_id=1, source_target_pairs={{0,1},{1,0},{2,3},{3,2},{4,5},{5,4},{6,7},{7,6},{8,9},{9,8},{10,11... | collective-permute-start | bytes 135176 | tf_op jit(solution)/shard_map/ppermute | solution.py:533
  39.9 7.2 %collective-permute-start.7 = (f32[11,8,128]{2,1,0:T(8,128)S(1)}, f32[11,8,128]{2,1,0:T(8,128)S(1)}, u32[]{:S(2)}, u32[]{:S(2)}) collective-permute-start(f32[11,8,128]{2,1,0:T(8,128)S(1)} %get-tuple-element.74), channel_id=1, source_target_pairs={{0,15},{1,2},{2,1},{3,4},{4,3},{5,6},{6,5},{7,8},{8,7},{9,10},{10,... | collective-permute-start | bytes 135176 | tf_op jit(solution)/shard_map/ppermute | solution.py:533
  50.5 4.9 %collective-permute-start.8 = (f32[3,3,8,128]{3,2,1,0:T(8,128)S(1)}, f32[3,3,8,128]{3,2,1,0:T(8,128)S(1)}, u32[]{:S(2)}, u32[]{:S(2)}) collective-permute-start(f32[3,3,8,128]{3,2,1,0:T(8,128)S(1)} %get-tuple-element.80), channel_id=1, source_target_pairs={{0,16},{16,0},{32,48},{48,32},{64,80},{80,64},{96,112},{112,96},{1... | collective-permute-start | bytes 110600 | tf_op jit(solution)/shard_map/ppermute | solution.py:533
  54.5 7.3 %collective-permute-start.9 = (f32[3,3,8,128]{3,2,1,0:T(8,128)S(1)}, f32[3,3,8,128]{3,2,1,0:T(8,128)S(1)}, u32[]{:S(2)}, u32[]{:S(2)}) collective-permute-start(f32[3,3,8,128]{3,2,1,0:T(8,128)S(1)} %get-tuple-element.81), channel_id=1, source_target_pairs={{0,240},{16,32},{32,16},{48,64},{64,48},{80,96},{96,80},{112,128},... | collective-permute-start | bytes 110600 | tf_op jit(solution)/shard_map/ppermute | solution.py:533
  61.8 3.6 %collective-permute-start.10 = (f32[3,8,128]{2,1,0:T(8,128)S(1)}, f32[3,8,128]{2,1,0:T(8,128)S(1)}, u32[]{:S(2)}, u32[]{:S(2)}) collective-permute-start(f32[3,8,128]{2,1,0:T(8,128)S(1)} %get-tuple-element.83), channel_id=1, source_target_pairs={{0,1},{1,0},{2,3},{3,2},{4,5},{5,4},{6,7},{7,6},{8,9},{9,8},{10,11... | collective-permute-start | bytes 36872 | tf_op jit(solution)/shard_map/ppermute | solution.py:533
  62.1 6.6 %collective-permute-start.11 = (f32[3,8,128]{2,1,0:T(8,128)S(1)}, f32[3,8,128]{2,1,0:T(8,128)S(1)}, u32[]{:S(2)}, u32[]{:S(2)}) collective-permute-start(f32[3,8,128]{2,1,0:T(8,128)S(1)} %get-tuple-element.84), channel_id=1, source_target_pairs={{0,15},{1,2},{2,1},{3,4},{4,3},{5,6},{6,5},{7,8},{8,7},{9,10},{10,... | collective-permute-start | bytes 36872 | tf_op jit(solution)/shard_map/ppermute | solution.py:533
  69.0 4.3 %collective-permute-start.12 = (f32[15,8,128]{2,1,0:T(8,128)S(1)}, f32[15,8,128]{2,1,0:T(8,128)S(1)}, u32[]{:S(2)}, u32[]{:S(2)}) collective-permute-start(f32[15,8,128]{2,1,0:T(8,128)S(1)} %get-tuple-element.87), channel_id=1, source_target_pairs={{0,16},{16,0},{32,48},{48,32},{64,80},{80,64},{96,112},{112,96},{1... | collective-permute-start | bytes 184328 | tf_op jit(solution)/shard_map/ppermute | solution.py:533
  72.4 7.6 %collective-permute-start.13 = (f32[15,8,128]{2,1,0:T(8,128)S(1)}, f32[15,8,128]{2,1,0:T(8,128)S(1)}, u32[]{:S(2)}, u32[]{:S(2)}) collective-permute-start(f32[15,8,128]{2,1,0:T(8,128)S(1)} %get-tuple-element.88), channel_id=1, source_target_pairs={{0,240},{16,32},{32,16},{48,64},{64,48},{80,96},{96,80},{112,128},... | collective-permute-start | bytes 184328 | tf_op jit(solution)/shard_map/ppermute | solution.py:533
  80.0 3.5 %collective-permute-start.14 = (f32[11,8,128]{2,1,0:T(8,128)S(1)}, f32[11,8,128]{2,1,0:T(8,128)S(1)}, u32[]{:S(2)}, u32[]{:S(2)}) collective-permute-start(f32[11,8,128]{2,1,0:T(8,128)S(1)} %get-tuple-element.92), channel_id=1, source_target_pairs={{0,1},{1,0},{2,3},{3,2},{4,5},{5,4},{6,7},{7,6},{8,9},{9,8},{10,11... | collective-permute-start | bytes 135176 | tf_op jit(solution)/shard_map/ppermute | solution.py:533
  80.1 7.2 %collective-permute-start.15 = (f32[11,8,128]{2,1,0:T(8,128)S(1)}, f32[11,8,128]{2,1,0:T(8,128)S(1)}, u32[]{:S(2)}, u32[]{:S(2)}) collective-permute-start(f32[11,8,128]{2,1,0:T(8,128)S(1)} %get-tuple-element.93), channel_id=1, source_target_pairs={{0,15},{1,2},{2,1},{3,4},{4,3},{5,6},{6,5},{7,8},{8,7},{9,10},{10,... | collective-permute-start | bytes 135176 | tf_op jit(solution)/shard_map/ppermute | solution.py:533
  90.7 4.0 %collective-permute-start.16 = (f32[3,3,8,128]{3,2,1,0:T(8,128)S(1)}, f32[3,3,8,128]{3,2,1,0:T(8,128)S(1)}, u32[]{:S(2)}, u32[]{:S(2)}) collective-permute-start(f32[3,3,8,128]{3,2,1,0:T(8,128)S(1)} %get-tuple-element.97), channel_id=1, source_target_pairs={{0,16},{16,0},{32,48},{48,32},{64,80},{80,64},{96,112},{112,96},{1... | collective-permute-start | bytes 110600 | tf_op jit(solution)/shard_map/ppermute | solution.py:533
  93.9 7.4 %collective-permute-start.17 = (f32[3,3,8,128]{3,2,1,0:T(8,128)S(1)}, f32[3,3,8,128]{3,2,1,0:T(8,128)S(1)}, u32[]{:S(2)}, u32[]{:S(2)}) collective-permute-start(f32[3,3,8,128]{3,2,1,0:T(8,128)S(1)} %get-tuple-element.98), channel_id=1, source_target_pairs={{0,240},{16,32},{32,16},{48,64},{64,48},{80,96},{96,80},{112,128},... | collective-permute-start | bytes 110600 | tf_op jit(solution)/shard_map/ppermute | solution.py:533
  101.3 3.3 %collective-permute-start.18 = (f32[3,8,128]{2,1,0:T(8,128)S(1)}, f32[3,8,128]{2,1,0:T(8,128)S(1)}, u32[]{:S(2)}, u32[]{:S(2)}) collective-permute-start(f32[3,8,128]{2,1,0:T(8,128)S(1)} %get-tuple-element.100), channel_id=1, source_target_pairs={{0,1},{1,0},{2,3},{3,2},{4,5},{5,4},{6,7},{7,6},{8,9},{9,8},{10,11... | collective-permute-start | bytes 36872 | tf_op jit(solution)/shard_map/ppermute | solution.py:533
  101.4 6.5 %collective-permute-start.19 = (f32[3,8,128]{2,1,0:T(8,128)S(1)}, f32[3,8,128]{2,1,0:T(8,128)S(1)}, u32[]{:S(2)}, u32[]{:S(2)}) collective-permute-start(f32[3,8,128]{2,1,0:T(8,128)S(1)} %get-tuple-element.101), channel_id=1, source_target_pairs={{0,15},{1,2},{2,1},{3,4},{4,3},{5,6},{6,5},{7,8},{8,7},{9,10},{10,... | collective-permute-start | bytes 36872 | tf_op jit(solution)/shard_map/ppermute | solution.py:533
  108.3 4.2 %collective-permute-start.20 = (f32[15,8,128]{2,1,0:T(8,128)S(1)}, f32[15,8,128]{2,1,0:T(8,128)S(1)}, u32[]{:S(2)}, u32[]{:S(2)}) collective-permute-start(f32[15,8,128]{2,1,0:T(8,128)S(1)} %get-tuple-element.104), channel_id=1, source_target_pairs={{0,16},{16,0},{32,48},{48,32},{64,80},{80,64},{96,112},{112,96},{1... | collective-permute-start | bytes 184328 | tf_op jit(solution)/shard_map/ppermute | solution.py:533
  111.6 7.6 %collective-permute-start.21 = (f32[15,8,128]{2,1,0:T(8,128)S(1)}, f32[15,8,128]{2,1,0:T(8,128)S(1)}, u32[]{:S(2)}, u32[]{:S(2)}) collective-permute-start(f32[15,8,128]{2,1,0:T(8,128)S(1)} %get-tuple-element.105), channel_id=1, source_target_pairs={{0,240},{16,32},{32,16},{48,64},{64,48},{80,96},{96,80},{112,128},... | collective-permute-start | bytes 184328 | tf_op jit(solution)/shard_map/ppermute | solution.py:533
  119.3 3.7 %collective-permute-start.22 = (f32[11,8,128]{2,1,0:T(8,128)S(1)}, f32[11,8,128]{2,1,0:T(8,128)S(1)}, u32[]{:S(2)}, u32[]{:S(2)}) collective-permute-start(f32[11,8,128]{2,1,0:T(8,128)S(1)} %get-tuple-element.109), channel_id=1, source_target_pairs={{0,1},{1,0},{2,3},{3,2},{4,5},{5,4},{6,7},{7,6},{8,9},{9,8},{10,11... | collective-permute-start | bytes 135176 | tf_op jit(solution)/shard_map/ppermute | solution.py:533
  119.4 7.0 %collective-permute-start.23 = (f32[11,8,128]{2,1,0:T(8,128)S(1)}, f32[11,8,128]{2,1,0:T(8,128)S(1)}, u32[]{:S(2)}, u32[]{:S(2)}) collective-permute-start(f32[11,8,128]{2,1,0:T(8,128)S(1)} %get-tuple-element.110), channel_id=1, source_target_pairs={{0,15},{1,2},{2,1},{3,4},{4,3},{5,6},{6,5},{7,8},{8,7},{9,10},{10,... | collective-permute-start | bytes 135176 | tf_op jit(solution)/shard_map/ppermute | solution.py:533

commit v2 on v1

--- a/solution.py
+++ b/solution.py
@@ -8,8 +8,8 @@
 from jax.experimental.pallas import tpu as pltpu
 from jax.sharding import PartitionSpec as P
 
+
 SUBSTEPS = 3
-AX = ("gx", "gy")
 
 VELOCITIES = [
     [0, 0, 0],
@@ -42,7 +42,6 @@
 UP_Y = [q for q in range(19) if VELOCITIES[q][1] == 1]
 DOWN_Y = [q for q in range(19) if VELOCITIES[q][1] == -1]
 X_ORDER = [0, 1, 2, 3, 4, 5, -1]
-Y_RIM = [8, 9, -1]
 MAIN_ROWS = 3 * 7 * 8
 RIM_ROWS = 3 * 3 * 8
 TABLE_ROWS = MAIN_ROWS + RIM_ROWS
@@ -508,7 +507,7 @@
 INTERPRET = False
 
 
-def call(kernel, outs, scratch, *operands, name):
+def call(kernel, outs, scratch, *operands):
     return pl.pallas_call(
         kernel,
         out_shape=[jax.ShapeDtypeStruct(shape, dtype) for shape, dtype in outs],
@@ -517,7 +516,6 @@
         scratch_shapes=[pltpu.VMEM(shape, dtype) for shape, dtype in scratch],
         compiler_params=pltpu.CompilerParams(vmem_limit_bytes=24 * 1024 * 1024),
         interpret=INTERPRET,
-        name=name,
     )(*operands)
 
 
@@ -543,7 +541,7 @@
 STEPPED = ((19, 4, 8, CZ), F32)
 
 
-def local(populations, solid, base_cell, offset, rest_displacement, stiffness, occupied, triangles):
+def steps(populations, solid, base_cell, offset, rest_displacement, stiffness, occupied, triangles):
     place_x = lax.axis_index("gx")
     place_y = lax.axis_index("gy")
     held = occupied.reshape(SLOTS).astype(F32)
@@ -560,22 +558,19 @@
     terms = ((TABLE_ROWS, PAD), F32)
     flow = ((TABLE_ROWS, CZ), F32)
     corners = triangles.T
-    (incidence,) = call(
-        incidence_kernel, [((PAD, corners.shape[1]), jnp.bfloat16)], [], corners, name="incidence"
-    )
+    (incidence,) = call(incidence_kernel, [((PAD, corners.shape[1]), jnp.bfloat16)], [], corners)
     main, rim, first, second, where, rest, base, populations, solid = call(
         spread_kernel,
         SPREAD_OUT
         + [(rows, F32), (rows, F32), (rows, jnp.int32), STEPPED, (solid.shape, jnp.int32)],
         [terms],
         info, offset.reshape(stored), rest_displacement.reshape(stored), base_cell.reshape(stored),
-        populations, solid, incidence, name="spread",
+        populations, solid, incidence,
     )
     for substep in range(SUBSTEPS):
         first_x, second_x = exchange(first, second, "gx")
         corner = call(
             force_corner_kernel, [((3, 8, CZ), F32)] * 2, [], info, rim, first_x, second_x,
-            name="force_corner",
         )
         first_y, second_y = exchange(*corner, "gy")
         stepped, force, first, second = call(
@@ -583,7 +578,6 @@
             [STEPPED, ((3, 4, 8, CZ), F32), ((15, 8, CZ), F32), ((15, 8, CZ), F32)],
             [],
             info, populations, solid, main, first_x, second_x, first_y, second_y,
-            name="collide",
         )
         first_x, second_x = exchange(first, second, "gx")
         stepped, inside, leaving, first, second = call(
@@ -594,18 +588,17 @@
             ],
             [((3 * 8 * 8, CZ), F32), ((8, 8, CZ), F32), ((11, 8, CZ), F32)],
             info, stepped, force, first_x, second_x,
-            name="flow_corner",
         )
         first_y, second_y = exchange(first, second, "gy")
         fluid = (info, stepped, inside, leaving, first_y, second_y)
         if substep < SUBSTEPS - 1:
             populations, where, main, rim, first, second = call(
                 next_kernel, [STEPPED, (rows, F32)] + SPREAD_OUT, [flow, terms],
-                *fluid, where, rest, base, incidence, name="next",
+                *fluid, where, rest, base, incidence,
             )
         else:
             populations, where = call(
-                last_kernel, [STEPPED, (stored, F32)], [flow], *fluid, where, base, name="last"
+                last_kernel, [STEPPED, (stored, F32)], [flow], *fluid, where, base
             )
     return populations, where.reshape(offset.shape)
 
@@ -622,4 +615,4 @@
         P(),
     )
     out_specs = (P(None, "gx", "gy", None), P(None, "gx", "gy", None, None))
-    return jax.shard_map(local, mesh=mesh, in_specs=in_specs, out_specs=out_specs, check_vma=False)
+    return jax.shard_map(steps, mesh=mesh, in_specs=in_specs, out_specs=out_specs, check_vma=False)

time: 128 us -> 128 us (level)
  no operation moved by 1% of the time
where the time goes in v2:
time: 128 us
  starting transfers between devices  54.9 us (43%)
  waiting for transfers between devices  53.4 us (42%)
  Pallas kernels  13.1 us (10%)
  other arithmetic  3.93 us (3%)
  local copies, waits for them, and re-layouts  1.9 us (1%)
    ppermute x24, starting transfers between devices, exchange(): out[kind] = lax.ppermute(message, axis, pairs)  54.9 us
    ppermute x24, waiting for transfers between devices, exchange(): out[kind] = lax.ppermute(message, axis, pairs)  53.4 us
    pallas_call x14, Pallas kernels, call(): pl.pallas_call(kernel, out_shape=[jax.ShapeDtypeStruct(shape, dtype) for...  13.1 us
    select_n x1, other arithmetic, steps(): info = jnp.where(lead == n, number.astype(F32), info)  2.57 us
  transfers between devices with their start and end apart: 24, of which 16 were waited for; matrix products, arithmetic and copies ran while one was open for 0% of the time, Pallas kernels for 0%

profile of v2, /device:TPU:1, one launch (start us, length us, event | category | flops | bytes accessed | tf_op | source)
XLA Modules:
  0.0 128.1 jit_solution(1427344814947451240)
XLA Ops:
  0.7 0.7 convert_element_type.20
  1.4 0.7 convert_multiply_fusion
  2.1 0.6 fusion.1
  2.7 0.6 fusion
  3.2 0.7 copy-done.1
  4.0 1.0 shard_map.95.incidence_ref
  5.0 2.6 %select_select_fusion.info_ref = f32[6,8,128]{2,1,0:T(8,128)S(1)} fusion(f32[]{:T(128)} %bitcast.3, f32[]{:T(128)} %bitcast.2, f32[]{:T(128)} %bitcast.1, f32[]{:T(128)} %bitcast, s32[8]{0:T(128)S(1)} %get-tuple-element.120, s32[8]{0:T(128)S(1)} %get-tuple-element.121, f32[]{:T(128)S(6)} %convert_element_type.19, f32[]{:T(128)S(6)} %convert_element_type.18, ...), kind=kLoop, calls=%fused_computation | loop fusion | flops 55296 | bytes 24710 | tf_op jit(solution)/shard_map/jit(_where)/select_n | solution.py:555
  7.6 2.3 %shard_map.96 = (f32[3,7,8,128]{3,2,1,0:T(8,128)S(1)}, f32[3,3,8,128]{3,2,1,0:T(8,128)S(1)}, f32[3,3,8,128]{3,2,1,0:T(8,128)S(1)}, f32[3,3,8,128]{3,2,1,0:T(8,12...) custom-call(f32[6,8,128]{2,1,0:T(8,128)S(1)} %select_select_fusion.i, ...), custom_call_target="tpu_custom_call" | custom-call | tf_op jit(solution)/shard_map/pallas_call | solution.py:511
  9.9 3.3 %collective-permute-start = (f32[3,3,8,128]{3,2,1,0:T(8,128)S(1)}, f32[3,3,8,128]{3,2,1,0:T(8,128)S(1)}, u32[]{:S(2)}, u32[]{:S(2)}) collective-permute-start(f32[3,3,8,128]{3,2,1,0:T(8,128)S(1)} %get-tuple-element.61), channel_id=1, source_target_pairs={{0,16},{16,0},{32,48},{48,32},{64,80},{80,64},{96,112},{112,96},{1... | collective-permute-start | bytes 110600 | tf_op jit(solution)/shard_map/ppermute | solution.py:531
  13.2 5.2 %collective-permute-start.1 = (f32[3,3,8,128]{3,2,1,0:T(8,128)S(1)}, f32[3,3,8,128]{3,2,1,0:T(8,128)S(1)}, u32[]{:S(2)}, u32[]{:S(2)}) collective-permute-start(f32[3,3,8,128]{3,2,1,0:T(8,128)S(1)} %get-tuple-element.62), channel_id=1, source_target_pairs={{0,240},{16,32},{32,16},{48,64},{64,48},{80,96},{96,80},{112,128},... | collective-permute-start | bytes 110600 | tf_op jit(solution)/shard_map/ppermute | solution.py:531
  18.4 0.0 collective-permute-done.first_in.first_x
  18.4 2.1 %collective-permute-done.1.second_in.second_x = f32[3,3,8,128]{3,2,1,0:T(8,128)S(1)} collective-permute-done((f32[3,3,8,128]{3,2,1,0:T(8,128)S(1)}, f32[3,3,8,128]{3,2,1,0:T(8,128)S(1)}, u32[]{:S(2)}, u32[]{:S(2)}) %collective-permute-start.1) | collective-permute-done | bytes 36896 | tf_op jit(solution)/shard_map/ppermute | solution.py:531
  20.5 0.7 collective-permute-start.2
  21.2 5.4 %collective-permute-start.3 = (f32[3,8,128]{2,1,0:T(8,128)S(1)}, f32[3,8,128]{2,1,0:T(8,128)S(1)}, u32[]{:S(2)}, u32[]{:S(2)}) collective-permute-start(f32[3,8,128]{2,1,0:T(8,128)S(1)} %get-tuple-element.65), channel_id=1, source_target_pairs={{0,15},{1,2},{2,1},{3,4},{4,3},{5,6},{6,5},{7,8},{8,7},{9,10},{10,... | collective-permute-start | bytes 36872 | tf_op jit(solution)/shard_map/ppermute | solution.py:531
  26.6 0.0 collective-permute-done.2.first_y
  26.6 1.2 collective-permute-done.3.second_y
  27.8 0.3 shard_map.98
  28.1 4.0 %collective-permute-start.4 = (f32[15,8,128]{2,1,0:T(8,128)S(1)}, f32[15,8,128]{2,1,0:T(8,128)S(1)}, u32[]{:S(2)}, u32[]{:S(2)}) collective-permute-start(f32[15,8,128]{2,1,0:T(8,128)S(1)} %get-tuple-element.68), channel_id=1, source_target_pairs={{0,16},{16,0},{32,48},{48,32},{64,80},{80,64},{96,112},{112,96},{1... | collective-permute-start | bytes 184328 | tf_op jit(solution)/shard_map/ppermute | solution.py:531
  32.1 2.9 %collective-permute-start.5 = (f32[15,8,128]{2,1,0:T(8,128)S(1)}, f32[15,8,128]{2,1,0:T(8,128)S(1)}, u32[]{:S(2)}, u32[]{:S(2)}) collective-permute-start(f32[15,8,128]{2,1,0:T(8,128)S(1)} %get-tuple-element.69), channel_id=1, source_target_pairs={{0,240},{16,32},{32,16},{48,64},{64,48},{80,96},{96,80},{112,128},... | collective-permute-start | bytes 184328 | tf_op jit(solution)/shard_map/ppermute | solution.py:531
  35.0 0.0 collective-permute-done.4.first_x
  35.0 4.7 %collective-permute-done.5.second_x = f32[15,8,128]{2,1,0:T(8,128)S(1)} collective-permute-done((f32[15,8,128]{2,1,0:T(8,128)S(1)}, f32[15,8,128]{2,1,0:T(8,128)S(1)}, u32[]{:S(2)}, u32[]{:S(2)}) %collective-permute-start.5) | collective-permute-done | bytes 61472 | tf_op jit(solution)/shard_map/ppermute | solution.py:531
  39.7 0.1 shard_map.99
  39.8 0.1 collective-permute-start.6
  39.9 5.3 %collective-permute-start.7 = (f32[11,8,128]{2,1,0:T(8,128)S(1)}, f32[11,8,128]{2,1,0:T(8,128)S(1)}, u32[]{:S(2)}, u32[]{:S(2)}) collective-permute-start(f32[11,8,128]{2,1,0:T(8,128)S(1)} %get-tuple-element.74), channel_id=1, source_target_pairs={{0,15},{1,2},{2,1},{3,4},{4,3},{5,6},{6,5},{7,8},{8,7},{9,10},{10,... | collective-permute-start | bytes 135176 | tf_op jit(solution)/shard_map/ppermute | solution.py:531
  45.2 0.0 collective-permute-done.6.first_y
  45.2 1.9 %collective-permute-done.7.second_y = f32[11,8,128]{2,1,0:T(8,128)S(1)} collective-permute-done((f32[11,8,128]{2,1,0:T(8,128)S(1)}, f32[11,8,128]{2,1,0:T(8,128)S(1)}, u32[]{:S(2)}, u32[]{:S(2)}) %collective-permute-start.7) | collective-permute-done | bytes 45088 | tf_op jit(solution)/shard_map/ppermute | solution.py:531
  47.1 3.4 %shard_map.100 = (f32[19,4,8,128]{3,2,1,0:T(8,128)S(1)}, f32[8,768]{1,0:T(8,128)S(1)}, f32[3,7,8,128]{3,2,1,0:T(8,128)S(1)}, f32[3,3,8,128]{3,2,1,0:T(8,128)S(1)...) custom-call(f32[6,8,128]{2,1,0:T(8,128)S(1)} %select_select_fusion.info_ref, ...), custom_call_target="tpu_custom_call" | custom-call | tf_op jit(solution)/shard_map/pallas_call | solution.py:511
  50.5 4.0 %collective-permute-start.8 = (f32[3,3,8,128]{3,2,1,0:T(8,128)S(1)}, f32[3,3,8,128]{3,2,1,0:T(8,128)S(1)}, u32[]{:S(2)}, u32[]{:S(2)}) collective-permute-start(f32[3,3,8,128]{3,2,1,0:T(8,128)S(1)} %get-tuple-element.80), channel_id=1, source_target_pairs={{0,16},{16,0},{32,48},{48,32},{64,80},{80,64},{96,112},{112,96},{1... | collective-permute-start | bytes 110600 | tf_op jit(solution)/shard_map/ppermute | solution.py:531
  54.5 0.2 collective-permute-start.9
  54.6 0.7 collective-permute-done.8.first_in.first_x
  55.4 6.4 %collective-permute-done.9.second_in.second_x = f32[3,3,8,128]{3,2,1,0:T(8,128)S(1)} collective-permute-done((f32[3,3,8,128]{3,2,1,0:T(8,128)S(1)}, f32[3,3,8,128]{3,2,1,0:T(8,128)S(1)}, u32[]{:S(2)}, u32[]{:S(2)}) %collective-permute-start.9) | collective-permute-done | bytes 36896 | tf_op jit(solution)/shard_map/ppermute | solution.py:531
  61.8 0.3 collective-permute-start.10
  62.1 3.3 %collective-permute-start.11 = (f32[3,8,128]{2,1,0:T(8,128)S(1)}, f32[3,8,128]{2,1,0:T(8,128)S(1)}, u32[]{:S(2)}, u32[]{:S(2)}) collective-permute-start(f32[3,8,128]{2,1,0:T(8,128)S(1)} %get-tuple-element.84), channel_id=1, source_target_pairs={{0,15},{1,2},{2,1},{3,4},{4,3},{5,6},{6,5},{7,8},{8,7},{9,10},{10,... | collective-permute-start | bytes 36872 | tf_op jit(solution)/shard_map/ppermute | solution.py:531
  65.4 0.0 collective-permute-done.10.first_y
  65.4 3.3 %collective-permute-done.11.second_y = f32[3,8,128]{2,1,0:T(8,128)S(1)} collective-permute-done((f32[3,8,128]{2,1,0:T(8,128)S(1)}, f32[3,8,128]{2,1,0:T(8,128)S(1)}, u32[]{:S(2)}, u32[]{:S(2)}) %collective-permute-start.11) | collective-permute-done | bytes 12320 | tf_op jit(solution)/shard_map/ppermute | solution.py:531
  68.6 0.3 shard_map.102
  69.0 3.4 %collective-permute-start.12 = (f32[15,8,128]{2,1,0:T(8,128)S(1)}, f32[15,8,128]{2,1,0:T(8,128)S(1)}, u32[]{:S(2)}, u32[]{:S(2)}) collective-permute-start(f32[15,8,128]{2,1,0:T(8,128)S(1)} %get-tuple-element.87), channel_id=1, source_target_pairs={{0,16},{16,0},{32,48},{48,32},{64,80},{80,64},{96,112},{112,96},{1... | collective-permute-start | bytes 184328 | tf_op jit(solution)/shard_map/ppermute | solution.py:531
  72.4 0.0 collective-permute-start.13
  72.4 0.9 collective-permute-done.12.first_x
  73.3 6.7 %collective-permute-done.13.second_x = f32[15,8,128]{2,1,0:T(8,128)S(1)} collective-permute-done((f32[15,8,128]{2,1,0:T(8,128)S(1)}, f32[15,8,128]{2,1,0:T(8,128)S(1)}, u32[]{:S(2)}, u32[]{:S(2)}) %collective-permute-start.13) | collective-permute-done | bytes 61472 | tf_op jit(solution)/shard_map/ppermute | solution.py:531
  79.9 0.1 shard_map.103
  80.0 0.1 collective-permute-start.14
  80.1 3.4 %collective-permute-start.15 = (f32[11,8,128]{2,1,0:T(8,128)S(1)}, f32[11,8,128]{2,1,0:T(8,128)S(1)}, u32[]{:S(2)}, u32[]{:S(2)}) collective-permute-start(f32[11,8,128]{2,1,0:T(8,128)S(1)} %get-tuple-element.93), channel_id=1, source_target_pairs={{0,15},{1,2},{2,1},{3,4},{4,3},{5,6},{6,5},{7,8},{8,7},{9,10},{10,... | collective-permute-start | bytes 135176 | tf_op jit(solution)/shard_map/ppermute | solution.py:531
  83.5 0.0 collective-permute-done.14.first_y
  83.5 3.7 %collective-permute-done.15.second_y = f32[11,8,128]{2,1,0:T(8,128)S(1)} collective-permute-done((f32[11,8,128]{2,1,0:T(8,128)S(1)}, f32[11,8,128]{2,1,0:T(8,128)S(1)}, u32[]{:S(2)}, u32[]{:S(2)}) %collective-permute-start.15) | collective-permute-done | bytes 45088 | tf_op jit(solution)/shard_map/ppermute | solution.py:531
  87.3 3.4 %shard_map.104 = (f32[19,4,8,128]{3,2,1,0:T(8,128)S(1)}, f32[8,768]{1,0:T(8,128)S(1)}, f32[3,7,8,128]{3,2,1,0:T(8,128)S(1)}, f32[3,3,8,128]{3,2,1,0:T(8,128)S(1)...) custom-call(f32[6,8,128]{2,1,0:T(8,128)S(1)} %select_select_fusion.info_ref, ...), custom_call_target="tpu_custom_call" | custom-call | tf_op jit(solution)/shard_map/pallas_call | solution.py:511
  90.7 3.2 %collective-permute-start.16 = (f32[3,3,8,128]{3,2,1,0:T(8,128)S(1)}, f32[3,3,8,128]{3,2,1,0:T(8,128)S(1)}, u32[]{:S(2)}, u32[]{:S(2)}) collective-permute-start(f32[3,3,8,128]{3,2,1,0:T(8,128)S(1)} %get-tuple-element.97), channel_id=1, source_target_pairs={{0,16},{16,0},{32,48},{48,32},{64,80},{80,64},{96,112},{112,96},{1... | collective-permute-start | bytes 110600 | tf_op jit(solution)/shard_map/ppermute | solution.py:531
  93.9 0.0 collective-permute-start.17
  93.9 0.9 collective-permute-done.16.first_in.first_x
  94.7 6.6 %collective-permute-done.17.second_in.second_x = f32[3,3,8,128]{3,2,1,0:T(8,128)S(1)} collective-permute-done((f32[3,3,8,128]{3,2,1,0:T(8,128)S(1)}, f32[3,3,8,128]{3,2,1,0:T(8,128)S(1)}, u32[]{:S(2)}, u32[]{:S(2)}) %collective-permute-start.17) | collective-permute-done | bytes 36896 | tf_op jit(solution)/shard_map/ppermute | solution.py:531
  101.3 0.1 collective-permute-start.18
  101.4 3.2 %collective-permute-start.19 = (f32[3,8,128]{2,1,0:T(8,128)S(1)}, f32[3,8,128]{2,1,0:T(8,128)S(1)}, u32[]{:S(2)}, u32[]{:S(2)}) collective-permute-start(f32[3,8,128]{2,1,0:T(8,128)S(1)} %get-tuple-element.101), channel_id=1, source_target_pairs={{0,15},{1,2},{2,1},{3,4},{4,3},{5,6},{6,5},{7,8},{8,7},{9,10},{10,... | collective-permute-start | bytes 36872 | tf_op jit(solution)/shard_map/ppermute | solution.py:531
  104.7 0.0 collective-permute-done.18.first_y
  104.7 3.3 %collective-permute-done.19.second_y = f32[3,8,128]{2,1,0:T(8,128)S(1)} collective-permute-done((f32[3,8,128]{2,1,0:T(8,128)S(1)}, f32[3,8,128]{2,1,0:T(8,128)S(1)}, u32[]{:S(2)}, u32[]{:S(2)}) %collective-permute-start.19) | collective-permute-done | bytes 12320 | tf_op jit(solution)/shard_map/ppermute | solution.py:531
  108.0 0.3 shard_map.106
  108.3 3.3 %collective-permute-start.20 = (f32[15,8,128]{2,1,0:T(8,128)S(1)}, f32[15,8,128]{2,1,0:T(8,128)S(1)}, u32[]{:S(2)}, u32[]{:S(2)}) collective-permute-start(f32[15,8,128]{2,1,0:T(8,128)S(1)} %get-tuple-element.104), channel_id=1, source_target_pairs={{0,16},{16,0},{32,48},{48,32},{64,80},{80,64},{96,112},{112,96},{1... | collective-permute-start | bytes 184328 | tf_op jit(solution)/shard_map/ppermute | solution.py:531
  111.6 0.0 collective-permute-start.21
  111.6 0.9 collective-permute-done.20.first_x
  112.5 6.7 %collective-permute-done.21.second_x = f32[15,8,128]{2,1,0:T(8,128)S(1)} collective-permute-done((f32[15,8,128]{2,1,0:T(8,128)S(1)}, f32[15,8,128]{2,1,0:T(8,128)S(1)}, u32[]{:S(2)}, u32[]{:S(2)}) %collective-permute-start.21) | collective-permute-done | bytes 61472 | tf_op jit(solution)/shard_map/ppermute | solution.py:531
  119.2 0.1 shard_map.107
  119.3 0.1 collective-permute-start.22
  119.4 3.6 %collective-permute-start.23 = (f32[11,8,128]{2,1,0:T(8,128)S(1)}, f32[11,8,128]{2,1,0:T(8,128)S(1)}, u32[]{:S(2)}, u32[]{:S(2)}) collective-permute-start(f32[11,8,128]{2,1,0:T(8,128)S(1)} %get-tuple-element.110), channel_id=1, source_target_pairs={{0,15},{1,2},{2,1},{3,4},{4,3},{5,6},{6,5},{7,8},{8,7},{9,10},{10,... | collective-permute-start | bytes 135176 | tf_op jit(solution)/shard_map/ppermute | solution.py:531
  122.9 3.5 %collective-permute-done.23.second_y = f32[11,8,128]{2,1,0:T(8,128)S(1)} collective-permute-done((f32[11,8,128]{2,1,0:T(8,128)S(1)}, f32[11,8,128]{2,1,0:T(8,128)S(1)}, u32[]{:S(2)}, u32[]{:S(2)}) %collective-permute-start.23) | collective-permute-done | bytes 45088 | tf_op jit(solution)/shard_map/ppermute | solution.py:531
  126.4 1.7 %shard_map.108 = (f32[19,4,8,128]{3,2,1,0:T(8,128)}, f32[3,2,768]{2,1,0:T(2,128)}) custom-call(f32[6,8,128]{2,1,0:T(8,128)S(1)} %select_select_fusion.info_ref, f32[608,128]{1,0:T(8,128)S(1)} %get-tuple-element.106.stepped_ref, f32[256,128]{1,0:T(8,128)S(1)} %get-tuple-element.107.inside_ref, f32[6,8,128]{2,1,0:T(8,128)S(1)} %get-tuple-element.108.leaving_ref, ...), custom_call_target="tpu_custom_call" | custom-call | tf_op jit(solution)/shard_map/pallas_call | solution.py:511
  (20 shorter events, 0.1 us)
Async XLA Ops:
  0.6 6.9 %copy-start = (f32[19,4,8,128]{3,2,1,0:T(8,128)S(1)}, f32[19,4,8,128]{3,2,1,0:T(8,128)}, u32[]{:S(2)}) copy-start(f32[19,4,8,128]{3,2,1,0:T(8,128)} %populations_in.1) | copy-start | bytes 933892
  3.2 0.7 copy-start.1
  4.0 3.6 %copy-start.2 = (f32[3,1,1,2,768]{4,3,2,1,0:T(2,128)S(1)}, f32[3,1,1,2,768]{4,3,2,1,0:T(2,128)}, u32[]{:S(2)}) copy-start(f32[3,1,1,2,768]{4,3,2,1,0:T(2,128)} %param.11) | copy-start | bytes 55300
  4.0 3.6 %copy-start.3 = (f32[3,1,1,2,768]{4,3,2,1,0:T(2,128)S(1)}, f32[3,1,1,2,768]{4,3,2,1,0:T(2,128)}, u32[]{:S(2)}) copy-start(f32[3,1,1,2,768]{4,3,2,1,0:T(2,128)} %param.12) | copy-start | bytes 55300
  4.0 3.6 %copy-start.4 = (s32[3,1,1,2,768]{4,3,2,1,0:T(2,128)S(1)}, s32[3,1,1,2,768]{4,3,2,1,0:T(2,128)}, u32[]{:S(2)}) copy-start(s32[3,1,1,2,768]{4,3,2,1,0:T(2,128)} %param.10) | copy-start | bytes 55300
  4.0 3.6 %copy-start.5 = (s32[4,8,128]{2,1,0:T(8,128)S(1)}, s32[4,8,128]{2,1,0:T(8,128)}, u32[]{:S(2)}) copy-start(s32[4,8,128]{2,1,0:T(8,128)} %solid_in.1) | copy-start | bytes 49156
  9.9 8.5 %collective-permute-start = (f32[3,3,8,128]{3,2,1,0:T(8,128)S(1)}, f32[3,3,8,128]{3,2,1,0:T(8,128)S(1)}, u32[]{:S(2)}, u32[]{:S(2)}) collective-permute-start(f32[3,3,8,128]{3,2,1,0:T(8,128)S(1)} %get-tuple-element.61), channel_id=1, source_target_pairs={{0,16},{16,0},{32,48},{48,32},{64,80},{80,64},{96,112},{112,96},{1... | collective-permute-start | bytes 110600 | tf_op jit(solution)/shard_map/ppermute | solution.py:531
  13.2 7.3 %collective-permute-start.1 = (f32[3,3,8,128]{3,2,1,0:T(8,128)S(1)}, f32[3,3,8,128]{3,2,1,0:T(8,128)S(1)}, u32[]{:S(2)}, u32[]{:S(2)}) collective-permute-start(f32[3,3,8,128]{3,2,1,0:T(8,128)S(1)} %get-tuple-element.62), channel_id=1, source_target_pairs={{0,240},{16,32},{32,16},{48,64},{64,48},{80,96},{96,80},{112,128},... | collective-permute-start | bytes 110600 | tf_op jit(solution)/shard_map/ppermute | solution.py:531
  20.5 6.1 %collective-permute-start.2 = (f32[3,8,128]{2,1,0:T(8,128)S(1)}, f32[3,8,128]{2,1,0:T(8,128)S(1)}, u32[]{:S(2)}, u32[]{:S(2)}) collective-permute-start(f32[3,8,128]{2,1,0:T(8,128)S(1)} %get-tuple-element.64), channel_id=1, source_target_pairs={{0,1},{1,0},{2,3},{3,2},{4,5},{5,4},{6,7},{7,6},{8,9},{9,8},{10,11... | collective-permute-start | bytes 36872 | tf_op jit(solution)/shard_map/ppermute | solution.py:531
  21.2 6.6 %collective-permute-start.3 = (f32[3,8,128]{2,1,0:T(8,128)S(1)}, f32[3,8,128]{2,1,0:T(8,128)S(1)}, u32[]{:S(2)}, u32[]{:S(2)}) collective-permute-start(f32[3,8,128]{2,1,0:T(8,128)S(1)} %get-tuple-element.65), channel_id=1, source_target_pairs={{0,15},{1,2},{2,1},{3,4},{4,3},{5,6},{6,5},{7,8},{8,7},{9,10},{10,... | collective-permute-start | bytes 36872 | tf_op jit(solution)/shard_map/ppermute | solution.py:531
  28.1 6.9 %collective-permute-start.4 = (f32[15,8,128]{2,1,0:T(8,128)S(1)}, f32[15,8,128]{2,1,0:T(8,128)S(1)}, u32[]{:S(2)}, u32[]{:S(2)}) collective-permute-start(f32[15,8,128]{2,1,0:T(8,128)S(1)} %get-tuple-element.68), channel_id=1, source_target_pairs={{0,16},{16,0},{32,48},{48,32},{64,80},{80,64},{96,112},{112,96},{1... | collective-permute-start | bytes 184328 | tf_op jit(solution)/shard_map/ppermute | solution.py:531
  32.1 7.6 %collective-permute-start.5 = (f32[15,8,128]{2,1,0:T(8,128)S(1)}, f32[15,8,128]{2,1,0:T(8,128)S(1)}, u32[]{:S(2)}, u32[]{:S(2)}) collective-permute-start(f32[15,8,128]{2,1,0:T(8,128)S(1)} %get-tuple-element.69), channel_id=1, source_target_pairs={{0,240},{16,32},{32,16},{48,64},{64,48},{80,96},{96,80},{112,128},... | collective-permute-start | bytes 184328 | tf_op jit(solution)/shard_map/ppermute | solution.py:531
  39.8 5.4 %collective-permute-start.6 = (f32[11,8,128]{2,1,0:T(8,128)S(1)}, f32[11,8,128]{2,1,0:T(8,128)S(1)}, u32[]{:S(2)}, u32[]{:S(2)}) collective-permute-start(f32[11,8,128]{2,1,0:T(8,128)S(1)} %get-tuple-element.73), channel_id=1, source_target_pairs={{0,1},{1,0},{2,3},{3,2},{4,5},{5,4},{6,7},{7,6},{8,9},{9,8},{10,11... | collective-permute-start | bytes 135176 | tf_op jit(solution)/shard_map/ppermute | solution.py:531
  39.9 7.2 %collective-permute-start.7 = (f32[11,8,128]{2,1,0:T(8,128)S(1)}, f32[11,8,128]{2,1,0:T(8,128)S(1)}, u32[]{:S(2)}, u32[]{:S(2)}) collective-permute-start(f32[11,8,128]{2,1,0:T(8,128)S(1)} %get-tuple-element.74), channel_id=1, source_target_pairs={{0,15},{1,2},{2,1},{3,4},{4,3},{5,6},{6,5},{7,8},{8,7},{9,10},{10,... | collective-permute-start | bytes 135176 | tf_op jit(solution)/shard_map/ppermute | solution.py:531
  50.5 4.9 %collective-permute-start.8 = (f32[3,3,8,128]{3,2,1,0:T(8,128)S(1)}, f32[3,3,8,128]{3,2,1,0:T(8,128)S(1)}, u32[]{:S(2)}, u32[]{:S(2)}) collective-permute-start(f32[3,3,8,128]{3,2,1,0:T(8,128)S(1)} %get-tuple-element.80), channel_id=1, source_target_pairs={{0,16},{16,0},{32,48},{48,32},{64,80},{80,64},{96,112},{112,96},{1... | collective-permute-start | bytes 110600 | tf_op jit(solution)/shard_map/ppermute | solution.py:531
  54.5 7.3 %collective-permute-start.9 = (f32[3,3,8,128]{3,2,1,0:T(8,128)S(1)}, f32[3,3,8,128]{3,2,1,0:T(8,128)S(1)}, u32[]{:S(2)}, u32[]{:S(2)}) collective-permute-start(f32[3,3,8,128]{3,2,1,0:T(8,128)S(1)} %get-tuple-element.81), channel_id=1, source_target_pairs={{0,240},{16,32},{32,16},{48,64},{64,48},{80,96},{96,80},{112,128},... | collective-permute-start | bytes 110600 | tf_op jit(solution)/shard_map/ppermute | solution.py:531
  61.8 3.6 %collective-permute-start.10 = (f32[3,8,128]{2,1,0:T(8,128)S(1)}, f32[3,8,128]{2,1,0:T(8,128)S(1)}, u32[]{:S(2)}, u32[]{:S(2)}) collective-permute-start(f32[3,8,128]{2,1,0:T(8,128)S(1)} %get-tuple-element.83), channel_id=1, source_target_pairs={{0,1},{1,0},{2,3},{3,2},{4,5},{5,4},{6,7},{7,6},{8,9},{9,8},{10,11... | collective-permute-start | bytes 36872 | tf_op jit(solution)/shard_map/ppermute | solution.py:531
  62.1 6.6 %collective-permute-start.11 = (f32[3,8,128]{2,1,0:T(8,128)S(1)}, f32[3,8,128]{2,1,0:T(8,128)S(1)}, u32[]{:S(2)}, u32[]{:S(2)}) collective-permute-start(f32[3,8,128]{2,1,0:T(8,128)S(1)} %get-tuple-element.84), channel_id=1, source_target_pairs={{0,15},{1,2},{2,1},{3,4},{4,3},{5,6},{6,5},{7,8},{8,7},{9,10},{10,... | collective-permute-start | bytes 36872 | tf_op jit(solution)/shard_map/ppermute | solution.py:531
  69.0 4.3 %collective-permute-start.12 = (f32[15,8,128]{2,1,0:T(8,128)S(1)}, f32[15,8,128]{2,1,0:T(8,128)S(1)}, u32[]{:S(2)}, u32[]{:S(2)}) collective-permute-start(f32[15,8,128]{2,1,0:T(8,128)S(1)} %get-tuple-element.87), channel_id=1, source_target_pairs={{0,16},{16,0},{32,48},{48,32},{64,80},{80,64},{96,112},{112,96},{1... | collective-permute-start | bytes 184328 | tf_op jit(solution)/shard_map/ppermute | solution.py:531
  72.4 7.6 %collective-permute-start.13 = (f32[15,8,128]{2,1,0:T(8,128)S(1)}, f32[15,8,128]{2,1,0:T(8,128)S(1)}, u32[]{:S(2)}, u32[]{:S(2)}) collective-permute-start(f32[15,8,128]{2,1,0:T(8,128)S(1)} %get-tuple-element.88), channel_id=1, source_target_pairs={{0,240},{16,32},{32,16},{48,64},{64,48},{80,96},{96,80},{112,128},... | collective-permute-start | bytes 184328 | tf_op jit(solution)/shard_map/ppermute | solution.py:531
  80.0 3.5 %collective-permute-start.14 = (f32[11,8,128]{2,1,0:T(8,128)S(1)}, f32[11,8,128]{2,1,0:T(8,128)S(1)}, u32[]{:S(2)}, u32[]{:S(2)}) collective-permute-start(f32[11,8,128]{2,1,0:T(8,128)S(1)} %get-tuple-element.92), channel_id=1, source_target_pairs={{0,1},{1,0},{2,3},{3,2},{4,5},{5,4},{6,7},{7,6},{8,9},{9,8},{10,11... | collective-permute-start | bytes 135176 | tf_op jit(solution)/shard_map/ppermute | solution.py:531
  80.1 7.2 %collective-permute-start.15 = (f32[11,8,128]{2,1,0:T(8,128)S(1)}, f32[11,8,128]{2,1,0:T(8,128)S(1)}, u32[]{:S(2)}, u32[]{:S(2)}) collective-permute-start(f32[11,8,128]{2,1,0:T(8,128)S(1)} %get-tuple-element.93), channel_id=1, source_target_pairs={{0,15},{1,2},{2,1},{3,4},{4,3},{5,6},{6,5},{7,8},{8,7},{9,10},{10,... | collective-permute-start | bytes 135176 | tf_op jit(solution)/shard_map/ppermute | solution.py:531
  90.7 4.0 %collective-permute-start.16 = (f32[3,3,8,128]{3,2,1,0:T(8,128)S(1)}, f32[3,3,8,128]{3,2,1,0:T(8,128)S(1)}, u32[]{:S(2)}, u32[]{:S(2)}) collective-permute-start(f32[3,3,8,128]{3,2,1,0:T(8,128)S(1)} %get-tuple-element.97), channel_id=1, source_target_pairs={{0,16},{16,0},{32,48},{48,32},{64,80},{80,64},{96,112},{112,96},{1... | collective-permute-start | bytes 110600 | tf_op jit(solution)/shard_map/ppermute | solution.py:531
  93.9 7.4 %collective-permute-start.17 = (f32[3,3,8,128]{3,2,1,0:T(8,128)S(1)}, f32[3,3,8,128]{3,2,1,0:T(8,128)S(1)}, u32[]{:S(2)}, u32[]{:S(2)}) collective-permute-start(f32[3,3,8,128]{3,2,1,0:T(8,128)S(1)} %get-tuple-element.98), channel_id=1, source_target_pairs={{0,240},{16,32},{32,16},{48,64},{64,48},{80,96},{96,80},{112,128},... | collective-permute-start | bytes 110600 | tf_op jit(solution)/shard_map/ppermute | solution.py:531
  101.3 3.3 %collective-permute-start.18 = (f32[3,8,128]{2,1,0:T(8,128)S(1)}, f32[3,8,128]{2,1,0:T(8,128)S(1)}, u32[]{:S(2)}, u32[]{:S(2)}) collective-permute-start(f32[3,8,128]{2,1,0:T(8,128)S(1)} %get-tuple-element.100), channel_id=1, source_target_pairs={{0,1},{1,0},{2,3},{3,2},{4,5},{5,4},{6,7},{7,6},{8,9},{9,8},{10,11... | collective-permute-start | bytes 36872 | tf_op jit(solution)/shard_map/ppermute | solution.py:531
  101.4 6.5 %collective-permute-start.19 = (f32[3,8,128]{2,1,0:T(8,128)S(1)}, f32[3,8,128]{2,1,0:T(8,128)S(1)}, u32[]{:S(2)}, u32[]{:S(2)}) collective-permute-start(f32[3,8,128]{2,1,0:T(8,128)S(1)} %get-tuple-element.101), channel_id=1, source_target_pairs={{0,15},{1,2},{2,1},{3,4},{4,3},{5,6},{6,5},{7,8},{8,7},{9,10},{10,... | collective-permute-start | bytes 36872 | tf_op jit(solution)/shard_map/ppermute | solution.py:531
  108.3 4.2 %collective-permute-start.20 = (f32[15,8,128]{2,1,0:T(8,128)S(1)}, f32[15,8,128]{2,1,0:T(8,128)S(1)}, u32[]{:S(2)}, u32[]{:S(2)}) collective-permute-start(f32[15,8,128]{2,1,0:T(8,128)S(1)} %get-tuple-element.104), channel_id=1, source_target_pairs={{0,16},{16,0},{32,48},{48,32},{64,80},{80,64},{96,112},{112,96},{1... | collective-permute-start | bytes 184328 | tf_op jit(solution)/shard_map/ppermute | solution.py:531
  111.6 7.6 %collective-permute-start.21 = (f32[15,8,128]{2,1,0:T(8,128)S(1)}, f32[15,8,128]{2,1,0:T(8,128)S(1)}, u32[]{:S(2)}, u32[]{:S(2)}) collective-permute-start(f32[15,8,128]{2,1,0:T(8,128)S(1)} %get-tuple-element.105), channel_id=1, source_target_pairs={{0,240},{16,32},{32,16},{48,64},{64,48},{80,96},{96,80},{112,128},... | collective-permute-start | bytes 184328 | tf_op jit(solution)/shard_map/ppermute | solution.py:531
  119.3 3.7 %collective-permute-start.22 = (f32[11,8,128]{2,1,0:T(8,128)S(1)}, f32[11,8,128]{2,1,0:T(8,128)S(1)}, u32[]{:S(2)}, u32[]{:S(2)}) collective-permute-start(f32[11,8,128]{2,1,0:T(8,128)S(1)} %get-tuple-element.109), channel_id=1, source_target_pairs={{0,1},{1,0},{2,3},{3,2},{4,5},{5,4},{6,7},{7,6},{8,9},{9,8},{10,11... | collective-permute-start | bytes 135176 | tf_op jit(solution)/shard_map/ppermute | solution.py:531
  119.4 7.0 %collective-permute-start.23 = (f32[11,8,128]{2,1,0:T(8,128)S(1)}, f32[11,8,128]{2,1,0:T(8,128)S(1)}, u32[]{:S(2)}, u32[]{:S(2)}) collective-permute-start(f32[11,8,128]{2,1,0:T(8,128)S(1)} %get-tuple-element.110), channel_id=1, source_target_pairs={{0,15},{1,2},{2,1},{3,4},{4,3},{5,6},{6,5},{7,8},{8,7},{9,10},{10,... | collective-permute-start | bytes 135176 | tf_op jit(solution)/shard_map/ppermute | solution.py:531

commit v3 on v2

--- a/solution.py
+++ b/solution.py
@@ -46,7 +46,6 @@
 RIM_ROWS = 3 * 3 * 8
 TABLE_ROWS = MAIN_ROWS + RIM_ROWS
 F32 = jnp.float32
-HIGH = lax.Precision.HIGH
 TILE = (8, CZ)
 
 
@@ -121,12 +120,19 @@
     return scale * (pulled - 3.0 * pulled[6:7] * strain)
 
 
-def spread(offset, rest, scale, base, incidence, terms, main_ref, rim_ref):
+def spread(offset, rest, scale, base, incidence, terms, main_ref, rim_ref, plane_ref, depth_ref):
     force = vertex_force(offset, rest, scale, incidence)
     kernels = stencil_kernels(offset)
     grid = None
     for slot in range(SLOTS):
         table_x, table_y, table_rim, table_z = vertex_tables(base, kernels, slot)
+        high = table_z.astype(jnp.bfloat16)
+        low = (table_z - high.astype(F32)).astype(jnp.bfloat16)
+        if depth_ref is not None:
+            for n, table in enumerate((table_x, table_y, table_rim)):
+                plane_ref[slot, n] = table
+            depth_ref[slot, 0] = high
+            depth_ref[slot, 1] = low
         for a in range(3):
             pushed = force[2 * a + slot : 2 * a + slot + 1, :]
             along_x = table_x * pushed
@@ -136,9 +142,11 @@
             for n in range(3):
                 start = MAIN_ROWS + (a * 3 + n) * 8
                 terms[start : start + 8, :] = row_of(along_y, n) * table_x
-        part = lax.dot_general(
-            terms[...], table_z, (((1,), (1,)), ((), ())), precision=HIGH, preferred_element_type=F32
-        )
+        both = halves(terms[...])
+        contract = (((1,), (1,)), ((), ()))
+        part = lax.dot_general(both, high, contract, preferred_element_type=F32)
+        rest_part = lax.dot_general(both[:TABLE_ROWS], low, contract, preferred_element_type=F32)
+        part = part[:TABLE_ROWS] + part[TABLE_ROWS:] + rest_part
         grid = part if grid is None else grid + part
     main_ref[...] = grid[:MAIN_ROWS].reshape(3, 7, 8, CZ)
     rim_ref[...] = grid[MAIN_ROWS:].reshape(3, 3, 8, CZ)
@@ -168,10 +176,23 @@
 
 
 def spread_kernel(
-    info_ref, offset_in, rest_in, base_in, populations_in, solid_in, incidence_ref,
-    main_ref, rim_ref, first_ref, second_ref,
-    offset_ref, rest_ref, base_ref, populations_ref, solid_ref, terms,
+    stiffness_ref, occupied_ref, offset_in, rest_in, base_in, populations_in, solid_in, incidence_ref,
+    main_ref, rim_ref, first_ref, second_ref, plane_ref, depth_ref,
+    offset_ref, rest_ref, base_ref, populations_ref, solid_ref, info_ref, terms,
 ):
+    place_x = lax.axis_index("gx")
+    place_y = lax.axis_index("gy")
+    even_row = lax.rem(tile_rows(), 2) == 0
+
+    def by_slot(row):
+        return jnp.where(even_row, row[:, 0:1], row[:, 1:2])
+
+    held = by_slot(occupied_ref[...].astype(F32))
+    info_ref[4] = by_slot(stiffness_ref[...]) * held
+    info_ref[5] = held
+    numbers = (lax.rem(place_x, 2), lax.rem(place_y, 2), place_x * CX, place_y * CY)
+    for n, number in enumerate(numbers):
+        info_ref[n] = jnp.full(TILE, number, jnp.int32).astype(F32)
     offset_ref[...] = six_rows(offset_in)
     rest_ref[...] = six_rows(rest_in)
     base_ref[...] = own_base(info_ref, base_in)
@@ -179,7 +200,7 @@
     solid_ref[...] = solid_in[...]
     spread(
         offset_ref[...], rest_ref[...], wide(info_ref[4]), base_ref[...],
-        incidence_ref, terms, main_ref, rim_ref,
+        incidence_ref, terms, main_ref, rim_ref, plane_ref, depth_ref,
     )
     spread_messages(info_ref, main_ref, rim_ref, first_ref, second_ref)
 
@@ -456,13 +477,15 @@
         flow[start : start + 8, :] = above[8 + a]
 
 
-def sample(offset, live, base, flow):
-    kernels = stencil_kernels(offset)
+def sample(offset, live, plane_ref, depth_ref, flow):
     moved = [None] * 8
     zero = jnp.zeros((1, PAD), F32)
+    both = halves(flow[...])
     for slot in range(SLOTS):
-        table_x, table_y, table_rim, table_z = vertex_tables(base, kernels, slot)
-        along = jnp.dot(flow[...], table_z, precision=HIGH, preferred_element_type=F32)
+        table_x, table_y, table_rim = [plane_ref[slot, n] for n in range(3)]
+        along = jnp.dot(both, depth_ref[slot, 0], preferred_element_type=F32)
+        rest = jnp.dot(both[:TABLE_ROWS], depth_ref[slot, 1], preferred_element_type=F32)
+        along = along[:TABLE_ROWS] + along[TABLE_ROWS:] + rest
         for a in range(3):
             inner = None
             for n in range(7):
@@ -482,24 +505,26 @@
 
 
 def next_kernel(
-    info_ref, stepped_ref, inside_ref, leaving_ref, first_y, second_y,
+    info_ref, stepped_ref, inside_ref, leaving_ref, first_y, second_y, plane_in, depth_in,
     offset_ref, rest_ref, base_ref, incidence_ref,
-    out_ref, offset_out, main_ref, rim_ref, first_ref, second_ref, flow, terms,
+    out_ref, offset_out, main_ref, rim_ref, first_ref, second_ref, plane_ref, depth_ref, flow, terms,
 ):
     finish_fluid(info_ref, stepped_ref, inside_ref, leaving_ref, first_y, second_y, out_ref, flow)
-    base = base_ref[...]
-    offset = sample(offset_ref[...], wide(info_ref[5]), base, flow)
+    offset = sample(offset_ref[...], wide(info_ref[5]), plane_in, depth_in, flow)
     offset_out[...] = offset
-    spread(offset, rest_ref[...], wide(info_ref[4]), base, incidence_ref, terms, main_ref, rim_ref)
+    spread(
+        offset, rest_ref[...], wide(info_ref[4]), base_ref[...],
+        incidence_ref, terms, main_ref, rim_ref, plane_ref, depth_ref,
+    )
     spread_messages(info_ref, main_ref, rim_ref, first_ref, second_ref)
 
 
 def last_kernel(
-    info_ref, stepped_ref, inside_ref, leaving_ref, first_y, second_y, offset_ref, base_ref,
+    info_ref, stepped_ref, inside_ref, leaving_ref, first_y, second_y, plane_in, depth_in, offset_ref,
     out_ref, offset_out, flow,
 ):
     finish_fluid(info_ref, stepped_ref, inside_ref, leaving_ref, first_y, second_y, out_ref, flow)
-    offset = sample(offset_ref[...], wide(info_ref[5]), base_ref[...], flow)
+    offset = sample(offset_ref[...], wide(info_ref[5]), plane_in, depth_in, flow)
     for a in range(3):
         offset_out[a] = offset[2 * a : 2 * a + 2]
 
@@ -537,41 +562,30 @@
     ((3, 3, 8, CZ), F32),
     ((3, 3, 8, CZ), F32),
     ((3, 3, 8, CZ), F32),
+    ((SLOTS, 3, 8, PAD), F32),
+    ((SLOTS, 2, CZ, PAD), jnp.bfloat16),
 ]
 STEPPED = ((19, 4, 8, CZ), F32)
 
 
 def steps(populations, solid, base_cell, offset, rest_displacement, stiffness, occupied, triangles):
-    place_x = lax.axis_index("gx")
-    place_y = lax.axis_index("gy")
-    held = occupied.reshape(SLOTS).astype(F32)
-    spring = stiffness.reshape(SLOTS) * held
-    lead = lax.broadcasted_iota(jnp.int32, (6, 8, CZ), 0)
-    even_row = lax.broadcasted_iota(jnp.int32, (6, 8, CZ), 1) % 2 == 0
-    info = jnp.where(even_row, held[0], held[1])
-    info = jnp.where(lead == 4, jnp.where(even_row, spring[0], spring[1]), info)
-    numbers = (place_x % 2, place_y % 2, place_x * CX, place_y * CY)
-    for n, number in enumerate(numbers):
-        info = jnp.where(lead == n, number.astype(F32), info)
     stored = (3, SLOTS, PAD)
     rows = (8, PAD)
     terms = ((TABLE_ROWS, PAD), F32)
     flow = ((TABLE_ROWS, CZ), F32)
     corners = triangles.T
     (incidence,) = call(incidence_kernel, [((PAD, corners.shape[1]), jnp.bfloat16)], [], corners)
-    main, rim, first, second, where, rest, base, populations, solid = call(
+    main, rim, first, second, plane, depth, where, rest, base, populations, solid, info = call(
         spread_kernel,
         SPREAD_OUT
-        + [(rows, F32), (rows, F32), (rows, jnp.int32), STEPPED, (solid.shape, jnp.int32)],
+        + [(rows, F32), (rows, F32), (rows, jnp.int32), STEPPED, (solid.shape, jnp.int32), ((6, 8, CZ), F32)],
         [terms],
-        info, offset.reshape(stored), rest_displacement.reshape(stored), base_cell.reshape(stored),
+        stiffness.reshape(1, SLOTS), occupied.reshape(1, SLOTS), offset.reshape(stored), rest_displacement.reshape(stored), base_cell.reshape(stored),
         populations, solid, incidence,
     )
     for substep in range(SUBSTEPS):
         first_x, second_x = exchange(first, second, "gx")
-        corner = call(
-            force_corner_kernel, [((3, 8, CZ), F32)] * 2, [], info, rim, first_x, second_x,
-        )
+        corner = call(force_corner_kernel, [((3, 8, CZ), F32)] * 2, [], info, rim, first_x, second_x)
         first_y, second_y = exchange(*corner, "gy")
         stepped, force, first, second = call(
             collide_kernel,
@@ -590,16 +604,14 @@
             info, stepped, force, first_x, second_x,
         )
         first_y, second_y = exchange(first, second, "gy")
-        fluid = (info, stepped, inside, leaving, first_y, second_y)
+        fluid = (info, stepped, inside, leaving, first_y, second_y, plane, depth)
         if substep < SUBSTEPS - 1:
-            populations, where, main, rim, first, second = call(
+            populations, where, main, rim, first, second, plane, depth = call(
                 next_kernel, [STEPPED, (rows, F32)] + SPREAD_OUT, [flow, terms],
                 *fluid, where, rest, base, incidence,
             )
         else:
-            populations, where = call(
-                last_kernel, [STEPPED, (stored, F32)], [flow], *fluid, where, base
-            )
+            populations, where = call(last_kernel, [STEPPED, (stored, F32)], [flow], *fluid, where)
     return populations, where.reshape(offset.shape)
 
 

time: 128 us -> 122 us (0.953)
  other arithmetic: 3.93 us -> 0 us
    select_n x1 -> x0, other arithmetic: 2.57 us -> none  [steps(): info = jnp.where(lead == n, number.astype(F32), info)]
where the time goes in v3:
time: 122 us
  starting transfers between devices  54.6 us (45%)
  waiting for transfers between devices  53.9 us (44%)
  Pallas kernels  12 us (10%)
    ppermute x24, starting transfers between devices, exchange(): out[kind] = lax.ppermute(message, axis, pairs)  54.6 us
    ppermute x24, waiting for transfers between devices, exchange(): out[kind] = lax.ppermute(message, axis, pairs)  53.9 us
    pallas_call x14, Pallas kernels, call(): pl.pallas_call(kernel, out_shape=[jax.ShapeDtypeStruct(shape, dtype) for...  12 us
  transfers between devices with their start and end apart: 24, of which 16 were waited for; matrix products, arithmetic and copies ran while one was open for 0% of the time, Pallas kernels for 0%

profile of v3, /device:TPU:1, one launch (start us, length us, event | category | flops | bytes accessed | tf_op | source)
XLA Modules:
  0.0 122.1 jit_solution(2624873773160144196)
XLA Ops:
  0.6 0.0 copy-start
  0.6 0.0 copy-start.1
  0.7 0.8 copy-done.1
  1.4 0.0 copy-start.6
  1.4 0.0 copy-start.7
  1.4 1.0 shard_map.95.incidence_ref
  2.5 1.8 %shard_map.96 = (f32[3,7,8,128]{3,2,1,0:T(8,128)S(1)}, f32[3,3,8,128]{3,2,1,0:T(8,128)S(1)}, f32[3,3,8,128]{3,2,1,0:T(8,128)S(1)}, f32[3,3,8,128]{3,2,1,0:T(8,12...) custom-call(f32[1,2]{1,0:T(1,128)S(1)} %bitcast.13, ...), custom_call_target="tpu_custom_call" | custom-call | tf_op jit(solution)/shard_map/pallas_call | solution.py:536
  4.4 3.3 %collective-permute-start = (f32[3,3,8,128]{3,2,1,0:T(8,128)S(1)}, f32[3,3,8,128]{3,2,1,0:T(8,128)S(1)}, u32[]{:S(2)}, u32[]{:S(2)}) collective-permute-start(f32[3,3,8,128]{3,2,1,0:T(8,128)S(1)} %get-tuple-element.69), channel_id=1, source_target_pairs={{0,16},{16,0},{32,48},{48,32},{64,80},{80,64},{96,112},{112,96},{1... | collective-permute-start | bytes 110600 | tf_op jit(solution)/shard_map/ppermute | solution.py:556
  7.7 5.2 %collective-permute-start.1 = (f32[3,3,8,128]{3,2,1,0:T(8,128)S(1)}, f32[3,3,8,128]{3,2,1,0:T(8,128)S(1)}, u32[]{:S(2)}, u32[]{:S(2)}) collective-permute-start(f32[3,3,8,128]{3,2,1,0:T(8,128)S(1)} %get-tuple-element.70), channel_id=1, source_target_pairs={{0,240},{16,32},{32,16},{48,64},{64,48},{80,96},{96,80},{112,128},... | collective-permute-start | bytes 110600 | tf_op jit(solution)/shard_map/ppermute | solution.py:556
  12.8 0.0 collective-permute-done.first_in.first_x
  12.8 2.1 %collective-permute-done.1.second_in.second_x = f32[3,3,8,128]{3,2,1,0:T(8,128)S(1)} collective-permute-done((f32[3,3,8,128]{3,2,1,0:T(8,128)S(1)}, f32[3,3,8,128]{3,2,1,0:T(8,128)S(1)}, u32[]{:S(2)}, u32[]{:S(2)}) %collective-permute-start.1) | collective-permute-done | bytes 36896 | tf_op jit(solution)/shard_map/ppermute | solution.py:556
  15.0 0.7 collective-permute-start.2
  15.6 5.4 %collective-permute-start.3 = (f32[3,8,128]{2,1,0:T(8,128)S(1)}, f32[3,8,128]{2,1,0:T(8,128)S(1)}, u32[]{:S(2)}, u32[]{:S(2)}) collective-permute-start(f32[3,8,128]{2,1,0:T(8,128)S(1)} %get-tuple-element.73), channel_id=1, source_target_pairs={{0,15},{1,2},{2,1},{3,4},{4,3},{5,6},{6,5},{7,8},{8,7},{9,10},{10,... | collective-permute-start | bytes 36872 | tf_op jit(solution)/shard_map/ppermute | solution.py:556
  21.0 0.0 collective-permute-done.2.first_y
  21.0 1.2 collective-permute-done.3.second_y
  22.3 0.3 shard_map.98
  22.6 4.0 %collective-permute-start.4 = (f32[15,8,128]{2,1,0:T(8,128)S(1)}, f32[15,8,128]{2,1,0:T(8,128)S(1)}, u32[]{:S(2)}, u32[]{:S(2)}) collective-permute-start(f32[15,8,128]{2,1,0:T(8,128)S(1)} %get-tuple-element.76), channel_id=1, source_target_pairs={{0,16},{16,0},{32,48},{48,32},{64,80},{80,64},{96,112},{112,96},{1... | collective-permute-start | bytes 184328 | tf_op jit(solution)/shard_map/ppermute | solution.py:556
  26.6 2.9 %collective-permute-start.5 = (f32[15,8,128]{2,1,0:T(8,128)S(1)}, f32[15,8,128]{2,1,0:T(8,128)S(1)}, u32[]{:S(2)}, u32[]{:S(2)}) collective-permute-start(f32[15,8,128]{2,1,0:T(8,128)S(1)} %get-tuple-element.77), channel_id=1, source_target_pairs={{0,240},{16,32},{32,16},{48,64},{64,48},{80,96},{96,80},{112,128},... | collective-permute-start | bytes 184328 | tf_op jit(solution)/shard_map/ppermute | solution.py:556
  29.4 0.0 collective-permute-done.4.first_x
  29.4 4.7 %collective-permute-done.5.second_x = f32[15,8,128]{2,1,0:T(8,128)S(1)} collective-permute-done((f32[15,8,128]{2,1,0:T(8,128)S(1)}, f32[15,8,128]{2,1,0:T(8,128)S(1)}, u32[]{:S(2)}, u32[]{:S(2)}) %collective-permute-start.5) | collective-permute-done | bytes 61472 | tf_op jit(solution)/shard_map/ppermute | solution.py:556
  34.1 0.1 shard_map.99
  34.2 0.1 collective-permute-start.6
  34.3 5.3 %collective-permute-start.7 = (f32[11,8,128]{2,1,0:T(8,128)S(1)}, f32[11,8,128]{2,1,0:T(8,128)S(1)}, u32[]{:S(2)}, u32[]{:S(2)}) collective-permute-start(f32[11,8,128]{2,1,0:T(8,128)S(1)} %get-tuple-element.82), channel_id=1, source_target_pairs={{0,15},{1,2},{2,1},{3,4},{4,3},{5,6},{6,5},{7,8},{8,7},{9,10},{10,... | collective-permute-start | bytes 135176 | tf_op jit(solution)/shard_map/ppermute | solution.py:556
  39.6 0.0 collective-permute-done.6.first_y
  39.6 1.9 %collective-permute-done.7.second_y = f32[11,8,128]{2,1,0:T(8,128)S(1)} collective-permute-done((f32[11,8,128]{2,1,0:T(8,128)S(1)}, f32[11,8,128]{2,1,0:T(8,128)S(1)}, u32[]{:S(2)}, u32[]{:S(2)}) %collective-permute-start.7) | collective-permute-done | bytes 45088 | tf_op jit(solution)/shard_map/ppermute | solution.py:556
  41.5 3.2 %shard_map.100 = (f32[19,4,8,128]{3,2,1,0:T(8,128)S(1)}, f32[8,768]{1,0:T(8,128)S(1)}, f32[3,7,8,128]{3,2,1,0:T(8,128)S(1)}, f32[3,3,8,128]{3,2,1,0:T(8,128)S(1)...) custom-call(f32[6,8,128]{2,1,0:T(8,128)S(1)} %get-tuple-element.65.i, ...), custom_call_target="tpu_custom_call" | custom-call | tf_op jit(solution)/shard_map/pallas_call | solution.py:536
  44.8 4.0 %collective-permute-start.8 = (f32[3,3,8,128]{3,2,1,0:T(8,128)S(1)}, f32[3,3,8,128]{3,2,1,0:T(8,128)S(1)}, u32[]{:S(2)}, u32[]{:S(2)}) collective-permute-start(f32[3,3,8,128]{3,2,1,0:T(8,128)S(1)} %get-tuple-element.90), channel_id=1, source_target_pairs={{0,16},{16,0},{32,48},{48,32},{64,80},{80,64},{96,112},{112,96},{1... | collective-permute-start | bytes 110600 | tf_op jit(solution)/shard_map/ppermute | solution.py:556
  48.8 0.2 collective-permute-start.9
  48.9 0.7 collective-permute-done.8.first_in.first_x
  49.6 6.4 %collective-permute-done.9.second_in.second_x = f32[3,3,8,128]{3,2,1,0:T(8,128)S(1)} collective-permute-done((f32[3,3,8,128]{3,2,1,0:T(8,128)S(1)}, f32[3,3,8,128]{3,2,1,0:T(8,128)S(1)}, u32[]{:S(2)}, u32[]{:S(2)}) %collective-permute-start.9) | collective-permute-done | bytes 36896 | tf_op jit(solution)/shard_map/ppermute | solution.py:556
  56.1 0.1 collective-permute-start.10
  56.2 3.4 %collective-permute-start.11 = (f32[3,8,128]{2,1,0:T(8,128)S(1)}, f32[3,8,128]{2,1,0:T(8,128)S(1)}, u32[]{:S(2)}, u32[]{:S(2)}) collective-permute-start(f32[3,8,128]{2,1,0:T(8,128)S(1)} %get-tuple-element.94), channel_id=1, source_target_pairs={{0,15},{1,2},{2,1},{3,4},{4,3},{5,6},{6,5},{7,8},{8,7},{9,10},{10,... | collective-permute-start | bytes 36872 | tf_op jit(solution)/shard_map/ppermute | solution.py:556
  59.6 0.0 collective-permute-done.10.first_y
  59.6 3.3 %collective-permute-done.11.second_y = f32[3,8,128]{2,1,0:T(8,128)S(1)} collective-permute-done((f32[3,8,128]{2,1,0:T(8,128)S(1)}, f32[3,8,128]{2,1,0:T(8,128)S(1)}, u32[]{:S(2)}, u32[]{:S(2)}) %collective-permute-start.11) | collective-permute-done | bytes 12320 | tf_op jit(solution)/shard_map/ppermute | solution.py:556
  63.0 0.3 shard_map.102
  63.3 3.4 %collective-permute-start.12 = (f32[15,8,128]{2,1,0:T(8,128)S(1)}, f32[15,8,128]{2,1,0:T(8,128)S(1)}, u32[]{:S(2)}, u32[]{:S(2)}) collective-permute-start(f32[15,8,128]{2,1,0:T(8,128)S(1)} %get-tuple-element.97), channel_id=1, source_target_pairs={{0,16},{16,0},{32,48},{48,32},{64,80},{80,64},{96,112},{112,96},{1... | collective-permute-start | bytes 184328 | tf_op jit(solution)/shard_map/ppermute | solution.py:556
  66.7 0.0 collective-permute-start.13
  66.7 0.9 collective-permute-done.12.first_x
  67.5 6.7 %collective-permute-done.13.second_x = f32[15,8,128]{2,1,0:T(8,128)S(1)} collective-permute-done((f32[15,8,128]{2,1,0:T(8,128)S(1)}, f32[15,8,128]{2,1,0:T(8,128)S(1)}, u32[]{:S(2)}, u32[]{:S(2)}) %collective-permute-start.13) | collective-permute-done | bytes 61472 | tf_op jit(solution)/shard_map/ppermute | solution.py:556
  74.2 0.1 shard_map.103
  74.3 0.1 collective-permute-start.14
  74.4 3.3 %collective-permute-start.15 = (f32[11,8,128]{2,1,0:T(8,128)S(1)}, f32[11,8,128]{2,1,0:T(8,128)S(1)}, u32[]{:S(2)}, u32[]{:S(2)}) collective-permute-start(f32[11,8,128]{2,1,0:T(8,128)S(1)} %get-tuple-element.103), channel_id=1, source_target_pairs={{0,15},{1,2},{2,1},{3,4},{4,3},{5,6},{6,5},{7,8},{8,7},{9,10},{10,... | collective-permute-start | bytes 135176 | tf_op jit(solution)/shard_map/ppermute | solution.py:556
  77.7 0.0 collective-permute-done.14.first_y
  77.8 3.9 %collective-permute-done.15.second_y = f32[11,8,128]{2,1,0:T(8,128)S(1)} collective-permute-done((f32[11,8,128]{2,1,0:T(8,128)S(1)}, f32[11,8,128]{2,1,0:T(8,128)S(1)}, u32[]{:S(2)}, u32[]{:S(2)}) %collective-permute-start.15) | collective-permute-done | bytes 45088 | tf_op jit(solution)/shard_map/ppermute | solution.py:556
  81.6 3.2 %shard_map.104 = (f32[19,4,8,128]{3,2,1,0:T(8,128)S(1)}, f32[8,768]{1,0:T(8,128)S(1)}, f32[3,7,8,128]{3,2,1,0:T(8,128)S(1)}, f32[3,3,8,128]{3,2,1,0:T(8,128)S(1)...) custom-call(f32[6,8,128]{2,1,0:T(8,128)S(1)} %get-tuple-element.65.i, ...), custom_call_target="tpu_custom_call" | custom-call | tf_op jit(solution)/shard_map/pallas_call | solution.py:536
  84.9 3.1 %collective-permute-start.16 = (f32[3,3,8,128]{3,2,1,0:T(8,128)S(1)}, f32[3,3,8,128]{3,2,1,0:T(8,128)S(1)}, u32[]{:S(2)}, u32[]{:S(2)}) collective-permute-start(f32[3,3,8,128]{3,2,1,0:T(8,128)S(1)} %get-tuple-element.109), channel_id=1, source_target_pairs={{0,16},{16,0},{32,48},{48,32},{64,80},{80,64},{96,112},{112,96},{1... | collective-permute-start | bytes 110600 | tf_op jit(solution)/shard_map/ppermute | solution.py:556
  88.0 0.0 collective-permute-start.17
  88.0 0.9 collective-permute-done.16.first_in.first_x
  88.8 6.6 %collective-permute-done.17.second_in.second_x = f32[3,3,8,128]{3,2,1,0:T(8,128)S(1)} collective-permute-done((f32[3,3,8,128]{3,2,1,0:T(8,128)S(1)}, f32[3,3,8,128]{3,2,1,0:T(8,128)S(1)}, u32[]{:S(2)}, u32[]{:S(2)}) %collective-permute-start.17) | collective-permute-done | bytes 36896 | tf_op jit(solution)/shard_map/ppermute | solution.py:556
  95.4 0.1 collective-permute-start.18
  95.5 3.2 %collective-permute-start.19 = (f32[3,8,128]{2,1,0:T(8,128)S(1)}, f32[3,8,128]{2,1,0:T(8,128)S(1)}, u32[]{:S(2)}, u32[]{:S(2)}) collective-permute-start(f32[3,8,128]{2,1,0:T(8,128)S(1)} %get-tuple-element.113), channel_id=1, source_target_pairs={{0,15},{1,2},{2,1},{3,4},{4,3},{5,6},{6,5},{7,8},{8,7},{9,10},{10,... | collective-permute-start | bytes 36872 | tf_op jit(solution)/shard_map/ppermute | solution.py:556
  98.7 0.0 collective-permute-done.18.first_y
  98.7 3.4 %collective-permute-done.19.second_y = f32[3,8,128]{2,1,0:T(8,128)S(1)} collective-permute-done((f32[3,8,128]{2,1,0:T(8,128)S(1)}, f32[3,8,128]{2,1,0:T(8,128)S(1)}, u32[]{:S(2)}, u32[]{:S(2)}) %collective-permute-start.19) | collective-permute-done | bytes 12320 | tf_op jit(solution)/shard_map/ppermute | solution.py:556
  102.1 0.3 shard_map.106
  102.4 3.3 %collective-permute-start.20 = (f32[15,8,128]{2,1,0:T(8,128)S(1)}, f32[15,8,128]{2,1,0:T(8,128)S(1)}, u32[]{:S(2)}, u32[]{:S(2)}) collective-permute-start(f32[15,8,128]{2,1,0:T(8,128)S(1)} %get-tuple-element.116), channel_id=1, source_target_pairs={{0,16},{16,0},{32,48},{48,32},{64,80},{80,64},{96,112},{112,96},{1... | collective-permute-start | bytes 184328 | tf_op jit(solution)/shard_map/ppermute | solution.py:556
  105.7 0.0 collective-permute-start.21
  105.7 0.9 collective-permute-done.20.first_x
  106.6 6.7 %collective-permute-done.21.second_x = f32[15,8,128]{2,1,0:T(8,128)S(1)} collective-permute-done((f32[15,8,128]{2,1,0:T(8,128)S(1)}, f32[15,8,128]{2,1,0:T(8,128)S(1)}, u32[]{:S(2)}, u32[]{:S(2)}) %collective-permute-start.21) | collective-permute-done | bytes 61472 | tf_op jit(solution)/shard_map/ppermute | solution.py:556
  113.3 0.1 shard_map.107
  113.4 0.1 collective-permute-start.22
  113.5 3.5 %collective-permute-start.23 = (f32[11,8,128]{2,1,0:T(8,128)S(1)}, f32[11,8,128]{2,1,0:T(8,128)S(1)}, u32[]{:S(2)}, u32[]{:S(2)}) collective-permute-start(f32[11,8,128]{2,1,0:T(8,128)S(1)} %get-tuple-element.122), channel_id=1, source_target_pairs={{0,15},{1,2},{2,1},{3,4},{4,3},{5,6},{6,5},{7,8},{8,7},{9,10},{10,... | collective-permute-start | bytes 135176 | tf_op jit(solution)/shard_map/ppermute | solution.py:556
  117.0 0.0 collective-permute-done.22.first_y
  117.0 3.7 %collective-permute-done.23.second_y = f32[11,8,128]{2,1,0:T(8,128)S(1)} collective-permute-done((f32[11,8,128]{2,1,0:T(8,128)S(1)}, f32[11,8,128]{2,1,0:T(8,128)S(1)}, u32[]{:S(2)}, u32[]{:S(2)}) %collective-permute-start.23) | collective-permute-done | bytes 45088 | tf_op jit(solution)/shard_map/ppermute | solution.py:556
  120.7 1.4 %shard_map.108 = (f32[19,4,8,128]{3,2,1,0:T(8,128)}, f32[3,2,768]{2,1,0:T(2,128)}) custom-call(f32[6,8,128]{2,1,0:T(8,128)S(1)} %get-tuple-element.65.info_ref, f32[608,128]{1,0:T(8,128)S(1)} %get-tuple-element.118.stepped_ref, f32[256,128]{1,0:T(8,128)S(1)} %get-tuple-element.119.inside_ref, f32[6,8,128]{2,1,0:T(8,128)S(1)} %get-tuple-element.120.leaving_ref, ...), custom_call_target="tpu_custom_call" | custom-call | tf_op jit(solution)/shard_map/pallas_call | solution.py:536
  (14 shorter events, 0.1 us)
Async XLA Ops:
  0.6 1.8 %copy-start = (f32[19,4,8,128]{3,2,1,0:T(8,128)S(1)}, f32[19,4,8,128]{3,2,1,0:T(8,128)}, u32[]{:S(2)}) copy-start(f32[19,4,8,128]{3,2,1,0:T(8,128)} %populations_in.1) | copy-start | bytes 933892
  0.6 0.8 copy-start.1
  1.4 1.1 copy-start.2
  1.4 1.1 copy-start.3
  1.4 1.1 copy-start.4
  1.4 1.1 copy-start.5
  1.4 1.1 copy-start.6
  1.4 1.1 copy-start.7
  4.4 8.5 %collective-permute-start = (f32[3,3,8,128]{3,2,1,0:T(8,128)S(1)}, f32[3,3,8,128]{3,2,1,0:T(8,128)S(1)}, u32[]{:S(2)}, u32[]{:S(2)}) collective-permute-start(f32[3,3,8,128]{3,2,1,0:T(8,128)S(1)} %get-tuple-element.69), channel_id=1, source_target_pairs={{0,16},{16,0},{32,48},{48,32},{64,80},{80,64},{96,112},{112,96},{1... | collective-permute-start | bytes 110600 | tf_op jit(solution)/shard_map/ppermute | solution.py:556
  7.7 7.3 %collective-permute-start.1 = (f32[3,3,8,128]{3,2,1,0:T(8,128)S(1)}, f32[3,3,8,128]{3,2,1,0:T(8,128)S(1)}, u32[]{:S(2)}, u32[]{:S(2)}) collective-permute-start(f32[3,3,8,128]{3,2,1,0:T(8,128)S(1)} %get-tuple-element.70), channel_id=1, source_target_pairs={{0,240},{16,32},{32,16},{48,64},{64,48},{80,96},{96,80},{112,128},... | collective-permute-start | bytes 110600 | tf_op jit(solution)/shard_map/ppermute | solution.py:556
  15.0 6.1 %collective-permute-start.2 = (f32[3,8,128]{2,1,0:T(8,128)S(1)}, f32[3,8,128]{2,1,0:T(8,128)S(1)}, u32[]{:S(2)}, u32[]{:S(2)}) collective-permute-start(f32[3,8,128]{2,1,0:T(8,128)S(1)} %get-tuple-element.72), channel_id=1, source_target_pairs={{0,1},{1,0},{2,3},{3,2},{4,5},{5,4},{6,7},{7,6},{8,9},{9,8},{10,11... | collective-permute-start | bytes 36872 | tf_op jit(solution)/shard_map/ppermute | solution.py:556
  15.6 6.6 %collective-permute-start.3 = (f32[3,8,128]{2,1,0:T(8,128)S(1)}, f32[3,8,128]{2,1,0:T(8,128)S(1)}, u32[]{:S(2)}, u32[]{:S(2)}) collective-permute-start(f32[3,8,128]{2,1,0:T(8,128)S(1)} %get-tuple-element.73), channel_id=1, source_target_pairs={{0,15},{1,2},{2,1},{3,4},{4,3},{5,6},{6,5},{7,8},{8,7},{9,10},{10,... | collective-permute-start | bytes 36872 | tf_op jit(solution)/shard_map/ppermute | solution.py:556
  22.6 6.9 %collective-permute-start.4 = (f32[15,8,128]{2,1,0:T(8,128)S(1)}, f32[15,8,128]{2,1,0:T(8,128)S(1)}, u32[]{:S(2)}, u32[]{:S(2)}) collective-permute-start(f32[15,8,128]{2,1,0:T(8,128)S(1)} %get-tuple-element.76), channel_id=1, source_target_pairs={{0,16},{16,0},{32,48},{48,32},{64,80},{80,64},{96,112},{112,96},{1... | collective-permute-start | bytes 184328 | tf_op jit(solution)/shard_map/ppermute | solution.py:556
  26.6 7.6 %collective-permute-start.5 = (f32[15,8,128]{2,1,0:T(8,128)S(1)}, f32[15,8,128]{2,1,0:T(8,128)S(1)}, u32[]{:S(2)}, u32[]{:S(2)}) collective-permute-start(f32[15,8,128]{2,1,0:T(8,128)S(1)} %get-tuple-element.77), channel_id=1, source_target_pairs={{0,240},{16,32},{32,16},{48,64},{64,48},{80,96},{96,80},{112,128},... | collective-permute-start | bytes 184328 | tf_op jit(solution)/shard_map/ppermute | solution.py:556
  34.2 5.4 %collective-permute-start.6 = (f32[11,8,128]{2,1,0:T(8,128)S(1)}, f32[11,8,128]{2,1,0:T(8,128)S(1)}, u32[]{:S(2)}, u32[]{:S(2)}) collective-permute-start(f32[11,8,128]{2,1,0:T(8,128)S(1)} %get-tuple-element.81), channel_id=1, source_target_pairs={{0,1},{1,0},{2,3},{3,2},{4,5},{5,4},{6,7},{7,6},{8,9},{9,8},{10,11... | collective-permute-start | bytes 135176 | tf_op jit(solution)/shard_map/ppermute | solution.py:556
  34.3 7.2 %collective-permute-start.7 = (f32[11,8,128]{2,1,0:T(8,128)S(1)}, f32[11,8,128]{2,1,0:T(8,128)S(1)}, u32[]{:S(2)}, u32[]{:S(2)}) collective-permute-start(f32[11,8,128]{2,1,0:T(8,128)S(1)} %get-tuple-element.82), channel_id=1, source_target_pairs={{0,15},{1,2},{2,1},{3,4},{4,3},{5,6},{6,5},{7,8},{8,7},{9,10},{10,... | collective-permute-start | bytes 135176 | tf_op jit(solution)/shard_map/ppermute | solution.py:556
  44.8 4.9 %collective-permute-start.8 = (f32[3,3,8,128]{3,2,1,0:T(8,128)S(1)}, f32[3,3,8,128]{3,2,1,0:T(8,128)S(1)}, u32[]{:S(2)}, u32[]{:S(2)}) collective-permute-start(f32[3,3,8,128]{3,2,1,0:T(8,128)S(1)} %get-tuple-element.90), channel_id=1, source_target_pairs={{0,16},{16,0},{32,48},{48,32},{64,80},{80,64},{96,112},{112,96},{1... | collective-permute-start | bytes 110600 | tf_op jit(solution)/shard_map/ppermute | solution.py:556
  48.8 7.3 %collective-permute-start.9 = (f32[3,3,8,128]{3,2,1,0:T(8,128)S(1)}, f32[3,3,8,128]{3,2,1,0:T(8,128)S(1)}, u32[]{:S(2)}, u32[]{:S(2)}) collective-permute-start(f32[3,3,8,128]{3,2,1,0:T(8,128)S(1)} %get-tuple-element.91), channel_id=1, source_target_pairs={{0,240},{16,32},{32,16},{48,64},{64,48},{80,96},{96,80},{112,128},... | collective-permute-start | bytes 110600 | tf_op jit(solution)/shard_map/ppermute | solution.py:556
  56.1 3.5 %collective-permute-start.10 = (f32[3,8,128]{2,1,0:T(8,128)S(1)}, f32[3,8,128]{2,1,0:T(8,128)S(1)}, u32[]{:S(2)}, u32[]{:S(2)}) collective-permute-start(f32[3,8,128]{2,1,0:T(8,128)S(1)} %get-tuple-element.93), channel_id=1, source_target_pairs={{0,1},{1,0},{2,3},{3,2},{4,5},{5,4},{6,7},{7,6},{8,9},{9,8},{10,11... | collective-permute-start | bytes 36872 | tf_op jit(solution)/shard_map/ppermute | solution.py:556
  56.2 6.8 %collective-permute-start.11 = (f32[3,8,128]{2,1,0:T(8,128)S(1)}, f32[3,8,128]{2,1,0:T(8,128)S(1)}, u32[]{:S(2)}, u32[]{:S(2)}) collective-permute-start(f32[3,8,128]{2,1,0:T(8,128)S(1)} %get-tuple-element.94), channel_id=1, source_target_pairs={{0,15},{1,2},{2,1},{3,4},{4,3},{5,6},{6,5},{7,8},{8,7},{9,10},{10,... | collective-permute-start | bytes 36872 | tf_op jit(solution)/shard_map/ppermute | solution.py:556
  63.3 4.3 %collective-permute-start.12 = (f32[15,8,128]{2,1,0:T(8,128)S(1)}, f32[15,8,128]{2,1,0:T(8,128)S(1)}, u32[]{:S(2)}, u32[]{:S(2)}) collective-permute-start(f32[15,8,128]{2,1,0:T(8,128)S(1)} %get-tuple-element.97), channel_id=1, source_target_pairs={{0,16},{16,0},{32,48},{48,32},{64,80},{80,64},{96,112},{112,96},{1... | collective-permute-start | bytes 184328 | tf_op jit(solution)/shard_map/ppermute | solution.py:556
  66.7 7.6 %collective-permute-start.13 = (f32[15,8,128]{2,1,0:T(8,128)S(1)}, f32[15,8,128]{2,1,0:T(8,128)S(1)}, u32[]{:S(2)}, u32[]{:S(2)}) collective-permute-start(f32[15,8,128]{2,1,0:T(8,128)S(1)} %get-tuple-element.98), channel_id=1, source_target_pairs={{0,240},{16,32},{32,16},{48,64},{64,48},{80,96},{96,80},{112,128},... | collective-permute-start | bytes 184328 | tf_op jit(solution)/shard_map/ppermute | solution.py:556
  74.3 3.5 %collective-permute-start.14 = (f32[11,8,128]{2,1,0:T(8,128)S(1)}, f32[11,8,128]{2,1,0:T(8,128)S(1)}, u32[]{:S(2)}, u32[]{:S(2)}) collective-permute-start(f32[11,8,128]{2,1,0:T(8,128)S(1)} %get-tuple-element.102), channel_id=1, source_target_pairs={{0,1},{1,0},{2,3},{3,2},{4,5},{5,4},{6,7},{7,6},{8,9},{9,8},{10,11... | collective-permute-start | bytes 135176 | tf_op jit(solution)/shard_map/ppermute | solution.py:556
  74.4 7.2 %collective-permute-start.15 = (f32[11,8,128]{2,1,0:T(8,128)S(1)}, f32[11,8,128]{2,1,0:T(8,128)S(1)}, u32[]{:S(2)}, u32[]{:S(2)}) collective-permute-start(f32[11,8,128]{2,1,0:T(8,128)S(1)} %get-tuple-element.103), channel_id=1, source_target_pairs={{0,15},{1,2},{2,1},{3,4},{4,3},{5,6},{6,5},{7,8},{8,7},{9,10},{10,... | collective-permute-start | bytes 135176 | tf_op jit(solution)/shard_map/ppermute | solution.py:556
  84.9 4.0 %collective-permute-start.16 = (f32[3,3,8,128]{3,2,1,0:T(8,128)S(1)}, f32[3,3,8,128]{3,2,1,0:T(8,128)S(1)}, u32[]{:S(2)}, u32[]{:S(2)}) collective-permute-start(f32[3,3,8,128]{3,2,1,0:T(8,128)S(1)} %get-tuple-element.109), channel_id=1, source_target_pairs={{0,16},{16,0},{32,48},{48,32},{64,80},{80,64},{96,112},{112,96},{1... | collective-permute-start | bytes 110600 | tf_op jit(solution)/shard_map/ppermute | solution.py:556
  88.0 7.4 %collective-permute-start.17 = (f32[3,3,8,128]{3,2,1,0:T(8,128)S(1)}, f32[3,3,8,128]{3,2,1,0:T(8,128)S(1)}, u32[]{:S(2)}, u32[]{:S(2)}) collective-permute-start(f32[3,3,8,128]{3,2,1,0:T(8,128)S(1)} %get-tuple-element.110), channel_id=1, source_target_pairs={{0,240},{16,32},{32,16},{48,64},{64,48},{80,96},{96,80},{112,128},... | collective-permute-start | bytes 110600 | tf_op jit(solution)/shard_map/ppermute | solution.py:556
  95.4 3.3 %collective-permute-start.18 = (f32[3,8,128]{2,1,0:T(8,128)S(1)}, f32[3,8,128]{2,1,0:T(8,128)S(1)}, u32[]{:S(2)}, u32[]{:S(2)}) collective-permute-start(f32[3,8,128]{2,1,0:T(8,128)S(1)} %get-tuple-element.112), channel_id=1, source_target_pairs={{0,1},{1,0},{2,3},{3,2},{4,5},{5,4},{6,7},{7,6},{8,9},{9,8},{10,11... | collective-permute-start | bytes 36872 | tf_op jit(solution)/shard_map/ppermute | solution.py:556
  95.5 6.6 %collective-permute-start.19 = (f32[3,8,128]{2,1,0:T(8,128)S(1)}, f32[3,8,128]{2,1,0:T(8,128)S(1)}, u32[]{:S(2)}, u32[]{:S(2)}) collective-permute-start(f32[3,8,128]{2,1,0:T(8,128)S(1)} %get-tuple-element.113), channel_id=1, source_target_pairs={{0,15},{1,2},{2,1},{3,4},{4,3},{5,6},{6,5},{7,8},{8,7},{9,10},{10,... | collective-permute-start | bytes 36872 | tf_op jit(solution)/shard_map/ppermute | solution.py:556
  102.4 4.2 %collective-permute-start.20 = (f32[15,8,128]{2,1,0:T(8,128)S(1)}, f32[15,8,128]{2,1,0:T(8,128)S(1)}, u32[]{:S(2)}, u32[]{:S(2)}) collective-permute-start(f32[15,8,128]{2,1,0:T(8,128)S(1)} %get-tuple-element.116), channel_id=1, source_target_pairs={{0,16},{16,0},{32,48},{48,32},{64,80},{80,64},{96,112},{112,96},{1... | collective-permute-start | bytes 184328 | tf_op jit(solution)/shard_map/ppermute | solution.py:556
  105.7 7.6 %collective-permute-start.21 = (f32[15,8,128]{2,1,0:T(8,128)S(1)}, f32[15,8,128]{2,1,0:T(8,128)S(1)}, u32[]{:S(2)}, u32[]{:S(2)}) collective-permute-start(f32[15,8,128]{2,1,0:T(8,128)S(1)} %get-tuple-element.117), channel_id=1, source_target_pairs={{0,240},{16,32},{32,16},{48,64},{64,48},{80,96},{96,80},{112,128},... | collective-permute-start | bytes 184328 | tf_op jit(solution)/shard_map/ppermute | solution.py:556
  113.4 3.6 %collective-permute-start.22 = (f32[11,8,128]{2,1,0:T(8,128)S(1)}, f32[11,8,128]{2,1,0:T(8,128)S(1)}, u32[]{:S(2)}, u32[]{:S(2)}) collective-permute-start(f32[11,8,128]{2,1,0:T(8,128)S(1)} %get-tuple-element.121), channel_id=1, source_target_pairs={{0,1},{1,0},{2,3},{3,2},{4,5},{5,4},{6,7},{7,6},{8,9},{9,8},{10,11... | collective-permute-start | bytes 135176 | tf_op jit(solution)/shard_map/ppermute | solution.py:556
  113.5 7.2 %collective-permute-start.23 = (f32[11,8,128]{2,1,0:T(8,128)S(1)}, f32[11,8,128]{2,1,0:T(8,128)S(1)}, u32[]{:S(2)}, u32[]{:S(2)}) collective-permute-start(f32[11,8,128]{2,1,0:T(8,128)S(1)} %get-tuple-element.122), channel_id=1, source_target_pairs={{0,15},{1,2},{2,1},{3,4},{4,3},{5,6},{6,5},{7,8},{8,7},{9,10},{10,... | collective-permute-start | bytes 135176 | tf_op jit(solution)/shard_map/ppermute | solution.py:556

commit v4 on v3

--- a/solution.py
+++ b/solution.py
@@ -41,6 +41,7 @@
 DOWN_X = [q for q in range(19) if VELOCITIES[q][0] == -1]
 UP_Y = [q for q in range(19) if VELOCITIES[q][1] == 1]
 DOWN_Y = [q for q in range(19) if VELOCITIES[q][1] == -1]
+FLAT_X = [q for q in range(19) if VELOCITIES[q][0] == 0]
 X_ORDER = [0, 1, 2, 3, 4, 5, -1]
 MAIN_ROWS = 3 * 7 * 8
 RIM_ROWS = 3 * 3 * 8
@@ -152,20 +153,14 @@
     rim_ref[...] = grid[MAIN_ROWS:].reshape(3, 3, 8, CZ)
 
 
-def spread_messages(info_ref, main_ref, rim_ref, first_ref, second_ref):
-    even = info_ref[0] == 0.0
-    zero = jnp.zeros((2, CZ), F32)
+def spread_messages(info_ref, rim_ref, first_ref, second_ref):
+    even = info_ref[1] == 0.0
     for a in range(3):
-        up_rows, down_rows = [], []
-        for n in range(3):
-            rim = rim_ref[a, n]
-            up_rows.append(rim[4:6])
-            down_rows.append(rim[6:8])
-        ups = [main_ref[a, 4], main_ref[a, 5], jnp.concatenate(up_rows + [zero], axis=0)]
-        downs = [main_ref[a, 6], main_ref[a, 6], jnp.concatenate(down_rows + [zero], axis=0)]
-        for t in range(3):
-            first_ref[a, t] = choose(even, ups[t], downs[t])
-            second_ref[a, t] = choose(even, downs[t], ups[t])
+        down = rim_ref[a, 2]
+        for n in range(2):
+            up = rim_ref[a, n]
+            first_ref[a, n] = choose(even, up, down)
+            second_ref[a, n] = choose(even, down, up)
 
 
 def incidence_kernel(triangles_ref, incidence_ref):
@@ -176,54 +171,40 @@
 
 
 def spread_kernel(
-    stiffness_ref, occupied_ref, offset_in, rest_in, base_in, populations_in, solid_in, incidence_ref,
-    main_ref, rim_ref, first_ref, second_ref, plane_ref, depth_ref,
-    offset_ref, rest_ref, base_ref, populations_ref, solid_ref, info_ref, terms,
+    info_ref, offset_in, rest_in, base_in, incidence_ref,
+    main_ref, first_ref, second_ref, plane_ref, depth_ref, offset_ref, rest_ref, base_ref, rim_ref, terms,
 ):
-    place_x = lax.axis_index("gx")
-    place_y = lax.axis_index("gy")
-    even_row = lax.rem(tile_rows(), 2) == 0
-
-    def by_slot(row):
-        return jnp.where(even_row, row[:, 0:1], row[:, 1:2])
-
-    held = by_slot(occupied_ref[...].astype(F32))
-    info_ref[4] = by_slot(stiffness_ref[...]) * held
-    info_ref[5] = held
-    numbers = (lax.rem(place_x, 2), lax.rem(place_y, 2), place_x * CX, place_y * CY)
-    for n, number in enumerate(numbers):
-        info_ref[n] = jnp.full(TILE, number, jnp.int32).astype(F32)
     offset_ref[...] = six_rows(offset_in)
     rest_ref[...] = six_rows(rest_in)
     base_ref[...] = own_base(info_ref, base_in)
-    populations_ref[...] = populations_in[...]
-    solid_ref[...] = solid_in[...]
     spread(
         offset_ref[...], rest_ref[...], wide(info_ref[4]), base_ref[...],
         incidence_ref, terms, main_ref, rim_ref, plane_ref, depth_ref,
     )
-    spread_messages(info_ref, main_ref, rim_ref, first_ref, second_ref)
-
-
-def force_corner_kernel(info_ref, rim_ref, first_in, second_in, first_ref, second_ref):
+    spread_messages(info_ref, rim_ref, first_ref, second_ref)
+
+
+def force_kernel(info_ref, main_ref, first_y, second_y, whole_ref, first_ref, second_ref):
     even_x = info_ref[0] == 0.0
     even_y = info_ref[1] == 0.0
     rows = tile_rows()
     for a in range(3):
-        above = choose(even_x, first_in[a, 2], second_in[a, 2])
-        below = choose(even_x, second_in[a, 2], first_in[a, 2])
-        whole = []
-        for n in range(3):
-            from_below = below[2 * n : 2 * n + 2]
-            from_above = above[2 * n : 2 * n + 1]
-            part = rim_ref[a, n][:4]
-            whole.append(
-                jnp.concatenate([part[0:2] + from_below, part[2:3], part[3:4] + from_above], axis=0)
+        below = [choose(even_y, second_y[a, n], first_y[a, n]) for n in range(2)]
+        above = choose(even_y, first_y[a, 0], second_y[a, 0])
+        tiles = []
+        for n in range(7):
+            added = jnp.where(
+                rows == 0,
+                row_of(below[0], n),
+                jnp.where(rows == 1, row_of(below[1], n), jnp.where(rows == 7, row_of(above, n), 0.0)),
             )
-        up = jnp.concatenate([whole[0], whole[1]], axis=0)
-        down = jnp.concatenate([whole[2], whole[2]], axis=0)
-        first_ref[a] = choose(even_y, up, down)
-        second_ref[a] = choose(even_y, down, up)
+            tiles.append(main_ref[a, n] + added)
+            whole_ref[a, n] = tiles[n]
+        ups = [tiles[2], tiles[3], tiles[4], tiles[5]]
+        downs = [tiles[6], tiles[0], tiles[1], tiles[2]]
+        for t in range(4):
+            first_ref[a, t] = choose(even_x, ups[t], downs[t])
+            second_ref[a, t] = choose(even_x, downs[t], ups[t])
 
 
 def moment_sums(members, rows):
@@ -261,126 +242,195 @@
     return [jnp.where(keep, t, 0.0) for t in tiles]
 
 
-def collide_kernel(
-    info_ref, populations_ref, solid_ref, main_ref, first_x, second_x, first_y, second_y,
-    stepped_ref, force_ref, first_ref, second_ref,
-):
+def push(tile, q):
+    vector = VELOCITIES[q]
+    if vector[2] != 0:
+        tile = pltpu.roll(tile, vector[2] % CZ, 1)
+    if vector[1] != 0:
+        tile = pltpu.roll(tile, vector[1] % 8, 0)
+    return tile
+
+
+def momentum(current, a):
+    total = None
+    for q in range(19):
+        if VELOCITIES[q][a] != 0:
+            term = current[q] if VELOCITIES[q][a] == 1 else -current[q]
+            total = term if total is None else total + term
+    return total
+
+
+def gained(density, carried, force, directions):
+    inverse = 1.0 / density
+    return gained_from(density, [(0.5 * force[a] + carried[a]) * inverse for a in range(3)], force, directions)
+
+
+def gained_from(density, velocity, force, directions):
+    squared = velocity[0] * velocity[0] + velocity[1] * velocity[1] + velocity[2] * velocity[2]
+    working = velocity[0] * force[0] + velocity[1] * force[1] + velocity[2] * force[2]
+    common = 1.0 - 1.5 * squared
+    factor = 1.0 - 0.5 / RELAX
+    out = {}
+    for q in directions:
+        vector = VELOCITIES[q]
+        w = LATTICE_WEIGHTS[q]
+        if q == 0:
+            out[q] = (w / RELAX) * density * common - (3.0 * factor * w) * working
+            continue
+        along, pushed = None, None
+        for a in range(3):
+            if vector[a] == 0:
+                continue
+            u = velocity[a] if vector[a] == 1 else -velocity[a]
+            f = force[a] if vector[a] == 1 else -force[a]
+            along = u if along is None else along + u
+            pushed = f if pushed is None else pushed + f
+        equilibrium = (w / RELAX) * density * (common + along * (3.0 + 4.5 * along))
+        source = (factor * w) * (3.0 * (pushed - working) + 9.0 * along * pushed)
+        out[q] = equilibrium + source
+    return out
+
+
+def kept(current, walled, q):
+    return jnp.where(walled, current[OPPOSITE[q]], (1.0 - 1.0 / RELAX) * current[q])
+
+
+def halo_messages(info_ref, populations_ref, solid_ref, first_ref, second_ref):
     even_x = info_ref[0] == 0.0
-    even_y = info_ref[1] == 0.0
     rows = tile_rows()
-    for x in range(4):
-        force = []
-        for a in range(3):
-            f = main_ref[a, x]
-            if x < 2:
-                f = f + choose(even_x, second_x[a, x], first_x[a, x])
-            if x == 3:
-                f = f + choose(even_x, first_x[a, 0], second_x[a, 0])
-            below = choose(even_y, second_y[a], first_y[a])
-            above = choose(even_y, first_y[a], second_y[a])
-            f = f + jnp.where(
-                rows == 0,
-                row_of(below, x),
-                jnp.where(rows == 1, row_of(below, 4 + x), jnp.where(rows == 7, row_of(above, x), 0.0)),
-            )
-            force_ref[a, x] = f
-            force.append(f)
-        current = [populations_ref[q, x] for q in range(19)]
-        density = functools.reduce(lambda u, v: u + v, current)
-        velocity = []
-        for a in range(3):
-            moving = force[a] * 0.5
-            for q in range(19):
-                if VELOCITIES[q][a] == 1:
-                    moving = moving + current[q]
-                elif VELOCITIES[q][a] == -1:
-                    moving = moving - current[q]
-            velocity.append(moving)
-        inverse = 1.0 / density
-        velocity = [m * inverse for m in velocity]
-        squared = velocity[0] * velocity[0] + velocity[1] * velocity[1] + velocity[2] * velocity[2]
-        working = velocity[0] * force[0] + velocity[1] * force[1] + velocity[2] * force[2]
-        walled = solid_ref[x] != 0
-        common = 1.0 - 1.5 * squared
-        factor = 1.0 - 0.5 / RELAX
-        for q in range(19):
-            vector = VELOCITIES[q]
-            w = LATTICE_WEIGHTS[q]
-            if q == 0:
-                equilibrium = w * density * common
-                source = (-3.0 * factor * w) * working
-            else:
-                along, pushed = None, None
-                for a in range(3):
-                    if vector[a] == 0:
-                        continue
-                    u = velocity[a] if vector[a] == 1 else -velocity[a]
-                    f = force[a] if vector[a] == 1 else -force[a]
-                    along = u if along is None else along + u
-                    pushed = f if pushed is None else pushed + f
-                equilibrium = w * density * (common + along * (3.0 + 4.5 * along))
-                source = (factor * w) * (3.0 * (pushed - working) + 9.0 * along * pushed)
-            updated = current[q] - (current[q] - equilibrium) / RELAX + source
-            relaxed = jnp.where(walled, current[OPPOSITE[q]], updated)
-            if vector[2] != 0:
-                relaxed = pltpu.roll(relaxed, vector[2] % CZ, 1)
-            if vector[1] != 0:
-                relaxed = pltpu.roll(relaxed, vector[1] % 8, 0)
-            stepped_ref[q, (x + vector[0]) % 4] = relaxed
-    messages = []
-    for crossing, lines in ((UP_X, (3,)), (DOWN_X, (0, 1))):
-        slot = 0 if crossing is UP_X else 3
-        tiles = [stepped_ref[q, slot] for q in crossing]
-        for x in lines:
-            members = [
-                (q, stepped_ref[q, x])
-                for q in range(19)
-                if not (x == 0 and VELOCITIES[q][0] == 1) and not (x == 3 and VELOCITIES[q][0] == -1)
-            ]
-            inside, edge = moment_sums(members, rows)
-            for k in range(3):
-                inside[1 + k] = inside[1 + k] + 0.5 * force_ref[k, x]
-            tiles += inside + [pack_edges(edge)]
-        messages.append(tiles)
-    up, down = messages
-    for t in range(15):
-        u = up[t] if t < len(up) else down[t]
+    current = [[populations_ref[q, x] for q in range(19)] for x in range(4)]
+    walled = [solid_ref[x] != 0 for x in range(4)]
+
+    def state(x):
+        density = functools.reduce(lambda u, v: u + v, current[x])
+        tiles = [density] + [momentum(current[x], a) for a in range(3)]
+        return [jnp.where(walled[x], 0.0, t) for t in tiles]
+
+    def carried(x, directions):
+        return [(q, push(kept(current[x], walled[x], q), q)) for q in directions]
+
+    def sums(members):
+        inside, edge = moment_sums(members, rows)
+        return inside + [pack_edges(edge)]
+
+    up = state(2) + state(3)
+    up += sums(carried(2, UP_X) + carried(3, FLAT_X))
+    up += [t for _, t in carried(3, UP_X)]
+    down = state(0) + state(1) + state(2)
+    down += sums(carried(0, FLAT_X) + carried(1, DOWN_X))
+    down += sums(carried(0, UP_X) + carried(1, FLAT_X) + carried(2, DOWN_X))
+    down += [t for _, t in carried(0, DOWN_X)]
+    for t in range(27):
+        u = up[t] if t < 18 else down[t]
         first_ref[t] = choose(even_x, u, down[t])
         second_ref[t] = choose(even_x, down[t], u)
 
 
-def flow_corner_kernel(
-    info_ref, stepped_in, force_ref, first_x, second_x,
+def halo_kernel(
+    stiffness_ref, occupied_ref, populations_in, solid_in,
+    info_ref, populations_ref, solid_ref, first_ref, second_ref,
+):
+    place_x = lax.axis_index("gx")
+    place_y = lax.axis_index("gy")
+    even_row = lax.rem(tile_rows(), 2) == 0
+
+    def by_slot(row):
+        return jnp.where(even_row, row[:, 0:1], row[:, 1:2])
+
+    held = by_slot(occupied_ref[...].astype(F32))
+    info_ref[4] = by_slot(stiffness_ref[...]) * held
+    info_ref[5] = held
+    numbers = (lax.rem(place_x, 2), lax.rem(place_y, 2), place_x * CX, place_y * CY)
+    for n, number in enumerate(numbers):
+        info_ref[n] = jnp.full(TILE, number, jnp.int32).astype(F32)
+    populations_ref[...] = populations_in[...]
+    solid_ref[...] = solid_in[...]
+    halo_messages(info_ref, populations_ref, solid_ref, first_ref, second_ref)
+
+
+def collide_kernel(
+    info_ref, populations_ref, solid_ref, whole_ref, first_x, second_x, first_h, second_h,
     stepped_ref, inside_ref, leaving_ref, first_ref, second_ref, edges, up_tiles, down_tiles,
 ):
     even_x = info_ref[0] == 0.0
     even_y = info_ref[1] == 0.0
     rows = tile_rows()
-    below = [choose(even_x, second_x[t], first_x[t]) for t in range(10)]
-    above = [choose(even_x, first_x[t], second_x[t]) for t in range(15)]
-    out_up = [(q, stepped_in[q, 0]) for q in UP_X]
-    out_down = [(q, stepped_in[q, 3]) for q in DOWN_X]
-    for q in range(19):
-        for x in range(4):
-            s = stepped_in[q, x]
-            if q in UP_X and x == 0:
-                s = below[UP_X.index(q)]
-            if q in DOWN_X and x == 3:
-                s = above[DOWN_X.index(q)]
-            stepped_ref[(q * 4 + x) * 8 : (q * 4 + x + 1) * 8, :] = s
+    below = [choose(even_x, second_h[t], first_h[t]) for t in range(18)]
+    above = [choose(even_x, first_h[t], second_h[t]) for t in range(27)]
+    from_below = [[choose(even_x, second_x[a, t], first_x[a, t]) for t in range(4)] for a in range(3)]
+    from_above = [[choose(even_x, first_x[a, t], second_x[a, t]) for t in range(4)] for a in range(3)]
+    force = {}
+    for x in range(-2, 7):
+        parts = []
+        for a in range(3):
+            terms = []
+            if -1 <= x <= 5:
+                terms.append(whole_ref[a, X_ORDER.index(x)])
+            if x < 2:
+                terms.append(from_below[a][x + 2])
+            if x > 2:
+                terms.append(from_above[a][x - 3])
+            parts.append(functools.reduce(lambda u, v: u + v, terms))
+        force[x] = parts
+
+    def place(q, x, tile):
+        stepped_ref[(q * 4 + x) * 8 : (q * 4 + x + 1) * 8, :] = tile
+
+    out_up, out_down = [], []
+    for x in range(4):
+        current = [populations_ref[q, x] for q in range(19)]
+        walled = solid_ref[x] != 0
+        density = functools.reduce(lambda u, v: u + v, current)
+        new = gained(density, [momentum(current, a) for a in range(3)], force[x], range(19))
+        for q in range(19):
+            relaxed = jnp.where(walled, current[OPPOSITE[q]], (1.0 - 1.0 / RELAX) * current[q] + new[q])
+            relaxed = push(relaxed, q)
+            target = x + VELOCITIES[q][0]
+            if target == 4:
+                out_up.append((q, relaxed))
+            elif target == -1:
+                out_down.append((q, relaxed))
+            else:
+                place(q, target, relaxed)
+
+    def halo(x, tiles, directions):
+        fluid = tiles[0] != 0.0
+        pulled = [jnp.where(fluid, f, 0.0) for f in force[x]]
+        density = tiles[0]
+        inverse = 1.0 / jnp.where(fluid, density, 1.0)
+        velocity = [(0.5 * pulled[a] + tiles[1 + a]) * inverse for a in range(3)]
+        new = gained_from(density, velocity, pulled, directions)
+        return {q: push(new[q], q) for q in directions}
+
+    def members(part, directions):
+        return [(q, part[q]) for q in directions]
+
+    before = halo(-2, below[0:4], UP_X)
+    last = halo(-1, below[4:8], FLAT_X + UP_X)
+    for n, q in enumerate(UP_X):
+        place(q, 0, below[13 + n] + last[q])
+    reached = {-1: (below[8:13], members(before, UP_X) + members(last, FLAT_X) + out_down)}
+    four = halo(4, above[0:4], range(19))
+    five = halo(5, above[4:8], FLAT_X + DOWN_X)
+    six = halo(6, above[8:12], DOWN_X)
+    for n, q in enumerate(DOWN_X):
+        place(q, 3, above[22 + n] + four[q])
+    reached[4] = (above[12:17], members(four, FLAT_X) + members(five, DOWN_X) + out_up)
+    reached[5] = (
+        above[17:22],
+        members(four, UP_X) + members(five, FLAT_X) + members(six, DOWN_X),
+    )
     for n, x in enumerate(X_ORDER):
         if 0 <= x < 4:
-            members = [(q, stepped_ref[(q * 4 + x) * 8 : (q * 4 + x + 1) * 8, :]) for q in range(19)]
-            inside, edge = moment_sums(members, rows)
-            for k in range(3):
-                inside[1 + k] = inside[1 + k] + 0.5 * force_ref[k, x]
+            every = [(q, stepped_ref[(q * 4 + x) * 8 : (q * 4 + x + 1) * 8, :]) for q in range(19)]
+            inside, edge = moment_sums(every, rows)
         else:
-            received = below[5:10] if x == -1 else above[5 + 5 * (x - 4) : 10 + 5 * (x - 4)]
-            inside, edge = received[:4], unpack_edges(received[4], rows)
-            if x != 5:
-                own_inside, own_edge = moment_sums(out_down if x == -1 else out_up, rows)
-                inside = [u + v for u, v in zip(inside, own_inside)]
-                edge = [u + v for u, v in zip(edge, own_edge)]
+            received, arrived = reached[x]
+            inside, edge = moment_sums(arrived, rows)
+            inside = [u + v for u, v in zip(inside, received[:4])]
+            edge = [u + v for u, v in zip(edge, unpack_edges(received[4], rows))]
+        for k in range(3):
+            inside[1 + k] = inside[1 + k] + 0.5 * force[x][k]
         for k in range(4):
             inside_ref[(k * 8 + n) * 8 : (k * 8 + n + 1) * 8, :] = inside[k]
         for k in range(3):
@@ -504,19 +554,25 @@
     return offset + live * stacked
 
 
+def finish_kernel(
+    info_ref, stepped_ref, inside_ref, leaving_ref, first_y, second_y, solid_ref,
+    out_ref, flow_ref, first_ref, second_ref,
+):
+    finish_fluid(info_ref, stepped_ref, inside_ref, leaving_ref, first_y, second_y, out_ref, flow_ref)
+    halo_messages(info_ref, out_ref, solid_ref, first_ref, second_ref)
+
+
 def next_kernel(
-    info_ref, stepped_ref, inside_ref, leaving_ref, first_y, second_y, plane_in, depth_in,
-    offset_ref, rest_ref, base_ref, incidence_ref,
-    out_ref, offset_out, main_ref, rim_ref, first_ref, second_ref, plane_ref, depth_ref, flow, terms,
+    info_ref, flow_ref, plane_in, depth_in, offset_ref, rest_ref, base_ref, incidence_ref,
+    main_ref, first_ref, second_ref, plane_ref, depth_ref, offset_out, rim_ref, terms,
 ):
-    finish_fluid(info_ref, stepped_ref, inside_ref, leaving_ref, first_y, second_y, out_ref, flow)
-    offset = sample(offset_ref[...], wide(info_ref[5]), plane_in, depth_in, flow)
+    offset = sample(offset_ref[...], wide(info_ref[5]), plane_in, depth_in, flow_ref)
     offset_out[...] = offset
     spread(
         offset, rest_ref[...], wide(info_ref[4]), base_ref[...],
         incidence_ref, terms, main_ref, rim_ref, plane_ref, depth_ref,
     )
-    spread_messages(info_ref, main_ref, rim_ref, first_ref, second_ref)
+    spread_messages(info_ref, rim_ref, first_ref, second_ref)
 
 
 def last_kernel(
@@ -559,59 +615,61 @@
 
 SPREAD_OUT = [
     ((3, 7, 8, CZ), F32),
-    ((3, 3, 8, CZ), F32),
-    ((3, 3, 8, CZ), F32),
-    ((3, 3, 8, CZ), F32),
+    ((3, 2, 8, CZ), F32),
+    ((3, 2, 8, CZ), F32),
     ((SLOTS, 3, 8, PAD), F32),
     ((SLOTS, 2, CZ, PAD), jnp.bfloat16),
 ]
+HALO_OUT = [((27, 8, CZ), F32)] * 2
 STEPPED = ((19, 4, 8, CZ), F32)
 
 
 def steps(populations, solid, base_cell, offset, rest_displacement, stiffness, occupied, triangles):
     stored = (3, SLOTS, PAD)
     rows = (8, PAD)
-    terms = ((TABLE_ROWS, PAD), F32)
-    flow = ((TABLE_ROWS, CZ), F32)
+    scratch = [((3, 3, 8, CZ), F32), ((TABLE_ROWS, PAD), F32)]
+    flow_out = ((TABLE_ROWS, CZ), F32)
     corners = triangles.T
     (incidence,) = call(incidence_kernel, [((PAD, corners.shape[1]), jnp.bfloat16)], [], corners)
-    main, rim, first, second, plane, depth, where, rest, base, populations, solid, info = call(
-        spread_kernel,
-        SPREAD_OUT
-        + [(rows, F32), (rows, F32), (rows, jnp.int32), STEPPED, (solid.shape, jnp.int32), ((6, 8, CZ), F32)],
-        [terms],
-        stiffness.reshape(1, SLOTS), occupied.reshape(1, SLOTS), offset.reshape(stored), rest_displacement.reshape(stored), base_cell.reshape(stored),
-        populations, solid, incidence,
+    info, populations, solid, first_h, second_h = call(
+        halo_kernel,
+        [((6, 8, CZ), F32), STEPPED, (solid.shape, jnp.int32)] + HALO_OUT, [],
+        stiffness.reshape(1, SLOTS), occupied.reshape(1, SLOTS), populations, solid,
+    )
+    main, first, second, plane, depth, where, rest, base = call(
+        spread_kernel, SPREAD_OUT + [(rows, F32), (rows, F32), (rows, jnp.int32)], scratch,
+        info, offset.reshape(stored), rest_displacement.reshape(stored), base_cell.reshape(stored),
+        incidence,
     )
     for substep in range(SUBSTEPS):
-        first_x, second_x = exchange(first, second, "gx")
-        corner = call(force_corner_kernel, [((3, 8, CZ), F32)] * 2, [], info, rim, first_x, second_x)
-        first_y, second_y = exchange(*corner, "gy")
-        stepped, force, first, second = call(
+        first_h, second_h = exchange(first_h, second_h, "gx")
+        first, second = exchange(first, second, "gy")
+        whole, first, second = call(
+            force_kernel, [((3, 7, 8, CZ), F32), ((3, 4, 8, CZ), F32), ((3, 4, 8, CZ), F32)], [],
+            info, main, first, second,
+        )
+        first, second = exchange(first, second, "gx")
+        stepped, inside, leaving, first, second = call(
             collide_kernel,
-            [STEPPED, ((3, 4, 8, CZ), F32), ((15, 8, CZ), F32), ((15, 8, CZ), F32)],
-            [],
-            info, populations, solid, main, first_x, second_x, first_y, second_y,
-        )
-        first_x, second_x = exchange(first, second, "gx")
-        stepped, inside, leaving, first, second = call(
-            flow_corner_kernel,
             [
                 ((19 * 4 * 8, CZ), F32), ((4 * 8 * 8, CZ), F32), ((6, 8, CZ), F32),
                 ((11, 8, CZ), F32), ((11, 8, CZ), F32),
             ],
             [((3 * 8 * 8, CZ), F32), ((8, 8, CZ), F32), ((11, 8, CZ), F32)],
-            info, stepped, force, first_x, second_x,
+            info, populations, solid, whole, first, second, first_h, second_h,
         )
-        first_y, second_y = exchange(first, second, "gy")
-        fluid = (info, stepped, inside, leaving, first_y, second_y, plane, depth)
+        first, second = exchange(first, second, "gy")
+        fluid = (info, stepped, inside, leaving, first, second)
         if substep < SUBSTEPS - 1:
-            populations, where, main, rim, first, second, plane, depth = call(
-                next_kernel, [STEPPED, (rows, F32)] + SPREAD_OUT, [flow, terms],
-                *fluid, where, rest, base, incidence,
+            populations, flow, first_h, second_h = call(
+                finish_kernel, [STEPPED, flow_out] + HALO_OUT, [], *fluid, solid
+            )
+            main, first, second, plane, depth, where = call(
+                next_kernel, SPREAD_OUT + [(rows, F32)], scratch,
+                info, flow, plane, depth, where, rest, base, incidence,
             )
         else:
-            populations, where = call(last_kernel, [STEPPED, (stored, F32)], [flow], *fluid, where)
+            populations, where = call(last_kernel, [STEPPED, (stored, F32)], [flow_out], *fluid, plane, depth, where)
     return populations, where.reshape(offset.shape)
 
 

time: 122 us -> 110 us (0.902)
  waiting for transfers between devices: 53.9 us -> 34.1 us
  starting transfers between devices: 54.6 us -> 58.1 us
  local copies, waits for them, and re-layouts: 0.79 us -> 3.72 us
    ppermute x24, waiting for transfers between devices: 53.9 us -> 34.1 us  [exchange(): out[kind] = lax.ppermute(message, axis, pairs)]
    ppermute x24, starting transfers between devices: 54.6 us -> 58.1 us  [exchange(): out[kind] = lax.ppermute(message, axis, pairs)]
    unnamed x16, local copies, waits for them, and re-layouts: 0.79 us -> 3.72 us
  transfers between devices with their start and end apart: 24 -> 24, of which waited for: 16 -> 11; matrix products, arithmetic and copies ran while one was open for 0% -> 0% of each run, Pallas kernels for 0% -> 8%
where the time goes in v4:
time: 110 us; the launch traced here: 109 us
  starting transfers between devices  58.1 us (53%)
  waiting for transfers between devices  34.1 us (31%)
  Pallas kernels  12.5 us (11%)
  local copies, waits for them, and re-layouts  3.72 us (3%)
    ppermute x24, starting transfers between devices, exchange(): out[kind] = lax.ppermute(message, axis, pairs)  58.1 us
    ppermute x24, waiting for transfers between devices, exchange(): out[kind] = lax.ppermute(message, axis, pairs)  34.1 us
    pallas_call x14, Pallas kernels, call(): pl.pallas_call(kernel, out_shape=[jax.ShapeDtypeStruct(shape, dtype) for...  12.5 us
    unnamed x16, local copies, waits for them, and re-layouts  3.72 us
  transfers between devices with their start and end apart: 24, of which 11 were waited for; matrix products, arithmetic and copies ran while one was open for 0% of the time, Pallas kernels for 8%

profile of v4, /device:TPU:1, one launch (start us, length us, event | category | flops | bytes accessed | tf_op | source)
XLA Modules:
  0.0 109.3 jit_solution(12880210283025723003)
XLA Ops:
  0.6 1.0 copy-done
  1.6 0.7 copy-done.5
  2.3 0.7 copy-done.6
  3.0 0.7 copy-done.7
  3.6 0.1 shard_map.95
  3.8 3.3 %collective-permute-start.4 = (f32[27,8,128]{2,1,0:T(8,128)S(1)}, f32[27,8,128]{2,1,0:T(8,128)S(1)}, u32[]{:S(2)}, u32[]{:S(2)}) collective-permute-start(f32[27,8,128]{2,1,0:T(8,128)S(1)} %get-tuple-element.70), channel_id=1, source_target_pairs={{0,16},{16,0},{32,48},{48,32},{64,80},{80,64},{96,112},{112,96},{1... | collective-permute-start | bytes 331784 | tf_op jit(solution)/shard_map/ppermute | solution.py:612
  7.1 5.2 %collective-permute-start.5 = (f32[27,8,128]{2,1,0:T(8,128)S(1)}, f32[27,8,128]{2,1,0:T(8,128)S(1)}, u32[]{:S(2)}, u32[]{:S(2)}) collective-permute-start(f32[27,8,128]{2,1,0:T(8,128)S(1)} %get-tuple-element.71), channel_id=1, source_target_pairs={{0,240},{16,32},{32,16},{48,64},{64,48},{80,96},{96,80},{112,128},... | collective-permute-start | bytes 331784 | tf_op jit(solution)/shard_map/ppermute | solution.py:612
  12.2 0.7 copy-done.1
  13.0 1.0 shard_map.96.incidence_ref
  14.0 1.8 %shard_map.97 = (f32[3,7,8,128]{3,2,1,0:T(8,128)S(1)}, f32[3,2,8,128]{3,2,1,0:T(8,128)S(1)}, f32[3,2,8,128]{3,2,1,0:T(8,128)S(1)}, f32[2,3,8,768]{3,2,1,0:T(8,12...) custom-call(f32[6,8,128]{2,1,0:T(8,128)S(1)} %get-tuple-element.61.i, ...), custom_call_target="tpu_custom_call" | custom-call | tf_op jit(solution)/shard_map/pallas_call | solution.py:592
  15.8 0.8 collective-permute-start
  16.6 3.8 %collective-permute-start.1 = (f32[3,2,8,128]{3,2,1,0:T(8,128)S(1)}, f32[3,2,8,128]{3,2,1,0:T(8,128)S(1)}, u32[]{:S(2)}, u32[]{:S(2)}) collective-permute-start(f32[3,2,8,128]{3,2,1,0:T(8,128)S(1)} %get-tuple-element.66), channel_id=1, source_target_pairs={{0,15},{1,2},{2,1},{3,4},{4,3},{5,6},{6,5},{7,8},{8,7},{9,10},{10,... | collective-permute-start | bytes 73736 | tf_op jit(solution)/shard_map/ppermute | solution.py:612
  20.5 0.0 collective-permute-done.first_y
  20.5 2.7 %collective-permute-done.1.second_y = f32[3,2,8,128]{3,2,1,0:T(8,128)S(1)} collective-permute-done((f32[3,2,8,128]{3,2,1,0:T(8,128)S(1)}, f32[3,2,8,128]{3,2,1,0:T(8,128)S(1)}, u32[]{:S(2)}, u32[]{:S(2)}) %collective-permute-start.1) | collective-permute-done | bytes 24608 | tf_op jit(solution)/shard_map/ppermute | solution.py:612
  23.3 4.4 %collective-permute-start.2 = (f32[3,4,8,128]{3,2,1,0:T(8,128)S(1)}, f32[3,4,8,128]{3,2,1,0:T(8,128)S(1)}, u32[]{:S(2)}, u32[]{:S(2)}) collective-permute-start(f32[3,4,8,128]{3,2,1,0:T(8,128)S(1)} %get-tuple-element.68), channel_id=1, source_target_pairs={{0,16},{16,0},{32,48},{48,32},{64,80},{80,64},{96,112},{112,96},{1... | collective-permute-start | bytes 147464 | tf_op jit(solution)/shard_map/ppermute | solution.py:612
  27.6 0.0 collective-permute-start.3
  27.6 0.9 collective-permute-done.2.first_x
  28.5 6.5 %collective-permute-done.3.second_x = f32[3,4,8,128]{3,2,1,0:T(8,128)S(1)} collective-permute-done((f32[3,4,8,128]{3,2,1,0:T(8,128)S(1)}, f32[3,4,8,128]{3,2,1,0:T(8,128)S(1)}, u32[]{:S(2)}, u32[]{:S(2)}) %collective-permute-start.3) | collective-permute-done | bytes 49184 | tf_op jit(solution)/shard_map/ppermute | solution.py:612
  35.1 0.0 collective-permute-done.4.first_h
  35.1 0.0 collective-permute-done.5.second_h
  35.1 0.5 shard_map.99
  35.6 0.1 collective-permute-start.6
  35.7 3.9 %collective-permute-start.7 = (f32[11,8,128]{2,1,0:T(8,128)S(1)}, f32[11,8,128]{2,1,0:T(8,128)S(1)}, u32[]{:S(2)}, u32[]{:S(2)}) collective-permute-start(f32[11,8,128]{2,1,0:T(8,128)S(1)} %get-tuple-element.76), channel_id=1, source_target_pairs={{0,15},{1,2},{2,1},{3,4},{4,3},{5,6},{6,5},{7,8},{8,7},{9,10},{10,... | collective-permute-start | bytes 135176 | tf_op jit(solution)/shard_map/ppermute | solution.py:612
  39.6 0.0 collective-permute-done.6.first_y
  39.6 3.1 %collective-permute-done.7.second_y = f32[11,8,128]{2,1,0:T(8,128)S(1)} collective-permute-done((f32[11,8,128]{2,1,0:T(8,128)S(1)}, f32[11,8,128]{2,1,0:T(8,128)S(1)}, u32[]{:S(2)}, u32[]{:S(2)}) %collective-permute-start.7) | collective-permute-done | bytes 45088 | tf_op jit(solution)/shard_map/ppermute | solution.py:612
  42.6 0.1 shard_map.100
  42.8 3.3 %collective-permute-start.12 = (f32[27,8,128]{2,1,0:T(8,128)S(1)}, f32[27,8,128]{2,1,0:T(8,128)S(1)}, u32[]{:S(2)}, u32[]{:S(2)}) collective-permute-start(f32[27,8,128]{2,1,0:T(8,128)S(1)} %get-tuple-element.90), channel_id=1, source_target_pairs={{0,16},{16,0},{32,48},{48,32},{64,80},{80,64},{96,112},{112,96},{1... | collective-permute-start | bytes 331784 | tf_op jit(solution)/shard_map/ppermute | solution.py:612
  46.1 0.0 collective-permute-start.13
  46.1 3.2 %shard_map.101 = (f32[3,7,8,128]{3,2,1,0:T(8,128)S(1)}, f32[3,2,8,128]{3,2,1,0:T(8,128)S(1)}, f32[3,2,8,128]{3,2,1,0:T(8,128)S(1)}, f32[2,3,8,768]{3,2,1,0:T(8,1...) custom-call(f32[6,8,128]{2,1,0:T(8,128)S(1)} %get-tuple-element.61.info_ref, ...), custom_call_target="tpu_custom_call" | custom-call | tf_op jit(solution)/shard_map/pallas_call | solution.py:592
  49.3 0.1 collective-permute-start.8
  49.4 4.2 %collective-permute-start.9 = (f32[3,2,8,128]{3,2,1,0:T(8,128)S(1)}, f32[3,2,8,128]{3,2,1,0:T(8,128)S(1)}, u32[]{:S(2)}, u32[]{:S(2)}) collective-permute-start(f32[3,2,8,128]{3,2,1,0:T(8,128)S(1)} %get-tuple-element.86), channel_id=1, source_target_pairs={{0,15},{1,2},{2,1},{3,4},{4,3},{5,6},{6,5},{7,8},{8,7},{9,10},{10,... | collective-permute-start | bytes 73736 | tf_op jit(solution)/shard_map/ppermute | solution.py:612
  53.7 0.0 collective-permute-done.8.first_y
  53.7 2.6 %collective-permute-done.9.second_y = f32[3,2,8,128]{3,2,1,0:T(8,128)S(1)} collective-permute-done((f32[3,2,8,128]{3,2,1,0:T(8,128)S(1)}, f32[3,2,8,128]{3,2,1,0:T(8,128)S(1)}, u32[]{:S(2)}, u32[]{:S(2)}) %collective-permute-start.9) | collective-permute-done | bytes 24608 | tf_op jit(solution)/shard_map/ppermute | solution.py:612
  56.3 1.3 %collective-permute-start.10 = (f32[3,4,8,128]{3,2,1,0:T(8,128)S(1)}, f32[3,4,8,128]{3,2,1,0:T(8,128)S(1)}, u32[]{:S(2)}, u32[]{:S(2)}) collective-permute-start(f32[3,4,8,128]{3,2,1,0:T(8,128)S(1)} %get-tuple-element.88), channel_id=1, source_target_pairs={{0,16},{16,0},{32,48},{48,32},{64,80},{80,64},{96,112},{112,96},{1... | collective-permute-start | bytes 147464 | tf_op jit(solution)/shard_map/ppermute | solution.py:612
  57.7 5.6 %collective-permute-start.11 = (f32[3,4,8,128]{3,2,1,0:T(8,128)S(1)}, f32[3,4,8,128]{3,2,1,0:T(8,128)S(1)}, u32[]{:S(2)}, u32[]{:S(2)}) collective-permute-start(f32[3,4,8,128]{3,2,1,0:T(8,128)S(1)} %get-tuple-element.89), channel_id=1, source_target_pairs={{0,240},{16,32},{32,16},{48,64},{64,48},{80,96},{96,80},{112,128},... | collective-permute-start | bytes 147464 | tf_op jit(solution)/shard_map/ppermute | solution.py:612
  63.3 0.0 collective-permute-done.10.first_x
  63.3 3.4 %collective-permute-done.11.second_x = f32[3,4,8,128]{3,2,1,0:T(8,128)S(1)} collective-permute-done((f32[3,4,8,128]{3,2,1,0:T(8,128)S(1)}, f32[3,4,8,128]{3,2,1,0:T(8,128)S(1)}, u32[]{:S(2)}, u32[]{:S(2)}) %collective-permute-start.11) | collective-permute-done | bytes 49184 | tf_op jit(solution)/shard_map/ppermute | solution.py:612
  66.7 0.0 collective-permute-done.12.first_h
  66.7 0.0 collective-permute-done.13.second_h
  66.7 0.5 shard_map.103
  67.2 0.1 collective-permute-start.14
  67.3 4.0 %collective-permute-start.15 = (f32[11,8,128]{2,1,0:T(8,128)S(1)}, f32[11,8,128]{2,1,0:T(8,128)S(1)}, u32[]{:S(2)}, u32[]{:S(2)}) collective-permute-start(f32[11,8,128]{2,1,0:T(8,128)S(1)} %get-tuple-element.96), channel_id=1, source_target_pairs={{0,15},{1,2},{2,1},{3,4},{4,3},{5,6},{6,5},{7,8},{8,7},{9,10},{10,... | collective-permute-start | bytes 135176 | tf_op jit(solution)/shard_map/ppermute | solution.py:612
  71.3 0.0 collective-permute-done.14.first_y
  71.3 2.9 %collective-permute-done.15.second_y = f32[11,8,128]{2,1,0:T(8,128)S(1)} collective-permute-done((f32[11,8,128]{2,1,0:T(8,128)S(1)}, f32[11,8,128]{2,1,0:T(8,128)S(1)}, u32[]{:S(2)}, u32[]{:S(2)}) %collective-permute-start.15) | collective-permute-done | bytes 45088 | tf_op jit(solution)/shard_map/ppermute | solution.py:612
  74.2 0.1 shard_map.104
  74.3 2.0 %collective-permute-start.20 = (f32[27,8,128]{2,1,0:T(8,128)S(1)}, f32[27,8,128]{2,1,0:T(8,128)S(1)}, u32[]{:S(2)}, u32[]{:S(2)}) collective-permute-start(f32[27,8,128]{2,1,0:T(8,128)S(1)} %get-tuple-element.108), channel_id=1, source_target_pairs={{0,16},{16,0},{32,48},{48,32},{64,80},{80,64},{96,112},{112,96},{1... | collective-permute-start | bytes 331784 | tf_op jit(solution)/shard_map/ppermute | solution.py:612
  76.3 3.7 %collective-permute-start.21 = (f32[27,8,128]{2,1,0:T(8,128)S(1)}, f32[27,8,128]{2,1,0:T(8,128)S(1)}, u32[]{:S(2)}, u32[]{:S(2)}) collective-permute-start(f32[27,8,128]{2,1,0:T(8,128)S(1)} %get-tuple-element.109), channel_id=1, source_target_pairs={{0,240},{16,32},{32,16},{48,64},{64,48},{80,96},{96,80},{112,128},... | collective-permute-start | bytes 331784 | tf_op jit(solution)/shard_map/ppermute | solution.py:612
  80.0 3.2 %shard_map.105 = (f32[3,7,8,128]{3,2,1,0:T(8,128)S(1)}, f32[3,2,8,128]{3,2,1,0:T(8,128)S(1)}, f32[3,2,8,128]{3,2,1,0:T(8,128)S(1)}, f32[2,3,8,768]{3,2,1,0:T(8,1...) custom-call(f32[6,8,128]{2,1,0:T(8,128)S(1)} %get-tuple-element.61.info_ref, ...), custom_call_target="tpu_custom_call" | custom-call | tf_op jit(solution)/shard_map/pallas_call | solution.py:592
  83.2 0.1 collective-permute-start.16
  83.3 4.2 %collective-permute-start.17 = (f32[3,2,8,128]{3,2,1,0:T(8,128)S(1)}, f32[3,2,8,128]{3,2,1,0:T(8,128)S(1)}, u32[]{:S(2)}, u32[]{:S(2)}) collective-permute-start(f32[3,2,8,128]{3,2,1,0:T(8,128)S(1)} %get-tuple-element.104), channel_id=1, source_target_pairs={{0,15},{1,2},{2,1},{3,4},{4,3},{5,6},{6,5},{7,8},{8,7},{9,10},{10,... | collective-permute-start | bytes 73736 | tf_op jit(solution)/shard_map/ppermute | solution.py:612
  87.5 0.0 collective-permute-done.16.first_y
  87.5 2.5 %collective-permute-done.17.second_y = f32[3,2,8,128]{3,2,1,0:T(8,128)S(1)} collective-permute-done((f32[3,2,8,128]{3,2,1,0:T(8,128)S(1)}, f32[3,2,8,128]{3,2,1,0:T(8,128)S(1)}, u32[]{:S(2)}, u32[]{:S(2)}) %collective-permute-start.17) | collective-permute-done | bytes 24608 | tf_op jit(solution)/shard_map/ppermute | solution.py:612
  90.0 2.9 %collective-permute-start.18 = (f32[3,4,8,128]{3,2,1,0:T(8,128)S(1)}, f32[3,4,8,128]{3,2,1,0:T(8,128)S(1)}, u32[]{:S(2)}, u32[]{:S(2)}) collective-permute-start(f32[3,4,8,128]{3,2,1,0:T(8,128)S(1)} %get-tuple-element.106), channel_id=1, source_target_pairs={{0,16},{16,0},{32,48},{48,32},{64,80},{80,64},{96,112},{112,96},{1... | collective-permute-start | bytes 147464 | tf_op jit(solution)/shard_map/ppermute | solution.py:612
  92.9 0.4 collective-permute-start.19
  93.3 0.5 collective-permute-done.18.first_x
  93.8 6.5 %collective-permute-done.19.second_x = f32[3,4,8,128]{3,2,1,0:T(8,128)S(1)} collective-permute-done((f32[3,4,8,128]{3,2,1,0:T(8,128)S(1)}, f32[3,4,8,128]{3,2,1,0:T(8,128)S(1)}, u32[]{:S(2)}, u32[]{:S(2)}) %collective-permute-start.19) | collective-permute-done | bytes 49184 | tf_op jit(solution)/shard_map/ppermute | solution.py:612
  100.4 0.0 collective-permute-done.20.first_h
  100.4 0.0 collective-permute-done.21.second_h
  100.4 0.5 shard_map.107
  100.9 0.1 collective-permute-start.22
  101.0 4.4 %collective-permute-start.23 = (f32[11,8,128]{2,1,0:T(8,128)S(1)}, f32[11,8,128]{2,1,0:T(8,128)S(1)}, u32[]{:S(2)}, u32[]{:S(2)}) collective-permute-start(f32[11,8,128]{2,1,0:T(8,128)S(1)} %get-tuple-element.114), channel_id=1, source_target_pairs={{0,15},{1,2},{2,1},{3,4},{4,3},{5,6},{6,5},{7,8},{8,7},{9,10},{10,... | collective-permute-start | bytes 135176 | tf_op jit(solution)/shard_map/ppermute | solution.py:612
  105.4 0.0 collective-permute-done.22.first_y
  105.4 2.4 %collective-permute-done.23.second_y = f32[11,8,128]{2,1,0:T(8,128)S(1)} collective-permute-done((f32[11,8,128]{2,1,0:T(8,128)S(1)}, f32[11,8,128]{2,1,0:T(8,128)S(1)}, u32[]{:S(2)}, u32[]{:S(2)}) %collective-permute-start.23) | collective-permute-done | bytes 45088 | tf_op jit(solution)/shard_map/ppermute | solution.py:612
  107.8 1.4 %shard_map.108 = (f32[19,4,8,128]{3,2,1,0:T(8,128)}, f32[3,2,768]{2,1,0:T(2,128)}) custom-call(f32[6,8,128]{2,1,0:T(8,128)S(1)} %get-tuple-element.61.info_ref, f32[608,128]{1,0:T(8,128)S(1)} %get-tuple-element.110.stepped_ref, f32[256,128]{1,0:T(8,128)S(1)} %get-tuple-element.111.inside_ref, f32[6,8,128]{2,1,0:T(8,128)S(1)} %get-tuple-element.112.leaving_ref, ...), custom_call_target="tpu_custom_call" | custom-call | tf_op jit(solution)/shard_map/pallas_call | solution.py:592
  (14 shorter events, 0.1 us)
Async XLA Ops:
  0.6 1.0 copy-start
  1.6 0.7 copy-start.5
  2.3 0.7 copy-start.6
  3.0 0.7 copy-start.7
  3.6 10.4 %copy-start.2 = (f32[3,1,1,2,768]{4,3,2,1,0:T(2,128)S(1)}, f32[3,1,1,2,768]{4,3,2,1,0:T(2,128)}, u32[]{:S(2)}) copy-start(f32[3,1,1,2,768]{4,3,2,1,0:T(2,128)} %param.11) | copy-start | bytes 55300
  3.6 10.4 %copy-start.3 = (f32[3,1,1,2,768]{4,3,2,1,0:T(2,128)S(1)}, f32[3,1,1,2,768]{4,3,2,1,0:T(2,128)}, u32[]{:S(2)}) copy-start(f32[3,1,1,2,768]{4,3,2,1,0:T(2,128)} %param.12) | copy-start | bytes 55300
  3.6 10.4 %copy-start.4 = (s32[3,1,1,2,768]{4,3,2,1,0:T(2,128)S(1)}, s32[3,1,1,2,768]{4,3,2,1,0:T(2,128)}, u32[]{:S(2)}) copy-start(s32[3,1,1,2,768]{4,3,2,1,0:T(2,128)} %param.10) | copy-start | bytes 55300
  3.8 31.3 %collective-permute-start.4 = (f32[27,8,128]{2,1,0:T(8,128)S(1)}, f32[27,8,128]{2,1,0:T(8,128)S(1)}, u32[]{:S(2)}, u32[]{:S(2)}) collective-permute-start(f32[27,8,128]{2,1,0:T(8,128)S(1)} %get-tuple-element.70), channel_id=1, source_target_pairs={{0,16},{16,0},{32,48},{48,32},{64,80},{80,64},{96,112},{112,96},{1... | collective-permute-start | bytes 331784 | tf_op jit(solution)/shard_map/ppermute | solution.py:612
  7.1 28.0 %collective-permute-start.5 = (f32[27,8,128]{2,1,0:T(8,128)S(1)}, f32[27,8,128]{2,1,0:T(8,128)S(1)}, u32[]{:S(2)}, u32[]{:S(2)}) collective-permute-start(f32[27,8,128]{2,1,0:T(8,128)S(1)} %get-tuple-element.71), channel_id=1, source_target_pairs={{0,240},{16,32},{32,16},{48,64},{64,48},{80,96},{96,80},{112,128},... | collective-permute-start | bytes 331784 | tf_op jit(solution)/shard_map/ppermute | solution.py:612
  12.2 0.7 copy-start.1
  15.8 4.7 %collective-permute-start = (f32[3,2,8,128]{3,2,1,0:T(8,128)S(1)}, f32[3,2,8,128]{3,2,1,0:T(8,128)S(1)}, u32[]{:S(2)}, u32[]{:S(2)}) collective-permute-start(f32[3,2,8,128]{3,2,1,0:T(8,128)S(1)} %get-tuple-element.65), channel_id=1, source_target_pairs={{0,1},{1,0},{2,3},{3,2},{4,5},{5,4},{6,7},{7,6},{8,9},{9,8},{10,11... | collective-permute-start | bytes 73736 | tf_op jit(solution)/shard_map/ppermute | solution.py:612
  16.6 6.6 %collective-permute-start.1 = (f32[3,2,8,128]{3,2,1,0:T(8,128)S(1)}, f32[3,2,8,128]{3,2,1,0:T(8,128)S(1)}, u32[]{:S(2)}, u32[]{:S(2)}) collective-permute-start(f32[3,2,8,128]{3,2,1,0:T(8,128)S(1)} %get-tuple-element.66), channel_id=1, source_target_pairs={{0,15},{1,2},{2,1},{3,4},{4,3},{5,6},{6,5},{7,8},{8,7},{9,10},{10,... | collective-permute-start | bytes 73736 | tf_op jit(solution)/shard_map/ppermute | solution.py:612
  23.3 5.3 %collective-permute-start.2 = (f32[3,4,8,128]{3,2,1,0:T(8,128)S(1)}, f32[3,4,8,128]{3,2,1,0:T(8,128)S(1)}, u32[]{:S(2)}, u32[]{:S(2)}) collective-permute-start(f32[3,4,8,128]{3,2,1,0:T(8,128)S(1)} %get-tuple-element.68), channel_id=1, source_target_pairs={{0,16},{16,0},{32,48},{48,32},{64,80},{80,64},{96,112},{112,96},{1... | collective-permute-start | bytes 147464 | tf_op jit(solution)/shard_map/ppermute | solution.py:612
  27.6 7.4 %collective-permute-start.3 = (f32[3,4,8,128]{3,2,1,0:T(8,128)S(1)}, f32[3,4,8,128]{3,2,1,0:T(8,128)S(1)}, u32[]{:S(2)}, u32[]{:S(2)}) collective-permute-start(f32[3,4,8,128]{3,2,1,0:T(8,128)S(1)} %get-tuple-element.69), channel_id=1, source_target_pairs={{0,240},{16,32},{32,16},{48,64},{64,48},{80,96},{96,80},{112,128},... | collective-permute-start | bytes 147464 | tf_op jit(solution)/shard_map/ppermute | solution.py:612
  35.6 4.0 %collective-permute-start.6 = (f32[11,8,128]{2,1,0:T(8,128)S(1)}, f32[11,8,128]{2,1,0:T(8,128)S(1)}, u32[]{:S(2)}, u32[]{:S(2)}) collective-permute-start(f32[11,8,128]{2,1,0:T(8,128)S(1)} %get-tuple-element.75), channel_id=1, source_target_pairs={{0,1},{1,0},{2,3},{3,2},{4,5},{5,4},{6,7},{7,6},{8,9},{9,8},{10,11... | collective-permute-start | bytes 135176 | tf_op jit(solution)/shard_map/ppermute | solution.py:612
  35.7 7.0 %collective-permute-start.7 = (f32[11,8,128]{2,1,0:T(8,128)S(1)}, f32[11,8,128]{2,1,0:T(8,128)S(1)}, u32[]{:S(2)}, u32[]{:S(2)}) collective-permute-start(f32[11,8,128]{2,1,0:T(8,128)S(1)} %get-tuple-element.76), channel_id=1, source_target_pairs={{0,15},{1,2},{2,1},{3,4},{4,3},{5,6},{6,5},{7,8},{8,7},{9,10},{10,... | collective-permute-start | bytes 135176 | tf_op jit(solution)/shard_map/ppermute | solution.py:612
  42.8 23.9 %collective-permute-start.12 = (f32[27,8,128]{2,1,0:T(8,128)S(1)}, f32[27,8,128]{2,1,0:T(8,128)S(1)}, u32[]{:S(2)}, u32[]{:S(2)}) collective-permute-start(f32[27,8,128]{2,1,0:T(8,128)S(1)} %get-tuple-element.90), channel_id=1, source_target_pairs={{0,16},{16,0},{32,48},{48,32},{64,80},{80,64},{96,112},{112,96},{1... | collective-permute-start | bytes 331784 | tf_op jit(solution)/shard_map/ppermute | solution.py:612
  46.1 20.5 %collective-permute-start.13 = (f32[27,8,128]{2,1,0:T(8,128)S(1)}, f32[27,8,128]{2,1,0:T(8,128)S(1)}, u32[]{:S(2)}, u32[]{:S(2)}) collective-permute-start(f32[27,8,128]{2,1,0:T(8,128)S(1)} %get-tuple-element.91), channel_id=1, source_target_pairs={{0,240},{16,32},{32,16},{48,64},{64,48},{80,96},{96,80},{112,128},... | collective-permute-start | bytes 331784 | tf_op jit(solution)/shard_map/ppermute | solution.py:612
  49.3 4.3 %collective-permute-start.8 = (f32[3,2,8,128]{3,2,1,0:T(8,128)S(1)}, f32[3,2,8,128]{3,2,1,0:T(8,128)S(1)}, u32[]{:S(2)}, u32[]{:S(2)}) collective-permute-start(f32[3,2,8,128]{3,2,1,0:T(8,128)S(1)} %get-tuple-element.85), channel_id=1, source_target_pairs={{0,1},{1,0},{2,3},{3,2},{4,5},{5,4},{6,7},{7,6},{8,9},{9,8},{10,11... | collective-permute-start | bytes 73736 | tf_op jit(solution)/shard_map/ppermute | solution.py:612
  49.4 6.9 %collective-permute-start.9 = (f32[3,2,8,128]{3,2,1,0:T(8,128)S(1)}, f32[3,2,8,128]{3,2,1,0:T(8,128)S(1)}, u32[]{:S(2)}, u32[]{:S(2)}) collective-permute-start(f32[3,2,8,128]{3,2,1,0:T(8,128)S(1)} %get-tuple-element.86), channel_id=1, source_target_pairs={{0,15},{1,2},{2,1},{3,4},{4,3},{5,6},{6,5},{7,8},{8,7},{9,10},{10,... | collective-permute-start | bytes 73736 | tf_op jit(solution)/shard_map/ppermute | solution.py:612
  56.3 7.0 %collective-permute-start.10 = (f32[3,4,8,128]{3,2,1,0:T(8,128)S(1)}, f32[3,4,8,128]{3,2,1,0:T(8,128)S(1)}, u32[]{:S(2)}, u32[]{:S(2)}) collective-permute-start(f32[3,4,8,128]{3,2,1,0:T(8,128)S(1)} %get-tuple-element.88), channel_id=1, source_target_pairs={{0,16},{16,0},{32,48},{48,32},{64,80},{80,64},{96,112},{112,96},{1... | collective-permute-start | bytes 147464 | tf_op jit(solution)/shard_map/ppermute | solution.py:612
  57.7 9.0 %collective-permute-start.11 = (f32[3,4,8,128]{3,2,1,0:T(8,128)S(1)}, f32[3,4,8,128]{3,2,1,0:T(8,128)S(1)}, u32[]{:S(2)}, u32[]{:S(2)}) collective-permute-start(f32[3,4,8,128]{3,2,1,0:T(8,128)S(1)} %get-tuple-element.89), channel_id=1, source_target_pairs={{0,240},{16,32},{32,16},{48,64},{64,48},{80,96},{96,80},{112,128},... | collective-permute-start | bytes 147464 | tf_op jit(solution)/shard_map/ppermute | solution.py:612
  67.2 4.1 %collective-permute-start.14 = (f32[11,8,128]{2,1,0:T(8,128)S(1)}, f32[11,8,128]{2,1,0:T(8,128)S(1)}, u32[]{:S(2)}, u32[]{:S(2)}) collective-permute-start(f32[11,8,128]{2,1,0:T(8,128)S(1)} %get-tuple-element.95), channel_id=1, source_target_pairs={{0,1},{1,0},{2,3},{3,2},{4,5},{5,4},{6,7},{7,6},{8,9},{9,8},{10,11... | collective-permute-start | bytes 135176 | tf_op jit(solution)/shard_map/ppermute | solution.py:612
  67.3 6.9 %collective-permute-start.15 = (f32[11,8,128]{2,1,0:T(8,128)S(1)}, f32[11,8,128]{2,1,0:T(8,128)S(1)}, u32[]{:S(2)}, u32[]{:S(2)}) collective-permute-start(f32[11,8,128]{2,1,0:T(8,128)S(1)} %get-tuple-element.96), channel_id=1, source_target_pairs={{0,15},{1,2},{2,1},{3,4},{4,3},{5,6},{6,5},{7,8},{8,7},{9,10},{10,... | collective-permute-start | bytes 135176 | tf_op jit(solution)/shard_map/ppermute | solution.py:612
  74.3 26.0 %collective-permute-start.20 = (f32[27,8,128]{2,1,0:T(8,128)S(1)}, f32[27,8,128]{2,1,0:T(8,128)S(1)}, u32[]{:S(2)}, u32[]{:S(2)}) collective-permute-start(f32[27,8,128]{2,1,0:T(8,128)S(1)} %get-tuple-element.108), channel_id=1, source_target_pairs={{0,16},{16,0},{32,48},{48,32},{64,80},{80,64},{96,112},{112,96},{1... | collective-permute-start | bytes 331784 | tf_op jit(solution)/shard_map/ppermute | solution.py:612
  76.3 24.0 %collective-permute-start.21 = (f32[27,8,128]{2,1,0:T(8,128)S(1)}, f32[27,8,128]{2,1,0:T(8,128)S(1)}, u32[]{:S(2)}, u32[]{:S(2)}) collective-permute-start(f32[27,8,128]{2,1,0:T(8,128)S(1)} %get-tuple-element.109), channel_id=1, source_target_pairs={{0,240},{16,32},{32,16},{48,64},{64,48},{80,96},{96,80},{112,128},... | collective-permute-start | bytes 331784 | tf_op jit(solution)/shard_map/ppermute | solution.py:612
  83.2 4.3 %collective-permute-start.16 = (f32[3,2,8,128]{3,2,1,0:T(8,128)S(1)}, f32[3,2,8,128]{3,2,1,0:T(8,128)S(1)}, u32[]{:S(2)}, u32[]{:S(2)}) collective-permute-start(f32[3,2,8,128]{3,2,1,0:T(8,128)S(1)} %get-tuple-element.103), channel_id=1, source_target_pairs={{0,1},{1,0},{2,3},{3,2},{4,5},{5,4},{6,7},{7,6},{8,9},{9,8},{10,11... | collective-permute-start | bytes 73736 | tf_op jit(solution)/shard_map/ppermute | solution.py:612
  83.3 6.7 %collective-permute-start.17 = (f32[3,2,8,128]{3,2,1,0:T(8,128)S(1)}, f32[3,2,8,128]{3,2,1,0:T(8,128)S(1)}, u32[]{:S(2)}, u32[]{:S(2)}) collective-permute-start(f32[3,2,8,128]{3,2,1,0:T(8,128)S(1)} %get-tuple-element.104), channel_id=1, source_target_pairs={{0,15},{1,2},{2,1},{3,4},{4,3},{5,6},{6,5},{7,8},{8,7},{9,10},{10,... | collective-permute-start | bytes 73736 | tf_op jit(solution)/shard_map/ppermute | solution.py:612
  90.0 3.8 %collective-permute-start.18 = (f32[3,4,8,128]{3,2,1,0:T(8,128)S(1)}, f32[3,4,8,128]{3,2,1,0:T(8,128)S(1)}, u32[]{:S(2)}, u32[]{:S(2)}) collective-permute-start(f32[3,4,8,128]{3,2,1,0:T(8,128)S(1)} %get-tuple-element.106), channel_id=1, source_target_pairs={{0,16},{16,0},{32,48},{48,32},{64,80},{80,64},{96,112},{112,96},{1... | collective-permute-start | bytes 147464 | tf_op jit(solution)/shard_map/ppermute | solution.py:612
  92.9 7.4 %collective-permute-start.19 = (f32[3,4,8,128]{3,2,1,0:T(8,128)S(1)}, f32[3,4,8,128]{3,2,1,0:T(8,128)S(1)}, u32[]{:S(2)}, u32[]{:S(2)}) collective-permute-start(f32[3,4,8,128]{3,2,1,0:T(8,128)S(1)} %get-tuple-element.107), channel_id=1, source_target_pairs={{0,240},{16,32},{32,16},{48,64},{64,48},{80,96},{96,80},{112,128},... | collective-permute-start | bytes 147464 | tf_op jit(solution)/shard_map/ppermute | solution.py:612
  100.9 4.5 %collective-permute-start.22 = (f32[11,8,128]{2,1,0:T(8,128)S(1)}, f32[11,8,128]{2,1,0:T(8,128)S(1)}, u32[]{:S(2)}, u32[]{:S(2)}) collective-permute-start(f32[11,8,128]{2,1,0:T(8,128)S(1)} %get-tuple-element.113), channel_id=1, source_target_pairs={{0,1},{1,0},{2,3},{3,2},{4,5},{5,4},{6,7},{7,6},{8,9},{9,8},{10,11... | collective-permute-start | bytes 135176 | tf_op jit(solution)/shard_map/ppermute | solution.py:612
  101.0 6.9 %collective-permute-start.23 = (f32[11,8,128]{2,1,0:T(8,128)S(1)}, f32[11,8,128]{2,1,0:T(8,128)S(1)}, u32[]{:S(2)}, u32[]{:S(2)}) collective-permute-start(f32[11,8,128]{2,1,0:T(8,128)S(1)} %get-tuple-element.114), channel_id=1, source_target_pairs={{0,15},{1,2},{2,1},{3,4},{4,3},{5,6},{6,5},{7,8},{8,7},{9,10},{10,... | collective-permute-start | bytes 135176 | tf_op jit(solution)/shard_map/ppermute | solution.py:612

commit v5 on v4

--- a/solution.py
+++ b/solution.py
@@ -127,13 +127,9 @@
     grid = None
     for slot in range(SLOTS):
         table_x, table_y, table_rim, table_z = vertex_tables(base, kernels, slot)
-        high = table_z.astype(jnp.bfloat16)
-        low = (table_z - high.astype(F32)).astype(jnp.bfloat16)
-        if depth_ref is not None:
-            for n, table in enumerate((table_x, table_y, table_rim)):
-                plane_ref[slot, n] = table
-            depth_ref[slot, 0] = high
-            depth_ref[slot, 1] = low
+        for n, table in enumerate((table_x, table_y, table_rim)):
+            plane_ref[slot, n] = table
+        depth_ref[slot] = halves(table_z)
         for a in range(3):
             pushed = force[2 * a + slot : 2 * a + slot + 1, :]
             along_x = table_x * pushed
@@ -143,11 +139,11 @@
             for n in range(3):
                 start = MAIN_ROWS + (a * 3 + n) * 8
                 terms[start : start + 8, :] = row_of(along_y, n) * table_x
-        both = halves(terms[...])
-        contract = (((1,), (1,)), ((), ()))
-        part = lax.dot_general(both, high, contract, preferred_element_type=F32)
-        rest_part = lax.dot_general(both[:TABLE_ROWS], low, contract, preferred_element_type=F32)
-        part = part[:TABLE_ROWS] + part[TABLE_ROWS:] + rest_part
+        part = lax.dot_general(
+            halves(terms[...]), depth_ref[slot], (((1,), (1,)), ((), ())), preferred_element_type=F32
+        )
+        part = part[:TABLE_ROWS] + part[TABLE_ROWS:]
+        part = part[:, :CZ] + part[:, CZ:]
         grid = part if grid is None else grid + part
     main_ref[...] = grid[:MAIN_ROWS].reshape(3, 7, 8, CZ)
     rim_ref[...] = grid[MAIN_ROWS:].reshape(3, 3, 8, CZ)
@@ -531,11 +527,11 @@
     moved = [None] * 8
     zero = jnp.zeros((1, PAD), F32)
     both = halves(flow[...])
+    both = jnp.concatenate([both, both], axis=1)
     for slot in range(SLOTS):
         table_x, table_y, table_rim = [plane_ref[slot, n] for n in range(3)]
-        along = jnp.dot(both, depth_ref[slot, 0], preferred_element_type=F32)
-        rest = jnp.dot(both[:TABLE_ROWS], depth_ref[slot, 1], preferred_element_type=F32)
-        along = along[:TABLE_ROWS] + along[TABLE_ROWS:] + rest
+        along = jnp.dot(both, depth_ref[slot], preferred_element_type=F32)
+        along = along[:TABLE_ROWS] + along[TABLE_ROWS:]
         for a in range(3):
             inner = None
             for n in range(7):
@@ -618,7 +614,7 @@
     ((3, 2, 8, CZ), F32),
     ((3, 2, 8, CZ), F32),
     ((SLOTS, 3, 8, PAD), F32),
-    ((SLOTS, 2, CZ, PAD), jnp.bfloat16),
+    ((SLOTS, 2 * CZ, PAD), jnp.bfloat16),
 ]
 HALO_OUT = [((27, 8, CZ), F32)] * 2
 STEPPED = ((19, 4, 8, CZ), F32)

time: 110 us -> 107 us (0.973)
  Pallas kernels: 12.5 us -> 9.67 us
  waiting for transfers between devices: 34.1 us -> 35.2 us
    pallas_call x14, Pallas kernels: 12.5 us -> 9.67 us  [call(): pl.pallas_call(kernel, out_shape=[jax.ShapeDtypeStruct(shape, dtype) for...]
    ppermute x24, waiting for transfers between devices: 34.1 us -> 35.2 us  [exchange(): out[kind] = lax.ppermute(message, axis, pairs)]
  transfers between devices with their start and end apart: 24 -> 24, of which waited for: 11 -> 11; matrix products, arithmetic and copies ran while one was open for 0% -> 0% of each run, Pallas kernels for 8% -> 6%
where the time goes in v5:
time: 107 us
  starting transfers between devices  57.2 us (53%)
  waiting for transfers between devices  35.2 us (33%)
  Pallas kernels  9.67 us (9%)
  local copies, waits for them, and re-layouts  3.72 us (3%)
    ppermute x24, starting transfers between devices, exchange(): out[kind] = lax.ppermute(message, axis, pairs)  57.2 us
    ppermute x24, waiting for transfers between devices, exchange(): out[kind] = lax.ppermute(message, axis, pairs)  35.2 us
    pallas_call x14, Pallas kernels, call(): pl.pallas_call(kernel, out_shape=[jax.ShapeDtypeStruct(shape, dtype) for...  9.67 us
    unnamed x16, local copies, waits for them, and re-layouts  3.72 us
  transfers between devices with their start and end apart: 24, of which 11 were waited for; matrix products, arithmetic and copies ran while one was open for 0% of the time, Pallas kernels for 6%

profile of v5, /device:TPU:1, one launch (start us, length us, event | category | flops | bytes accessed | tf_op | source)
XLA Modules:
  0.0 106.6 jit_solution(7887772653563846115)
XLA Ops:
  0.6 1.0 copy-done
  1.6 0.7 copy-done.5
  2.3 0.7 copy-done.6
  3.0 0.7 copy-done.7
  3.6 0.1 shard_map.95
  3.8 3.3 %collective-permute-start.4 = (f32[27,8,128]{2,1,0:T(8,128)S(1)}, f32[27,8,128]{2,1,0:T(8,128)S(1)}, u32[]{:S(2)}, u32[]{:S(2)}) collective-permute-start(f32[27,8,128]{2,1,0:T(8,128)S(1)} %get-tuple-element.70), channel_id=1, source_target_pairs={{0,16},{16,0},{32,48},{48,32},{64,80},{80,64},{96,112},{112,96},{1... | collective-permute-start | bytes 331784 | tf_op jit(solution)/shard_map/ppermute | solution.py:608
  7.1 5.2 %collective-permute-start.5 = (f32[27,8,128]{2,1,0:T(8,128)S(1)}, f32[27,8,128]{2,1,0:T(8,128)S(1)}, u32[]{:S(2)}, u32[]{:S(2)}) collective-permute-start(f32[27,8,128]{2,1,0:T(8,128)S(1)} %get-tuple-element.71), channel_id=1, source_target_pairs={{0,240},{16,32},{32,16},{48,64},{64,48},{80,96},{96,80},{112,128},... | collective-permute-start | bytes 331784 | tf_op jit(solution)/shard_map/ppermute | solution.py:608
  12.2 0.7 copy-done.1
  13.0 1.0 shard_map.96.incidence_ref
  14.0 1.6 %shard_map.97 = (f32[3,7,8,128]{3,2,1,0:T(8,128)S(1)}, f32[3,2,8,128]{3,2,1,0:T(8,128)S(1)}, f32[3,2,8,128]{3,2,1,0:T(8,128)S(1)}, f32[2,3,8,768]{3,2,1,0:T(8,12...) custom-call(f32[6,8,128]{2,1,0:T(8,128)S(1)} %get-tuple-element.61.i, ...), custom_call_target="tpu_custom_call" | custom-call | tf_op jit(solution)/shard_map/pallas_call | solution.py:588
  15.6 0.8 collective-permute-start
  16.4 3.8 %collective-permute-start.1 = (f32[3,2,8,128]{3,2,1,0:T(8,128)S(1)}, f32[3,2,8,128]{3,2,1,0:T(8,128)S(1)}, u32[]{:S(2)}, u32[]{:S(2)}) collective-permute-start(f32[3,2,8,128]{3,2,1,0:T(8,128)S(1)} %get-tuple-element.66), channel_id=1, source_target_pairs={{0,15},{1,2},{2,1},{3,4},{4,3},{5,6},{6,5},{7,8},{8,7},{9,10},{10,... | collective-permute-start | bytes 73736 | tf_op jit(solution)/shard_map/ppermute | solution.py:608
  20.2 0.0 collective-permute-done.first_y
  20.2 2.7 %collective-permute-done.1.second_y = f32[3,2,8,128]{3,2,1,0:T(8,128)S(1)} collective-permute-done((f32[3,2,8,128]{3,2,1,0:T(8,128)S(1)}, f32[3,2,8,128]{3,2,1,0:T(8,128)S(1)}, u32[]{:S(2)}, u32[]{:S(2)}) %collective-permute-start.1) | collective-permute-done | bytes 24608 | tf_op jit(solution)/shard_map/ppermute | solution.py:608
  23.0 4.4 %collective-permute-start.2 = (f32[3,4,8,128]{3,2,1,0:T(8,128)S(1)}, f32[3,4,8,128]{3,2,1,0:T(8,128)S(1)}, u32[]{:S(2)}, u32[]{:S(2)}) collective-permute-start(f32[3,4,8,128]{3,2,1,0:T(8,128)S(1)} %get-tuple-element.68), channel_id=1, source_target_pairs={{0,16},{16,0},{32,48},{48,32},{64,80},{80,64},{96,112},{112,96},{1... | collective-permute-start | bytes 147464 | tf_op jit(solution)/shard_map/ppermute | solution.py:608
  27.4 0.0 collective-permute-start.3
  27.4 0.9 collective-permute-done.2.first_x
  28.3 6.5 %collective-permute-done.3.second_x = f32[3,4,8,128]{3,2,1,0:T(8,128)S(1)} collective-permute-done((f32[3,4,8,128]{3,2,1,0:T(8,128)S(1)}, f32[3,4,8,128]{3,2,1,0:T(8,128)S(1)}, u32[]{:S(2)}, u32[]{:S(2)}) %collective-permute-start.3) | collective-permute-done | bytes 49184 | tf_op jit(solution)/shard_map/ppermute | solution.py:608
  34.8 0.0 collective-permute-done.4.first_h
  34.8 0.0 collective-permute-done.5.second_h
  34.8 0.5 shard_map.99
  35.3 0.1 collective-permute-start.6
  35.4 3.9 %collective-permute-start.7 = (f32[11,8,128]{2,1,0:T(8,128)S(1)}, f32[11,8,128]{2,1,0:T(8,128)S(1)}, u32[]{:S(2)}, u32[]{:S(2)}) collective-permute-start(f32[11,8,128]{2,1,0:T(8,128)S(1)} %get-tuple-element.76), channel_id=1, source_target_pairs={{0,15},{1,2},{2,1},{3,4},{4,3},{5,6},{6,5},{7,8},{8,7},{9,10},{10,... | collective-permute-start | bytes 135176 | tf_op jit(solution)/shard_map/ppermute | solution.py:608
  39.3 0.0 collective-permute-done.6.first_y
  39.4 3.1 %collective-permute-done.7.second_y = f32[11,8,128]{2,1,0:T(8,128)S(1)} collective-permute-done((f32[11,8,128]{2,1,0:T(8,128)S(1)}, f32[11,8,128]{2,1,0:T(8,128)S(1)}, u32[]{:S(2)}, u32[]{:S(2)}) %collective-permute-start.7) | collective-permute-done | bytes 45088 | tf_op jit(solution)/shard_map/ppermute | solution.py:608
  42.4 0.1 shard_map.100
  42.6 3.4 %collective-permute-start.12 = (f32[27,8,128]{2,1,0:T(8,128)S(1)}, f32[27,8,128]{2,1,0:T(8,128)S(1)}, u32[]{:S(2)}, u32[]{:S(2)}) collective-permute-start(f32[27,8,128]{2,1,0:T(8,128)S(1)} %get-tuple-element.90), channel_id=1, source_target_pairs={{0,16},{16,0},{32,48},{48,32},{64,80},{80,64},{96,112},{112,96},{1... | collective-permute-start | bytes 331784 | tf_op jit(solution)/shard_map/ppermute | solution.py:608
  46.0 0.0 collective-permute-start.13
  46.0 2.0 %shard_map.101 = (f32[3,7,8,128]{3,2,1,0:T(8,128)S(1)}, f32[3,2,8,128]{3,2,1,0:T(8,128)S(1)}, f32[3,2,8,128]{3,2,1,0:T(8,128)S(1)}, f32[2,3,8,768]{3,2,1,0:T(8,1...) custom-call(f32[6,8,128]{2,1,0:T(8,128)S(1)} %get-tuple-element.61.info_ref, ...), custom_call_target="tpu_custom_call" | custom-call | tf_op jit(solution)/shard_map/pallas_call | solution.py:588
  48.0 0.1 collective-permute-start.8
  48.1 3.9 %collective-permute-start.9 = (f32[3,2,8,128]{3,2,1,0:T(8,128)S(1)}, f32[3,2,8,128]{3,2,1,0:T(8,128)S(1)}, u32[]{:S(2)}, u32[]{:S(2)}) collective-permute-start(f32[3,2,8,128]{3,2,1,0:T(8,128)S(1)} %get-tuple-element.86), channel_id=1, source_target_pairs={{0,15},{1,2},{2,1},{3,4},{4,3},{5,6},{6,5},{7,8},{8,7},{9,10},{10,... | collective-permute-start | bytes 73736 | tf_op jit(solution)/shard_map/ppermute | solution.py:608
  52.0 0.0 collective-permute-done.8.first_y
  52.0 3.4 %collective-permute-done.9.second_y = f32[3,2,8,128]{3,2,1,0:T(8,128)S(1)} collective-permute-done((f32[3,2,8,128]{3,2,1,0:T(8,128)S(1)}, f32[3,2,8,128]{3,2,1,0:T(8,128)S(1)}, u32[]{:S(2)}, u32[]{:S(2)}) %collective-permute-start.9) | collective-permute-done | bytes 24608 | tf_op jit(solution)/shard_map/ppermute | solution.py:608
  55.5 0.9 collective-permute-start.10
  56.4 5.5 %collective-permute-start.11 = (f32[3,4,8,128]{3,2,1,0:T(8,128)S(1)}, f32[3,4,8,128]{3,2,1,0:T(8,128)S(1)}, u32[]{:S(2)}, u32[]{:S(2)}) collective-permute-start(f32[3,4,8,128]{3,2,1,0:T(8,128)S(1)} %get-tuple-element.89), channel_id=1, source_target_pairs={{0,240},{16,32},{32,16},{48,64},{64,48},{80,96},{96,80},{112,128},... | collective-permute-start | bytes 147464 | tf_op jit(solution)/shard_map/ppermute | solution.py:608
  62.0 0.0 collective-permute-done.10.first_x
  62.0 3.4 %collective-permute-done.11.second_x = f32[3,4,8,128]{3,2,1,0:T(8,128)S(1)} collective-permute-done((f32[3,4,8,128]{3,2,1,0:T(8,128)S(1)}, f32[3,4,8,128]{3,2,1,0:T(8,128)S(1)}, u32[]{:S(2)}, u32[]{:S(2)}) %collective-permute-start.11) | collective-permute-done | bytes 49184 | tf_op jit(solution)/shard_map/ppermute | solution.py:608
  65.3 0.0 collective-permute-done.12.first_h
  65.3 0.0 collective-permute-done.13.second_h
  65.3 0.5 shard_map.103
  65.8 0.1 collective-permute-start.14
  65.9 4.0 %collective-permute-start.15 = (f32[11,8,128]{2,1,0:T(8,128)S(1)}, f32[11,8,128]{2,1,0:T(8,128)S(1)}, u32[]{:S(2)}, u32[]{:S(2)}) collective-permute-start(f32[11,8,128]{2,1,0:T(8,128)S(1)} %get-tuple-element.96), channel_id=1, source_target_pairs={{0,15},{1,2},{2,1},{3,4},{4,3},{5,6},{6,5},{7,8},{8,7},{9,10},{10,... | collective-permute-start | bytes 135176 | tf_op jit(solution)/shard_map/ppermute | solution.py:608
  69.9 0.0 collective-permute-done.14.first_y
  69.9 3.0 %collective-permute-done.15.second_y = f32[11,8,128]{2,1,0:T(8,128)S(1)} collective-permute-done((f32[11,8,128]{2,1,0:T(8,128)S(1)}, f32[11,8,128]{2,1,0:T(8,128)S(1)}, u32[]{:S(2)}, u32[]{:S(2)}) %collective-permute-start.15) | collective-permute-done | bytes 45088 | tf_op jit(solution)/shard_map/ppermute | solution.py:608
  72.9 0.1 shard_map.104
  73.0 2.1 %collective-permute-start.20 = (f32[27,8,128]{2,1,0:T(8,128)S(1)}, f32[27,8,128]{2,1,0:T(8,128)S(1)}, u32[]{:S(2)}, u32[]{:S(2)}) collective-permute-start(f32[27,8,128]{2,1,0:T(8,128)S(1)} %get-tuple-element.108), channel_id=1, source_target_pairs={{0,16},{16,0},{32,48},{48,32},{64,80},{80,64},{96,112},{112,96},{1... | collective-permute-start | bytes 331784 | tf_op jit(solution)/shard_map/ppermute | solution.py:608
  75.2 3.5 %collective-permute-start.21 = (f32[27,8,128]{2,1,0:T(8,128)S(1)}, f32[27,8,128]{2,1,0:T(8,128)S(1)}, u32[]{:S(2)}, u32[]{:S(2)}) collective-permute-start(f32[27,8,128]{2,1,0:T(8,128)S(1)} %get-tuple-element.109), channel_id=1, source_target_pairs={{0,240},{16,32},{32,16},{48,64},{64,48},{80,96},{96,80},{112,128},... | collective-permute-start | bytes 331784 | tf_op jit(solution)/shard_map/ppermute | solution.py:608
  78.7 1.9 %shard_map.105 = (f32[3,7,8,128]{3,2,1,0:T(8,128)S(1)}, f32[3,2,8,128]{3,2,1,0:T(8,128)S(1)}, f32[3,2,8,128]{3,2,1,0:T(8,128)S(1)}, f32[2,3,8,768]{3,2,1,0:T(8,1...) custom-call(f32[6,8,128]{2,1,0:T(8,128)S(1)} %get-tuple-element.61.info_ref, ...), custom_call_target="tpu_custom_call" | custom-call | tf_op jit(solution)/shard_map/pallas_call | solution.py:588
  80.6 0.1 collective-permute-start.16
  80.7 4.4 %collective-permute-start.17 = (f32[3,2,8,128]{3,2,1,0:T(8,128)S(1)}, f32[3,2,8,128]{3,2,1,0:T(8,128)S(1)}, u32[]{:S(2)}, u32[]{:S(2)}) collective-permute-start(f32[3,2,8,128]{3,2,1,0:T(8,128)S(1)} %get-tuple-element.104), channel_id=1, source_target_pairs={{0,15},{1,2},{2,1},{3,4},{4,3},{5,6},{6,5},{7,8},{8,7},{9,10},{10,... | collective-permute-start | bytes 73736 | tf_op jit(solution)/shard_map/ppermute | solution.py:608
  85.1 0.0 collective-permute-done.16.first_y
  85.1 2.3 %collective-permute-done.17.second_y = f32[3,2,8,128]{3,2,1,0:T(8,128)S(1)} collective-permute-done((f32[3,2,8,128]{3,2,1,0:T(8,128)S(1)}, f32[3,2,8,128]{3,2,1,0:T(8,128)S(1)}, u32[]{:S(2)}, u32[]{:S(2)}) %collective-permute-start.17) | collective-permute-done | bytes 24608 | tf_op jit(solution)/shard_map/ppermute | solution.py:608
  87.4 2.9 %collective-permute-start.18 = (f32[3,4,8,128]{3,2,1,0:T(8,128)S(1)}, f32[3,4,8,128]{3,2,1,0:T(8,128)S(1)}, u32[]{:S(2)}, u32[]{:S(2)}) collective-permute-start(f32[3,4,8,128]{3,2,1,0:T(8,128)S(1)} %get-tuple-element.106), channel_id=1, source_target_pairs={{0,16},{16,0},{32,48},{48,32},{64,80},{80,64},{96,112},{112,96},{1... | collective-permute-start | bytes 147464 | tf_op jit(solution)/shard_map/ppermute | solution.py:608
  90.4 0.6 collective-permute-start.19
  90.9 0.3 collective-permute-done.18.first_x
  91.2 6.6 %collective-permute-done.19.second_x = f32[3,4,8,128]{3,2,1,0:T(8,128)S(1)} collective-permute-done((f32[3,4,8,128]{3,2,1,0:T(8,128)S(1)}, f32[3,4,8,128]{3,2,1,0:T(8,128)S(1)}, u32[]{:S(2)}, u32[]{:S(2)}) %collective-permute-start.19) | collective-permute-done | bytes 49184 | tf_op jit(solution)/shard_map/ppermute | solution.py:608
  97.9 0.0 collective-permute-done.20.first_h
  97.9 0.0 collective-permute-done.21.second_h
  97.9 0.5 shard_map.107
  98.4 0.1 collective-permute-start.22
  98.5 3.9 %collective-permute-start.23 = (f32[11,8,128]{2,1,0:T(8,128)S(1)}, f32[11,8,128]{2,1,0:T(8,128)S(1)}, u32[]{:S(2)}, u32[]{:S(2)}) collective-permute-start(f32[11,8,128]{2,1,0:T(8,128)S(1)} %get-tuple-element.114), channel_id=1, source_target_pairs={{0,15},{1,2},{2,1},{3,4},{4,3},{5,6},{6,5},{7,8},{8,7},{9,10},{10,... | collective-permute-start | bytes 135176 | tf_op jit(solution)/shard_map/ppermute | solution.py:608
  102.4 0.0 collective-permute-done.22.first_y
  102.4 3.0 %collective-permute-done.23.second_y = f32[11,8,128]{2,1,0:T(8,128)S(1)} collective-permute-done((f32[11,8,128]{2,1,0:T(8,128)S(1)}, f32[11,8,128]{2,1,0:T(8,128)S(1)}, u32[]{:S(2)}, u32[]{:S(2)}) %collective-permute-start.23) | collective-permute-done | bytes 45088 | tf_op jit(solution)/shard_map/ppermute | solution.py:608
  105.4 1.2 %shard_map.108 = (f32[19,4,8,128]{3,2,1,0:T(8,128)}, f32[3,2,768]{2,1,0:T(2,128)}) custom-call(f32[6,8,128]{2,1,0:T(8,128)S(1)} %get-tuple-element.61.info_ref, f32[608,128]{1,0:T(8,128)S(1)} %get-tuple-element.110.stepped_ref, f32[256,128]{1,0:T(8,128)S(1)} %get-tuple-element.111.inside_ref, f32[6,8,128]{2,1,0:T(8,128)S(1)} %get-tuple-element.112.leaving_ref, ...), custom_call_target="tpu_custom_call" | custom-call | tf_op jit(solution)/shard_map/pallas_call | solution.py:588
  (14 shorter events, 0.1 us)
Async XLA Ops:
  0.6 1.0 copy-start
  1.6 0.7 copy-start.5
  2.3 0.7 copy-start.6
  3.0 0.7 copy-start.7
  3.6 10.4 %copy-start.2 = (f32[3,1,1,2,768]{4,3,2,1,0:T(2,128)S(1)}, f32[3,1,1,2,768]{4,3,2,1,0:T(2,128)}, u32[]{:S(2)}) copy-start(f32[3,1,1,2,768]{4,3,2,1,0:T(2,128)} %param.11) | copy-start | bytes 55300
  3.6 10.4 %copy-start.3 = (f32[3,1,1,2,768]{4,3,2,1,0:T(2,128)S(1)}, f32[3,1,1,2,768]{4,3,2,1,0:T(2,128)}, u32[]{:S(2)}) copy-start(f32[3,1,1,2,768]{4,3,2,1,0:T(2,128)} %param.12) | copy-start | bytes 55300
  3.6 10.4 %copy-start.4 = (s32[3,1,1,2,768]{4,3,2,1,0:T(2,128)S(1)}, s32[3,1,1,2,768]{4,3,2,1,0:T(2,128)}, u32[]{:S(2)}) copy-start(s32[3,1,1,2,768]{4,3,2,1,0:T(2,128)} %param.10) | copy-start | bytes 55300
  3.8 31.1 %collective-permute-start.4 = (f32[27,8,128]{2,1,0:T(8,128)S(1)}, f32[27,8,128]{2,1,0:T(8,128)S(1)}, u32[]{:S(2)}, u32[]{:S(2)}) collective-permute-start(f32[27,8,128]{2,1,0:T(8,128)S(1)} %get-tuple-element.70), channel_id=1, source_target_pairs={{0,16},{16,0},{32,48},{48,32},{64,80},{80,64},{96,112},{112,96},{1... | collective-permute-start | bytes 331784 | tf_op jit(solution)/shard_map/ppermute | solution.py:608
  7.1 27.8 %collective-permute-start.5 = (f32[27,8,128]{2,1,0:T(8,128)S(1)}, f32[27,8,128]{2,1,0:T(8,128)S(1)}, u32[]{:S(2)}, u32[]{:S(2)}) collective-permute-start(f32[27,8,128]{2,1,0:T(8,128)S(1)} %get-tuple-element.71), channel_id=1, source_target_pairs={{0,240},{16,32},{32,16},{48,64},{64,48},{80,96},{96,80},{112,128},... | collective-permute-start | bytes 331784 | tf_op jit(solution)/shard_map/ppermute | solution.py:608
  12.2 0.7 copy-start.1
  15.6 4.7 %collective-permute-start = (f32[3,2,8,128]{3,2,1,0:T(8,128)S(1)}, f32[3,2,8,128]{3,2,1,0:T(8,128)S(1)}, u32[]{:S(2)}, u32[]{:S(2)}) collective-permute-start(f32[3,2,8,128]{3,2,1,0:T(8,128)S(1)} %get-tuple-element.65), channel_id=1, source_target_pairs={{0,1},{1,0},{2,3},{3,2},{4,5},{5,4},{6,7},{7,6},{8,9},{9,8},{10,11... | collective-permute-start | bytes 73736 | tf_op jit(solution)/shard_map/ppermute | solution.py:608
  16.4 6.6 %collective-permute-start.1 = (f32[3,2,8,128]{3,2,1,0:T(8,128)S(1)}, f32[3,2,8,128]{3,2,1,0:T(8,128)S(1)}, u32[]{:S(2)}, u32[]{:S(2)}) collective-permute-start(f32[3,2,8,128]{3,2,1,0:T(8,128)S(1)} %get-tuple-element.66), channel_id=1, source_target_pairs={{0,15},{1,2},{2,1},{3,4},{4,3},{5,6},{6,5},{7,8},{8,7},{9,10},{10,... | collective-permute-start | bytes 73736 | tf_op jit(solution)/shard_map/ppermute | solution.py:608
  23.0 5.3 %collective-permute-start.2 = (f32[3,4,8,128]{3,2,1,0:T(8,128)S(1)}, f32[3,4,8,128]{3,2,1,0:T(8,128)S(1)}, u32[]{:S(2)}, u32[]{:S(2)}) collective-permute-start(f32[3,4,8,128]{3,2,1,0:T(8,128)S(1)} %get-tuple-element.68), channel_id=1, source_target_pairs={{0,16},{16,0},{32,48},{48,32},{64,80},{80,64},{96,112},{112,96},{1... | collective-permute-start | bytes 147464 | tf_op jit(solution)/shard_map/ppermute | solution.py:608
  27.4 7.4 %collective-permute-start.3 = (f32[3,4,8,128]{3,2,1,0:T(8,128)S(1)}, f32[3,4,8,128]{3,2,1,0:T(8,128)S(1)}, u32[]{:S(2)}, u32[]{:S(2)}) collective-permute-start(f32[3,4,8,128]{3,2,1,0:T(8,128)S(1)} %get-tuple-element.69), channel_id=1, source_target_pairs={{0,240},{16,32},{32,16},{48,64},{64,48},{80,96},{96,80},{112,128},... | collective-permute-start | bytes 147464 | tf_op jit(solution)/shard_map/ppermute | solution.py:608
  35.3 4.0 %collective-permute-start.6 = (f32[11,8,128]{2,1,0:T(8,128)S(1)}, f32[11,8,128]{2,1,0:T(8,128)S(1)}, u32[]{:S(2)}, u32[]{:S(2)}) collective-permute-start(f32[11,8,128]{2,1,0:T(8,128)S(1)} %get-tuple-element.75), channel_id=1, source_target_pairs={{0,1},{1,0},{2,3},{3,2},{4,5},{5,4},{6,7},{7,6},{8,9},{9,8},{10,11... | collective-permute-start | bytes 135176 | tf_op jit(solution)/shard_map/ppermute | solution.py:608
  35.4 7.0 %collective-permute-start.7 = (f32[11,8,128]{2,1,0:T(8,128)S(1)}, f32[11,8,128]{2,1,0:T(8,128)S(1)}, u32[]{:S(2)}, u32[]{:S(2)}) collective-permute-start(f32[11,8,128]{2,1,0:T(8,128)S(1)} %get-tuple-element.76), channel_id=1, source_target_pairs={{0,15},{1,2},{2,1},{3,4},{4,3},{5,6},{6,5},{7,8},{8,7},{9,10},{10,... | collective-permute-start | bytes 135176 | tf_op jit(solution)/shard_map/ppermute | solution.py:608
  42.6 22.8 %collective-permute-start.12 = (f32[27,8,128]{2,1,0:T(8,128)S(1)}, f32[27,8,128]{2,1,0:T(8,128)S(1)}, u32[]{:S(2)}, u32[]{:S(2)}) collective-permute-start(f32[27,8,128]{2,1,0:T(8,128)S(1)} %get-tuple-element.90), channel_id=1, source_target_pairs={{0,16},{16,0},{32,48},{48,32},{64,80},{80,64},{96,112},{112,96},{1... | collective-permute-start | bytes 331784 | tf_op jit(solution)/shard_map/ppermute | solution.py:608
  46.0 19.3 %collective-permute-start.13 = (f32[27,8,128]{2,1,0:T(8,128)S(1)}, f32[27,8,128]{2,1,0:T(8,128)S(1)}, u32[]{:S(2)}, u32[]{:S(2)}) collective-permute-start(f32[27,8,128]{2,1,0:T(8,128)S(1)} %get-tuple-element.91), channel_id=1, source_target_pairs={{0,240},{16,32},{32,16},{48,64},{64,48},{80,96},{96,80},{112,128},... | collective-permute-start | bytes 331784 | tf_op jit(solution)/shard_map/ppermute | solution.py:608
  48.0 4.1 %collective-permute-start.8 = (f32[3,2,8,128]{3,2,1,0:T(8,128)S(1)}, f32[3,2,8,128]{3,2,1,0:T(8,128)S(1)}, u32[]{:S(2)}, u32[]{:S(2)}) collective-permute-start(f32[3,2,8,128]{3,2,1,0:T(8,128)S(1)} %get-tuple-element.85), channel_id=1, source_target_pairs={{0,1},{1,0},{2,3},{3,2},{4,5},{5,4},{6,7},{7,6},{8,9},{9,8},{10,11... | collective-permute-start | bytes 73736 | tf_op jit(solution)/shard_map/ppermute | solution.py:608
  48.1 7.4 %collective-permute-start.9 = (f32[3,2,8,128]{3,2,1,0:T(8,128)S(1)}, f32[3,2,8,128]{3,2,1,0:T(8,128)S(1)}, u32[]{:S(2)}, u32[]{:S(2)}) collective-permute-start(f32[3,2,8,128]{3,2,1,0:T(8,128)S(1)} %get-tuple-element.86), channel_id=1, source_target_pairs={{0,15},{1,2},{2,1},{3,4},{4,3},{5,6},{6,5},{7,8},{8,7},{9,10},{10,... | collective-permute-start | bytes 73736 | tf_op jit(solution)/shard_map/ppermute | solution.py:608
  55.5 6.5 %collective-permute-start.10 = (f32[3,4,8,128]{3,2,1,0:T(8,128)S(1)}, f32[3,4,8,128]{3,2,1,0:T(8,128)S(1)}, u32[]{:S(2)}, u32[]{:S(2)}) collective-permute-start(f32[3,4,8,128]{3,2,1,0:T(8,128)S(1)} %get-tuple-element.88), channel_id=1, source_target_pairs={{0,16},{16,0},{32,48},{48,32},{64,80},{80,64},{96,112},{112,96},{1... | collective-permute-start | bytes 147464 | tf_op jit(solution)/shard_map/ppermute | solution.py:608
  56.4 8.9 %collective-permute-start.11 = (f32[3,4,8,128]{3,2,1,0:T(8,128)S(1)}, f32[3,4,8,128]{3,2,1,0:T(8,128)S(1)}, u32[]{:S(2)}, u32[]{:S(2)}) collective-permute-start(f32[3,4,8,128]{3,2,1,0:T(8,128)S(1)} %get-tuple-element.89), channel_id=1, source_target_pairs={{0,240},{16,32},{32,16},{48,64},{64,48},{80,96},{96,80},{112,128},... | collective-permute-start | bytes 147464 | tf_op jit(solution)/shard_map/ppermute | solution.py:608
  65.8 4.1 %collective-permute-start.14 = (f32[11,8,128]{2,1,0:T(8,128)S(1)}, f32[11,8,128]{2,1,0:T(8,128)S(1)}, u32[]{:S(2)}, u32[]{:S(2)}) collective-permute-start(f32[11,8,128]{2,1,0:T(8,128)S(1)} %get-tuple-element.95), channel_id=1, source_target_pairs={{0,1},{1,0},{2,3},{3,2},{4,5},{5,4},{6,7},{7,6},{8,9},{9,8},{10,11... | collective-permute-start | bytes 135176 | tf_op jit(solution)/shard_map/ppermute | solution.py:608
  65.9 7.0 %collective-permute-start.15 = (f32[11,8,128]{2,1,0:T(8,128)S(1)}, f32[11,8,128]{2,1,0:T(8,128)S(1)}, u32[]{:S(2)}, u32[]{:S(2)}) collective-permute-start(f32[11,8,128]{2,1,0:T(8,128)S(1)} %get-tuple-element.96), channel_id=1, source_target_pairs={{0,15},{1,2},{2,1},{3,4},{4,3},{5,6},{6,5},{7,8},{8,7},{9,10},{10,... | collective-permute-start | bytes 135176 | tf_op jit(solution)/shard_map/ppermute | solution.py:608
  73.0 24.9 %collective-permute-start.20 = (f32[27,8,128]{2,1,0:T(8,128)S(1)}, f32[27,8,128]{2,1,0:T(8,128)S(1)}, u32[]{:S(2)}, u32[]{:S(2)}) collective-permute-start(f32[27,8,128]{2,1,0:T(8,128)S(1)} %get-tuple-element.108), channel_id=1, source_target_pairs={{0,16},{16,0},{32,48},{48,32},{64,80},{80,64},{96,112},{112,96},{1... | collective-permute-start | bytes 331784 | tf_op jit(solution)/shard_map/ppermute | solution.py:608
  75.2 22.7 %collective-permute-start.21 = (f32[27,8,128]{2,1,0:T(8,128)S(1)}, f32[27,8,128]{2,1,0:T(8,128)S(1)}, u32[]{:S(2)}, u32[]{:S(2)}) collective-permute-start(f32[27,8,128]{2,1,0:T(8,128)S(1)} %get-tuple-element.109), channel_id=1, source_target_pairs={{0,240},{16,32},{32,16},{48,64},{64,48},{80,96},{96,80},{112,128},... | collective-permute-start | bytes 331784 | tf_op jit(solution)/shard_map/ppermute | solution.py:608
  80.6 4.5 %collective-permute-start.16 = (f32[3,2,8,128]{3,2,1,0:T(8,128)S(1)}, f32[3,2,8,128]{3,2,1,0:T(8,128)S(1)}, u32[]{:S(2)}, u32[]{:S(2)}) collective-permute-start(f32[3,2,8,128]{3,2,1,0:T(8,128)S(1)} %get-tuple-element.103), channel_id=1, source_target_pairs={{0,1},{1,0},{2,3},{3,2},{4,5},{5,4},{6,7},{7,6},{8,9},{9,8},{10,11... | collective-permute-start | bytes 73736 | tf_op jit(solution)/shard_map/ppermute | solution.py:608
  80.7 6.7 %collective-permute-start.17 = (f32[3,2,8,128]{3,2,1,0:T(8,128)S(1)}, f32[3,2,8,128]{3,2,1,0:T(8,128)S(1)}, u32[]{:S(2)}, u32[]{:S(2)}) collective-permute-start(f32[3,2,8,128]{3,2,1,0:T(8,128)S(1)} %get-tuple-element.104), channel_id=1, source_target_pairs={{0,15},{1,2},{2,1},{3,4},{4,3},{5,6},{6,5},{7,8},{8,7},{9,10},{10,... | collective-permute-start | bytes 73736 | tf_op jit(solution)/shard_map/ppermute | solution.py:608
  87.4 3.8 %collective-permute-start.18 = (f32[3,4,8,128]{3,2,1,0:T(8,128)S(1)}, f32[3,4,8,128]{3,2,1,0:T(8,128)S(1)}, u32[]{:S(2)}, u32[]{:S(2)}) collective-permute-start(f32[3,4,8,128]{3,2,1,0:T(8,128)S(1)} %get-tuple-element.106), channel_id=1, source_target_pairs={{0,16},{16,0},{32,48},{48,32},{64,80},{80,64},{96,112},{112,96},{1... | collective-permute-start | bytes 147464 | tf_op jit(solution)/shard_map/ppermute | solution.py:608
  90.4 7.5 %collective-permute-start.19 = (f32[3,4,8,128]{3,2,1,0:T(8,128)S(1)}, f32[3,4,8,128]{3,2,1,0:T(8,128)S(1)}, u32[]{:S(2)}, u32[]{:S(2)}) collective-permute-start(f32[3,4,8,128]{3,2,1,0:T(8,128)S(1)} %get-tuple-element.107), channel_id=1, source_target_pairs={{0,240},{16,32},{32,16},{48,64},{64,48},{80,96},{96,80},{112,128},... | collective-permute-start | bytes 147464 | tf_op jit(solution)/shard_map/ppermute | solution.py:608
  98.4 4.0 %collective-permute-start.22 = (f32[11,8,128]{2,1,0:T(8,128)S(1)}, f32[11,8,128]{2,1,0:T(8,128)S(1)}, u32[]{:S(2)}, u32[]{:S(2)}) collective-permute-start(f32[11,8,128]{2,1,0:T(8,128)S(1)} %get-tuple-element.113), channel_id=1, source_target_pairs={{0,1},{1,0},{2,3},{3,2},{4,5},{5,4},{6,7},{7,6},{8,9},{9,8},{10,11... | collective-permute-start | bytes 135176 | tf_op jit(solution)/shard_map/ppermute | solution.py:608
  98.5 6.9 %collective-permute-start.23 = (f32[11,8,128]{2,1,0:T(8,128)S(1)}, f32[11,8,128]{2,1,0:T(8,128)S(1)}, u32[]{:S(2)}, u32[]{:S(2)}) collective-permute-start(f32[11,8,128]{2,1,0:T(8,128)S(1)} %get-tuple-element.114), channel_id=1, source_target_pairs={{0,15},{1,2},{2,1},{3,4},{4,3},{5,6},{6,5},{7,8},{8,7},{9,10},{10,... | collective-permute-start | bytes 135176 | tf_op jit(solution)/shard_map/ppermute | solution.py:608
